TPU v7x, 256 devices: a whole 4x4x8 slice. The times are simulated.
256 devices in a mesh: row: 16 (over x, y), col: 16 (over z, core).
Axes of the slice: x: 4, y: 4, z: 8, core: 2. Of those that a mesh axis runs over, the one named last changes fastest.
Arguments:
- inv_hessian: float32 [12288, 12288], P('row', 'col'), as said below
- weights: bfloat16 [24576, 12288], P('row', 'col'), may hold values from -6 to 6
- calib: bfloat16 [128, 12288], replicated, may hold values from -6 to 6
- block: int32 [1], replicated, may hold values from 0 to 47
Outputs:
- updated: float32 [12288, 12288], P('row', 'col')
- pruned: bfloat16 [24576, 12288], P('row', 'col')
Inputs may be any that keep to these rules, and one draw needn't show every extreme that they name: `inv_hessian`: symmetric and positive definite.
All inputs are finite; a program needn't handle non-finite values.
Results may differ from a plain program's by a relative error of at most 0.002.
Values may be sent and summed in bfloat16 or wider, within the bound.
No kernel may reach another device: no remote copies, remote signals or barrier semaphores. Data moves between devices by JAX's collectives and lax.ppermute only.
A program may use at most 128 MiB of HBM per device.

v0:
```python
import jax
import jax.numpy as jnp
from jax import lax
from jax.sharding import Mesh
from jax.sharding import PartitionSpec as P

B = 256
COL = ("col_0", "col_1")


def filled_up(lines, peers):
    spare = -len(lines) % peers
    return jnp.pad(lines, [(0, spare)] + [(0, 0)] * (lines.ndim - 1))


def from_everyone(x, axis):
    copies = jnp.broadcast_to(x, (lax.axis_size(axis), *x.shape))
    return lax.all_to_all(copies, axis, split_axis=0, concat_axis=0, tiled=True)


def in_order(parts, dim):
    parts = jnp.moveaxis(parts, 0, dim)
    lengths = parts.shape
    return parts.reshape(*lengths[:dim], lengths[dim] * lengths[dim + 1], *lengths[dim + 2 :])


def gather_directly(x, axis, dim):
    parts = from_everyone(x, axis)
    return in_order(parts, dim)


def in_blocks(x, dim, peers):
    before, after = (x.shape[:dim], x.shape[dim + 1 :])
    return jnp.moveaxis(x.reshape(*before, peers, -1, *after), dim, 0)


def sent_and_summed(x, axis, dim):
    parts = in_blocks(x, dim, lax.axis_size(axis))
    arrived = lax.all_to_all(parts, axis, split_axis=0, concat_axis=0, tiled=True)
    return arrived.sum(axis=0)


def nested_sum(x, axes):
    lines = x.reshape(-1, x.shape[-1])
    padded = filled_up(lines, lax.axis_size(axes))
    whole = gather_directly(sent_and_summed(padded, axes, 0), axes, 0)
    return lax.slice_in_dim(whole, 0, len(lines)).reshape(x.shape)


def gather_axes(x, axes, dim):
    far, near = axes
    parts = from_everyone(from_everyone(x, far), near)
    return in_order(parts.swapaxes(0, 1).reshape(-1, *x.shape), dim)


def sum_in_two_steps(x, axes, dim):
    far, near = axes
    own = sent_and_summed(in_blocks(x, dim, lax.axis_size(far)), near, dim + 1)
    return jnp.sum(lax.all_to_all(own, far, 0, 0, tiled=True), axis=0)


def nested_sum_2(x, axes):
    padded = filled_up(x, lax.axis_size(axes[0]) * lax.axis_size(axes[1]))
    whole = gather_axes(sum_in_two_steps(padded, axes, 0), axes, 0)
    return lax.slice_in_dim(whole, 0, len(x)).reshape(x.shape)


def in_one(arrays, axis):
    ravelled, at, done = (jnp.concatenate([a.reshape(-1) for a in arrays]), 0, [])
    total = nested_sum_2(ravelled, axis)
    for a in arrays:
        done.append(total[at : at + a.size].reshape(a.shape))
        at += a.size
    return tuple(done)


def picked(x, axis, root):
    return lax.dynamic_index_in_dim(lax.all_gather(x, axis), root, 0, keepdims=False)


def per_device(inv_hessian, weights, calib, block):
    highest = lax.Precision.HIGHEST
    tile_rows, tile_cols = inv_hessian.shape
    row_index = lax.axis_index("row")
    col_index = lax.axis_index(COL)
    calib_rows = lax.dynamic_slice_in_dim(calib, row_index * tile_rows, tile_rows, 1).astype(
        jnp.float32
    )
    calib_cols = lax.dynamic_slice_in_dim(calib, col_index * tile_cols, tile_cols, 1).astype(
        jnp.float32
    )
    left_part = jnp.dot(calib_rows, inv_hessian, precision=highest)
    left_cols = nested_sum(left_part, "row")
    right_part = jnp.dot(inv_hessian, calib_cols.T, precision=highest)
    inner_part = jnp.dot(left_cols, calib_cols.T, precision=highest)
    right_rows, inner = in_one((right_part, inner_part), ("col_0", "col_1"))
    inner = jnp.eye(inner.shape[0], dtype=jnp.float32) + inner
    inner = 0.5 * (inner + inner.T)
    factor = jnp.linalg.cholesky(inner)
    solved = jax.scipy.linalg.cho_solve((factor, True), left_cols)
    updated = inv_hessian - jnp.dot(right_rows, solved, precision=highest)
    start = block[0] * B
    owner_row = start // tile_rows
    owner_col = start // tile_cols
    offset_row = start - owner_row * tile_rows
    offset_col = start - owner_col * tile_cols
    mine_rows = lax.dynamic_slice_in_dim(updated, offset_row, B, 0)
    strip = picked(mine_rows, "row", owner_row)
    mine_square = lax.dynamic_slice_in_dim(strip, offset_col, B, 1)
    square = picked(mine_square, COL, owner_col)
    mine_window = lax.dynamic_slice_in_dim(weights, offset_col, B, 1)
    window = picked(mine_window, COL, owner_col)
    square = 0.5 * (square + square.T)
    square_factor = jnp.linalg.cholesky(square)
    comp = jax.scipy.linalg.cho_solve((square_factor, True), strip).astype(jnp.bfloat16)
    product = jnp.dot(window, comp, preferred_element_type=jnp.float32)
    pruned = (weights.astype(jnp.float32) - product).astype(jnp.bfloat16)
    return (updated, pruned)


def solution(mesh):
    finer = Mesh(mesh.devices.reshape(mesh.shape["row"], 8, 2), ("row", "col_0", "col_1"))
    in_specs = (P("row", COL), P("row", COL), P(), P())
    out_specs = (P("row", COL), P("row", COL))
    return jax.shard_map(
        per_device, mesh=finer, in_specs=in_specs, out_specs=out_specs, check_vma=False
    )
```

profile of v0, /device:TPU:1, one launch (start us, length us, event | category | flops | bytes accessed | tf_op | source)
XLA Modules:
  0.0 367.1 jit_solution(16812215025209279737)
XLA Ops:
  7.2 1.9 copy-done
  9.1 2.6 convolution_bitcast_fusion.1
  11.7 15.6 %all_to_all.38 = f32[16,8,768]{2,1,0:T(8,128)S(1)} all-to-all(f32[16,8,768]{2,1,0:T(8,128)S(1)} %convolution_bitcast_fusion.1), channel_id=1, replica_groups=mesh['row'=16,'col_0'=8,'col_1'=2] {'row'}, dimensions={0} | all-to-all | bytes 786432 | tf_op jit(solution)/shard_map/all_to_all | solution.py:39
  29.5 4.1 %all-to-all-start.1 = ((f32[16,8,768]{2,1,0:T(8,128)}), f32[16,8,768]{2,1,0:T(8,128)S(1)}, u32[]{:S(2)}, u32[]{:S(2)}) async-start(f32[16,8,768]{2,1,0:T(8,128)} %broadcast_in_dim.13), calls=%async_computation.1 | async-start | bytes 786432 | tf_op jit(solution)/shard_map/all_to_all | solution.py:18
  33.6 3.8 %convolution_bitcast_fusion.2 = f32[768,128]{0,1:T(8,128)} fusion(f32[768,768]{1,0:T(8,128)} %param.4, bf16[128,12288]{1,0:T(8,128)(2,1)S(1)} %copy-done, s32[]{:T(128)S(6)} %select_n.37), kind=kOutput, calls=%fused_computation.8 | convolution fusion | flops 905969664 | bytes 2949124 | tf_op jit(solution)/shard_map/dot_general | solution.py:94
  37.5 1.9 copy.24
  39.4 2.2 all-to-all-done.1
  41.9 1.8 pad_maximum_fusion
  43.7 2.0 reshape_reshape.4
  47.0 7.7 %all_to_all.39 = f32[2,8,7168]{2,1,0:T(8,128)} all-to-all(f32[2,8,7168]{2,1,0:T(8,128)S(1)} %copy.25), channel_id=1, replica_groups=mesh['row'=16,'col_0'=8,'col_1'=2] {'col_1'}, dimensions={0} | all-to-all | bytes 917504 | tf_op jit(solution)/shard_map/all_to_all | solution.py:39
  54.6 1.8 reduce_sum.28
  57.5 18.3 %all_to_all.40 = f32[8,1,7168]{2,1,0:T(1,128)} all-to-all(f32[8,1,7168]{2,1,0:T(1,128)S(1)} %all_to_all.27), channel_id=1, replica_groups=mesh['row'=16,'col_0'=8,'col_1'=2] {'col_0'}, dimensions={0} | all-to-all | bytes 458752 | tf_op jit(solution)/shard_map/all_to_all | solution.py:59
  79.0 4.0 %all-to-all-start.4 = ((f32[8,1,7168]{2,1,0:T(1,128)}), f32[8,1,7168]{2,1,0:T(1,128)}, u32[]{:S(2)}, u32[]{:S(2)}) async-start(f32[8,1,7168]{2,1,0:T(1,128)} %broadcast_in_dim.14), calls=%async_computation.4 | async-start | bytes 458752 | tf_op jit(solution)/shard_map/all_to_all | solution.py:18
  83.8 8.1 %all-to-all-done.4 = f32[8,1,7168]{2,1,0:T(1,128)} async-done(((f32[8,1,7168]{2,1,0:T(1,128)}), f32[8,1,7168]{2,1,0:T(1,128)}, u32[]{:S(2)}, u32[]{:S(2)}) %all-to-all-start.4) | async-done | bytes 229408 | tf_op jit(solution)/shard_map/all_to_all | solution.py:18
  93.0 7.1 %all_to_all.41 = f32[2,8,7168]{2,1,0:T(8,128)S(1)} all-to-all(f32[2,8,7168]{2,1,0:T(8,128)S(1)} %broadcast_in_dim.15), channel_id=1, replica_groups=mesh['row'=16,'col_0'=8,'col_1'=2] {'col_1'}, dimensions={0} | all-to-all | bytes 917504 | tf_op jit(solution)/shard_map/all_to_all | solution.py:18
  101.2 2.2 slice.92
  111.0 13.2 %cholesky.53 = f32[128,128]{1,0:T(8,128)} custom-call(f32[128,128]{1,0:T(8,128)} %fusion.22), custom_call_target="Cholesky" | custom-call | tf_op jit(solution)/shard_map/jit(cholesky)/cholesky | solution.py:99
  125.7 2.1 fusion.15
  127.8 11.3 %custom-call.28 = f32[1,128,128]{1,2,0:T(8,128)} custom-call(f32[1,128,128]{2,1,0:T(8,128)} %fusion.15), custom_call_target="InvertDiagBlocksLowerTriangular" | custom-call | tf_op jit(solution)/shard_map/jit(_cho_solve)/triangular_solve | solution.py:100
  141.7 3.8 %convolution_subtract_fusion = f32[768,768]{1,0:T(8,128)S(1)} fusion(f32[768,768]{1,0:T(8,128)} %param.4, f32[128,768]{1,0:T(8,128)S(1)} %fusion.19, f32[896,128]{1,0:T(8,128)} %slice.92), kind=kOutput, calls=%fused_computation.4 | convolution fusion | flops 906559488 | bytes 5505024 | tf_op jit(solution)/shard_map/dot_general | solution.py:101
  148.0 87.5 %all-gather.10.cloned.1.call-done = f32[4096,768]{1,0:T(8,128)} async-done(((f32[256,768]{1,0:T(8,128)}), f32[4096,768]{1,0:T(8,128)}) %all-gather.10.cloned.1.call-update) | async-done | bytes 12582928 | tf_op jit(solution)/shard_map/all_gather | solution.py:78
  235.5 1.8 constant_dynamic-slice_fusion.2
  237.6 2.1 constant_dynamic-slice_fusion.4
  239.7 40.0 %all-gather.6.cloned.1.call-done = f32[16,256,256]{2,1,0:T(8,128)} async-done(((f32[1,256,256]{2,1,0:T(8,128)}), f32[16,256,256]{2,1,0:T(8,128)}) %all-gather.6.cloned.1.call-update) | async-done | bytes 4194320 | tf_op jit(solution)/shard_map/all_gather | solution.py:78
  285.1 11.7 %cholesky.106 = f32[128,128]{1,0:T(8,128)S(1)} custom-call(f32[128,128]{1,0:T(8,128)S(1)} %cholesky.132), custom_call_target="Cholesky" | custom-call | tf_op jit(solution)/shard_map/jit(cholesky)/cholesky | solution.py:114
  296.9 9.8 %custom-call.29 = f32[1,128,128]{1,2,0:T(8,128)S(1)} custom-call(f32[1,128,128]{2,1,0:T(8,128)S(1)} %get-tuple-element.23), custom_call_target="InvertDiagBlocksLowerTriangular" | custom-call | tf_op jit(solution)/shard_map/jit(cholesky)/cholesky | solution.py:114
  308.9 11.7 %cholesky.119 = f32[128,128]{1,0:T(8,128)S(1)} custom-call(f32[128,128]{1,0:T(8,128)S(1)} %convolution_subtract_fusion.3), custom_call_target="Cholesky" | custom-call | tf_op jit(solution)/shard_map/jit(cholesky)/cholesky | solution.py:114
  323.6 5.2 %while.1 = (s32[]{:T(128)}, f32[256,256]{1,0:T(8,128)S(1)}, s32[2,2]{1,0:T(2,128)S(1)}, f32[2,128,128]{2,1,0:T(8,128)}, s32[]{:T(128)}) while((s32[]{:T(128)}, f32[256,256]{1,0:T(8,128)S(1)}, s32[2,2]{1,0:T(2,128)S(1)}, f32[2,128,128]{2,1,0:T(8,128)}, s32[]{:T(128)}) %tuple.28), condition=%wide.while_cond, body=%wide.while_body.sunk | while | flops 2 | bytes 132705 | solution.py:115
  324.4 1.9 bitcast_dynamic-update-slice_fusion.2
  326.9 1.9 bitcast_dynamic-update-slice_fusion.2
  328.8 20.5 %custom-call.30 = f32[2,128,128]{1,2,0:T(8,128)S(1)} custom-call(f32[2,128,128]{2,1,0:T(8,128)} %get-tuple-element.9), custom_call_target="InvertDiagBlocksLowerTriangular" | custom-call | tf_op jit(solution)/shard_map/jit(_cho_solve)/triangular_solve | solution.py:115
  356.4 4.2 %subtract_convert_fusion = bf16[1536,768]{1,0:T(8,128)(2,1)} fusion(bf16[1536,768]{1,0:T(8,128)(2,1)} %param.5, bf16[16,1536,256]{2,1,0:T(8,128)(2,1)} %bitcast.102, s32[]{:T(128)S(6)} %select_n.42, bf16[128,768]{1,0:T(8,128)(2,1)} %get-tuple-element.26, bf16[128,768]{1,0:T(8,128)(2,1)S(1)} %convolution_convert_fusion), kind=kOutput, calls=%fused_computation.2 | convolution fusion | flops 608305152 | bytes 5898244 | tf_op jit(solution)/shard_map/dot_general | solution.py:116
  (60 shorter events, 42.4 us)
Async XLA Ops:
  7.2 1.9 copy-start
  29.5 12.1 %all-to-all-start.1 = ((f32[16,8,768]{2,1,0:T(8,128)}), f32[16,8,768]{2,1,0:T(8,128)S(1)}, u32[]{:S(2)}, u32[]{:S(2)}) async-start(f32[16,8,768]{2,1,0:T(8,128)} %broadcast_in_dim.13), calls=%async_computation.1 | async-start | bytes 786432 | tf_op jit(solution)/shard_map/all_to_all | solution.py:18
  79.0 12.9 %all-to-all-start.4 = ((f32[8,1,7168]{2,1,0:T(1,128)}), f32[8,1,7168]{2,1,0:T(1,128)}, u32[]{:S(2)}, u32[]{:S(2)}) async-start(f32[8,1,7168]{2,1,0:T(1,128)} %broadcast_in_dim.14), calls=%async_computation.4 | async-start | bytes 458752 | tf_op jit(solution)/shard_map/all_to_all | solution.py:18
  83.1 152.4 %all-gather.10.cloned.1.call-start = ((), (), s32[]{:S(2)}) async-start(), calls=%async_computation.8 | async-start | bytes 13369344 | tf_op jit(solution)/shard_map/all_gather | solution.py:78
  145.5 1.4 copy-start.1
  147.9 131.8 %all-gather.6.cloned.1.call-start = ((), (), s32[]{:S(2)}) async-start(), calls=%async_computation.6 | async-start | bytes 4456448 | tf_op jit(solution)/shard_map/all_gather | solution.py:78
  237.4 119.1 %all-gather.8.cloned.1.call-start = ((), (), s32[]{:S(2)}) async-start(), calls=%async_computation.7 | async-start | bytes 13369344 | tf_op jit(solution)/shard_map/all_gather | solution.py:78
  284.4 0.7 copy-start.3
  320.6 1.9 copy-start.2
Sparse Core Ops, SparseCore 0:
  148.0 87.4 all-gather.9
  237.5 42.1 all-gather.5
  282.1 74.2 all-gather.7
where the time goes:
time: 369 us; the launch traced here: 367 us
  waiting for transfers between devices  139 us (38%)
  other arithmetic  96 us (26%)
  blocking collectives  48.7 us (13%)
  local copies, waits for them, and re-layouts  33.2 us (9%)
  matrix products  25.2 us (7%)
  between operations  15.9 us (4%)
  starting transfers between devices  8.5 us (2%)
    all_gather x3, waiting for transfers between devices, picked(): lax.all_gather(x, axis)  129 us
    another operation x6, other arithmetic, per_device(): square_factor = jnp.linalg.cholesky(square)  34 us
    all_to_all x2, blocking collectives, sent_and_summed(): lax.all_to_all(parts, axis, split_axis=0, concat_axis=0, tiled=True)  23.3 us
    another operation x3, other arithmetic, per_device(): jax.scipy.linalg.cho_solve((square_factor, True), strip)  21.5 us
    all_to_all x1, blocking collectives, sum_in_two_steps(): return jnp.sum(lax.all_to_all(own, far, 0, 0, tiled=True), axis=0)  18.3 us
    another operation x3, other arithmetic, per_device(): factor = jnp.linalg.cholesky(inner)  14.7 us
    another operation x2, other arithmetic, per_device(): solved = jax.scipy.linalg.cho_solve((factor, True), left_cols)  13.4 us
    all_to_all x2, waiting for transfers between devices, from_everyone(): return lax.all_to_all(copies, axis, split_axis=0, concat_axis=0, tiled=True)  10.4 us
  transfers between devices with their start and end apart: 5, of which 5 were waited for; matrix products, arithmetic and copies ran while one was open for 22% of the time, Pallas kernels for 0%

commit v1 on v0

v1 whole, which is shorter than its diff:
```python
import jax
import jax.numpy as jnp
from jax import lax
from jax.sharding import Mesh
from jax.sharding import PartitionSpec as P

B = 256
COL = ("z", "core")
HIGHEST = lax.Precision.HIGHEST


def exchanged(parts, axis):
    return lax.all_to_all(parts, axis, split_axis=0, concat_axis=0, tiled=True)


def from_everyone(x, axis):
    return exchanged(jnp.broadcast_to(x, (lax.axis_size(axis), *x.shape)), axis)


def picked(parts, root):
    return lax.dynamic_index_in_dim(parts, root, 0, keepdims=False)


def from_all_columns(x):
    return from_everyone(from_everyone(x, "z"), "core")


def per_device(inv_hessian, weights, calib, block):
    tile_rows, tile = inv_hessian.shape
    peers = lax.axis_size("row")
    row = lax.axis_index("row")
    col = lax.axis_index(COL)
    start = block[0] * B
    owner = start // tile
    sub = (start - owner * tile) // B
    offset = sub * B
    groups = tile // B
    wide = tile // 128

    window = lax.dynamic_slice_in_dim(weights, offset, B, 1)
    lines = window.shape[0] // peers
    scattered = exchanged(window.reshape(2, -1, B), "core")
    scattered = picked(scattered.reshape(2, -1, B), owner % 2)
    scattered = exchanged(scattered.reshape(8, lines, B), "z")
    window_piece = picked(scattered, owner // 2)

    calib_rows = lax.dynamic_slice_in_dim(calib, row * tile_rows, tile_rows, 1).astype(jnp.float32)
    calib_cols = lax.dynamic_slice_in_dim(calib, col * tile, tile, 1).astype(jnp.float32)
    left_part = jnp.dot(calib_rows, inv_hessian, precision=HIGHEST)
    inner_part = jnp.dot(left_part, calib_cols.T, precision=HIGHEST)
    part = left_part.T
    strip = lax.dynamic_slice_in_dim(inv_hessian, offset, B, 0)
    thin = B // peers
    sent = jnp.concatenate(
        [
            part.reshape(groups, peers, thin, 128).swapaxes(0, 1).reshape(peers, -1, 128),
            inner_part.reshape(peers, -1, 128),
            strip.reshape(peers, thin, wide, 128).swapaxes(1, 2).reshape(peers, -1, 128),
        ],
        axis=1,
    )
    arrived = exchanged(sent, "row")
    piece_rows = groups * thin
    inner_rows = 128 // peers
    summed = arrived[:, : piece_rows + inner_rows].sum(axis=0)
    piece = summed[:piece_rows]
    strip_piece = picked(arrived, owner)[piece_rows + inner_rows :]

    n = peers
    turn = [(i * n + j, j * n + i) for i in range(n) for j in range(n)]
    turned = lax.ppermute(piece, ("row", *COL), turn)
    mine = picked(piece.reshape(groups, thin, 128), sub)
    mine_square = lax.dynamic_slice_in_dim(strip_piece.reshape(wide, thin, 128), 2 * sub, 2, 0)
    small = jnp.concatenate([summed[piece_rows:], mine, mine_square.reshape(-1, 128)], axis=0)
    small = lax.all_gather(small, COL)
    small = jnp.concatenate(
        [small[:, :inner_rows].sum(axis=0), picked(small, owner)[inner_rows:]], axis=0
    )
    large = from_everyone(jnp.concatenate([piece, strip_piece], axis=0), "row")
    small = from_everyone(small, "row")
    inner = small[:, :inner_rows].reshape(128, 128)
    block_right = small[:, inner_rows : inner_rows + thin].reshape(B, 128)
    square = small[:, inner_rows + thin :].reshape(peers, 2, thin, 128)
    square = square.swapaxes(1, 2).reshape(B, B)
    right_cols = large[:, :piece_rows].reshape(peers, groups, thin, 128)
    right_cols = right_cols.swapaxes(0, 1).reshape(tile, 128)
    strip = large[:, piece_rows:].reshape(peers, wide, thin, 128).swapaxes(1, 2).reshape(B, tile)

    right_rows = from_all_columns(turned).swapaxes(0, 1).reshape(peers, groups, thin, 128)
    right_rows = right_rows.swapaxes(0, 1).reshape(tile_rows, 128)
    window = from_all_columns(window_piece).reshape(window.shape)

    inner = jnp.eye(128, dtype=jnp.float32) + 0.5 * (inner + inner.T)
    factor = jnp.linalg.cholesky(inner)
    both = jnp.concatenate([block_right, right_cols], axis=0).T
    solved = jax.scipy.linalg.cho_solve((factor, True), both)
    changed = jnp.dot(block_right, solved, precision=HIGHEST)
    square = square - changed[:, :B]
    strip = strip - changed[:, B:]
    updated = inv_hessian - jnp.dot(right_rows, solved[:, B:], precision=HIGHEST)
    square = 0.5 * (square + square.T)
    square_factor = jnp.linalg.cholesky(square)
    comp = jax.scipy.linalg.cho_solve((square_factor, True), strip).astype(jnp.bfloat16)
    product = jnp.dot(window, comp, preferred_element_type=jnp.float32)
    pruned = (weights.astype(jnp.float32) - product).astype(jnp.bfloat16)
    return (updated, pruned)


def solution(mesh):
    finer = Mesh(mesh.devices.reshape(mesh.shape["row"], 8, 2), ("row", "z", "core"))
    specs = (P("row", COL), P("row", COL), P(), P())
    return jax.shard_map(
        per_device, mesh=finer, in_specs=specs, out_specs=specs[:2], check_vma=False
    )
```

time: 369 us -> 283 us (0.77)
  waiting for transfers between devices: 139 us -> 28.4 us
  starting transfers between devices: 8.5 us -> 57.2 us
  blocking collectives: 48.7 us -> 27 us
  between operations: 15.9 us -> 3.16 us
  local copies, waits for them, and re-layouts: 33.2 us -> 45.4 us
  matrix products: 25.2 us -> 21.5 us
    all_gather x3 -> x0, waiting for transfers between devices: 129 us -> none  [picked(): lax.all_gather(x, axis)]
    all_to_all x4 -> x1, blocking collectives: 48.7 us -> 3.84 us  [exchanged(): return lax.all_to_all(parts, axis, split_axis=0, concat_axis=0, tiled=True)]
    all_to_all x2 -> x8, starting transfers between devices: 8.16 us -> 51.4 us  [exchanged(): return lax.all_to_all(parts, axis, split_axis=0, concat_axis=0, tiled=True)]
    all_gather x0 -> x1, blocking collectives: none -> 23.2 us  [per_device(): small = lax.all_gather(small, COL)]
    all_to_all x2 -> x8, waiting for transfers between devices: 10.4 us -> 28 us  [exchanged(): return lax.all_to_all(parts, axis, split_axis=0, concat_axis=0, tiled=True)]
    reshape x0 -> x4, local copies, waits for them, and re-layouts: none -> 7.05 us  [the longest x2 3.03 us: per_device(): inner = small[:, :inner_rows].reshape(128, 128)]
    ppermute x0 -> x1, starting transfers between devices: none -> 5.75 us  [per_device(): turned = lax.ppermute(piece, ('row', *COL), turn)]
    broadcast_in_dim x3 -> x6, local copies, waits for them, and re-layouts: 3.09 us -> 7.63 us  [from_everyone(): return exchanged(jnp.broadcast_to(x, (lax.axis_size(axis), *x.shape)), axis)]
  transfers between devices with their start and end apart: 5 -> 9, of which waited for: 5 -> 6; matrix products, arithmetic and copies ran while one was open for 22% -> 53% of each run, Pallas kernels for 0% -> 0%
where the time goes in v1:
time: 283 us; the launch traced here: 280 us
  other arithmetic  97.8 us (35%)
  starting transfers between devices  57.2 us (20%)
  local copies, waits for them, and re-layouts  45.4 us (16%)
  waiting for transfers between devices  28.4 us (10%)
  blocking collectives  27 us (10%)
  matrix products  21.5 us (8%)
  between operations  3.16 us (1%)
    all_to_all x8, starting transfers between devices, exchanged(): return lax.all_to_all(parts, axis, split_axis=0, concat_axis=0, tiled=True)  51.4 us
    another operation x6, other arithmetic, per_device(): square_factor = jnp.linalg.cholesky(square)  34.2 us
    all_to_all x8, waiting for transfers between devices, exchanged(): return lax.all_to_all(parts, axis, split_axis=0, concat_axis=0, tiled=True)  28 us
    all_gather x1, blocking collectives, per_device(): small = lax.all_gather(small, COL)  23.2 us
    another operation x3, other arithmetic, per_device(): jax.scipy.linalg.cho_solve((square_factor, True), strip)  21.5 us
    another operation x3, other arithmetic, per_device(): factor = jnp.linalg.cholesky(inner)  14.8 us
    another operation x2, other arithmetic, per_device(): solved = jax.scipy.linalg.cho_solve((factor, True), both)  13.5 us
    broadcast_in_dim x6, local copies, waits for them, and re-layouts, from_everyone(): return exchanged(jnp.broadcast_to(x, (lax.axis_size(axis), *x.shape)), axis)  7.63 us
  transfers between devices with their start and end apart: 9, of which 6 were waited for; matrix products, arithmetic and copies ran while one was open for 53% of the time, Pallas kernels for 0%

profile of v1, /device:TPU:1, one launch (start us, length us, event | category | flops | bytes accessed | tf_op | source)
XLA Modules:
  0.0 280.4 jit_solution(10219303982682714574)
XLA Ops:
  1.5 2.2 constant_dynamic-slice_fusion.2
  3.7 7.5 %all-to-all-start.5 = ((bf16[2,768,256]{2,1,0:T(8,128)(2,1)}), bf16[2,768,256]{2,1,0:T(8,128)(2,1)}, u32[]{:S(2)}, u32[]{:S(2)}) async-start(bf16[2,768,256]{2,1,0:T(8,128)(2,1)} %bitcast.126), calls=%async_computation.5 | async-start | bytes 1572864 | tf_op jit(solution)/shard_map/all_to_all | solution.py:13
  14.6 6.5 %all-to-all-start.6 = ((bf16[8,96,256]{2,1,0:T(8,128)(2,1)}), bf16[8,96,256]{2,1,0:T(8,128)(2,1)}, u32[]{:S(2)}, u32[]{:S(2)}) async-start(bf16[8,96,256]{2,1,0:T(8,128)(2,1)} %bitcast.29), calls=%async_computation.6 | async-start | bytes 786432 | tf_op jit(solution)/shard_map/all_to_all | solution.py:13
  21.1 2.6 fusion.13
  26.4 2.1 constant_dynamic-slice_fusion.5
  28.5 2.2 reshape.113
  30.7 2.2 copy.39
  33.3 2.4 pad_maximum_fusion
  36.3 6.8 %all-to-all-start = ((f32[16,152,128]{2,1,0:T(8,128)}), f32[16,152,128]{2,1,0:T(8,128)}, u32[]{:S(2)}, u32[]{:S(2)}) async-start(f32[16,152,128]{2,1,0:T(8,128)} %pad_maximum_fusion), calls=%async_computation | async-start | bytes 2490368 | tf_op jit(solution)/shard_map/all_to_all | solution.py:13
  44.0 16.8 %all-to-all-done = f32[16,152,128]{2,1,0:T(8,128)} async-done(((f32[16,152,128]{2,1,0:T(8,128)}), f32[16,152,128]{2,1,0:T(8,128)}, u32[]{:S(2)}, u32[]{:S(2)}) %all-to-all-start) | async-done | bytes 1245216 | tf_op jit(solution)/shard_map/all_to_all | solution.py:13
  61.6 5.9 %all-to-all-start.7 = ((bf16[8,96,256]{2,1,0:T(8,128)(2,1)}), bf16[8,96,256]{2,1,0:T(8,128)(2,1)S(1)}, u32[]{:S(2)}, u32[]{:S(2)}) async-start(bf16[8,96,256]{2,1,0:T(8,128)(2,1)} %broadcast_in_dim.26), calls=%async_computation.7 | async-start | bytes 786432 | tf_op jit(solution)/shard_map/all_to_all | solution.py:13
  68.6 5.8 %collective-permute-start = (f32[48,128]{1,0:T(8,128)S(1)}, f32[48,128]{1,0:T(8,128)}, u32[]{:S(2)}, u32[]{:S(2)}) collective-permute-start(f32[48,128]{1,0:T(8,128)S(1)} %slice.156), channel_id=1, source_target_pairs={{0,0},{1,16},{2,32},{3,48},{4,64},{5,80},{6,96},{7,112},{8,128},{9... | collective-permute-start | bytes 73736 | tf_op jit(solution)/shard_map/ppermute | solution.py:71
  76.2 2.0 all-to-all-done.7
  79.6 9.6 %all-to-all-start.1 = ((f32[8,48,128]{2,1,0:T(8,128)}), f32[8,48,128]{2,1,0:T(8,128)}, u32[]{:S(2)}, u32[]{:S(2)}) async-start(f32[8,48,128]{2,1,0:T(8,128)} %broadcast_in_dim.22), calls=%async_computation.1 | async-start | bytes 393216 | tf_op jit(solution)/shard_map/all_to_all | solution.py:13
  89.2 23.2 %all-gather = f32[896,128]{1,0:T(8,128)S(1)} all-gather(f32[56,128]{1,0:T(8,128)} %pad_maximum_fusion.2), channel_id=2, replica_groups=mesh['row'=16,'z'=8,'core'=2] {'z','core'}, dimensions={0}, use_global_device_ids=true | all-gather | bytes 487424 | tf_op jit(solution)/shard_map/all_gather | solution.py:75
  114.0 3.8 %all_to_all.45 = f32[2,8,48,128]{3,2,1,0:T(8,128)S(1)} all-to-all(f32[2,8,48,128]{3,2,1,0:T(8,128)S(1)} %broadcast_in_dim.23), channel_id=1, replica_groups=mesh['row'=16,'z'=8,'core'=2] {'core'}, dimensions={0} | all-to-all | bytes 786432 | tf_op jit(solution)/shard_map/all_to_all | solution.py:13
  119.3 4.2 %all-to-all-start.3 = ((f32[16,56,128]{2,1,0:T(8,128)}), f32[16,56,128]{2,1,0:T(8,128)}, u32[]{:S(2)}, u32[]{:S(2)}) async-start(f32[16,56,128]{2,1,0:T(8,128)} %broadcast_in_dim.24), calls=%async_computation.3 | async-start | bytes 917504 | tf_op jit(solution)/shard_map/all_to_all | solution.py:13
  126.6 6.8 %all-to-all-done.3 = f32[16,56,128]{2,1,0:T(8,128)} async-done(((f32[16,56,128]{2,1,0:T(8,128)}), f32[16,56,128]{2,1,0:T(8,128)}, u32[]{:S(2)}, u32[]{:S(2)}) %all-to-all-start.3) | async-done | bytes 458784 | tf_op jit(solution)/shard_map/all_to_all | solution.py:13
  133.4 2.0 broadcast_in_dim.25
  135.3 4.5 %all-to-all-start.4 = ((f32[16,144,128]{2,1,0:T(8,128)}), f32[16,144,128]{2,1,0:T(8,128)}, u32[]{:S(2)}, u32[]{:S(2)}) async-start(f32[16,144,128]{2,1,0:T(8,128)} %broadcast_in_dim.25), calls=%async_computation.4 | async-start | bytes 2359296 | tf_op jit(solution)/shard_map/all_to_all | solution.py:13
  147.5 13.2 %cholesky.53 = f32[128,128]{1,0:T(8,128)} custom-call(f32[128,128]{1,0:T(8,128)} %fusion.22), custom_call_target="Cholesky" | custom-call | tf_op jit(solution)/shard_map/jit(cholesky)/cholesky | solution.py:94
  162.2 2.2 fusion.15
  164.4 11.3 %custom-call.28 = f32[1,128,128]{1,2,0:T(8,128)} custom-call(f32[1,128,128]{2,1,0:T(8,128)} %fusion.15), custom_call_target="InvertDiagBlocksLowerTriangular" | custom-call | tf_op jit(solution)/shard_map/jit(_cho_solve)/triangular_solve | solution.py:96
  181.9 6.4 %all-to-all-start.8 = ((bf16[2,8,96,256]{3,2,1,0:T(8,128)(2,1)}), bf16[2,8,96,256]{3,2,1,0:T(8,128)(2,1)}, u32[]{:S(2)}, u32[]{:S(2)}) async-start(bf16[2,8,96,256]{3,2,1,0:T(8,128)(2,1)} %broadcast_in_dim.27), calls=%async_computation.8 | async-start | bytes 1572864 | tf_op jit(solution)/shard_map/all_to_all | solution.py:13
  201.6 11.7 %cholesky.106 = f32[128,128]{1,0:T(8,128)S(1)} custom-call(f32[128,128]{1,0:T(8,128)S(1)} %cholesky.132), custom_call_target="Cholesky" | custom-call | tf_op jit(solution)/shard_map/jit(cholesky)/cholesky | solution.py:102
  213.4 9.8 %custom-call.29 = f32[1,128,128]{1,2,0:T(8,128)S(1)} custom-call(f32[1,128,128]{2,1,0:T(8,128)S(1)} %get-tuple-element.23), custom_call_target="InvertDiagBlocksLowerTriangular" | custom-call | tf_op jit(solution)/shard_map/jit(cholesky)/cholesky | solution.py:102
  225.4 11.9 %cholesky.119 = f32[128,128]{1,0:T(8,128)S(1)} custom-call(f32[128,128]{1,0:T(8,128)S(1)} %convolution_subtract_fusion.3), custom_call_target="Cholesky" | custom-call | tf_op jit(solution)/shard_map/jit(cholesky)/cholesky | solution.py:102
  240.3 5.3 %while.1 = (s32[]{:T(128)}, f32[256,256]{1,0:T(8,128)S(1)}, s32[2,2]{1,0:T(2,128)S(1)}, f32[2,128,128]{2,1,0:T(8,128)}, s32[]{:T(128)}) while((s32[]{:T(128)}, f32[256,256]{1,0:T(8,128)S(1)}, s32[2,2]{1,0:T(2,128)S(1)}, f32[2,128,128]{2,1,0:T(8,128)}, s32[]{:T(128)}) %tuple.28), condition=%wide.while_cond, body=%wide.while_body.sunk | while | flops 2 | bytes 132205 | solution.py:103
  243.6 2.0 bitcast_dynamic-update-slice_fusion.2
  245.6 20.5 %custom-call.30 = f32[2,128,128]{1,2,0:T(8,128)S(1)} custom-call(f32[2,128,128]{2,1,0:T(8,128)} %get-tuple-element.9), custom_call_target="InvertDiagBlocksLowerTriangular" | custom-call | tf_op jit(solution)/shard_map/jit(_cho_solve)/triangular_solve | solution.py:103
  272.9 3.4 %convolution_subtract_fusion = f32[768,768]{1,0:T(8,128)} fusion(f32[768,768]{1,0:T(8,128)S(1)} %copy-done.1, f32[768,128]{1,0:T(8,128)S(1)} %bitcast.132, f32[128,1024]{1,0:T(8,128)S(1)} %copy-done.3), kind=kOutput, calls=%fused_computation.3 | convolution fusion | flops 906559488 | bytes 5505024 | tf_op jit(solution)/shard_map/dot_general | solution.py:100
  276.3 4.1 %subtract_convert_fusion = bf16[1536,768]{1,0:T(8,128)(2,1)} fusion(bf16[1536,768]{1,0:T(8,128)(2,1)} %param.5, bf16[1536,256]{1,0:T(8,128)(2,1)} %bitcast.31, bf16[128,768]{1,0:T(8,128)(2,1)S(1)} %copy-done.10, bf16[128,768]{1,0:T(8,128)(2,1)S(1)} %convolution_convert_fusion), kind=kOutput, calls=%fused_computation.2 | convolution fusion | flops 608305152 | bytes 5898240 | tf_op jit(solution)/shard_map/dot_general | solution.py:104
  (107 shorter events, 61.8 us)
Async XLA Ops:
  0.6 20.5 %copy-start = (bf16[128,12288]{1,0:T(8,128)(2,1)S(1)}, bf16[128,12288]{1,0:T(8,128)(2,1)}, u32[]{:S(2)}) copy-start(bf16[128,12288]{1,0:T(8,128)(2,1)} %param.6) | copy-start | bytes 9437188
  3.7 9.2 %all-to-all-start.5 = ((bf16[2,768,256]{2,1,0:T(8,128)(2,1)}), bf16[2,768,256]{2,1,0:T(8,128)(2,1)}, u32[]{:S(2)}, u32[]{:S(2)}) async-start(bf16[2,768,256]{2,1,0:T(8,128)(2,1)} %bitcast.126), calls=%async_computation.5 | async-start | bytes 1572864 | tf_op jit(solution)/shard_map/all_to_all | solution.py:13
  14.6 21.7 %all-to-all-start.6 = ((bf16[8,96,256]{2,1,0:T(8,128)(2,1)}), bf16[8,96,256]{2,1,0:T(8,128)(2,1)}, u32[]{:S(2)}, u32[]{:S(2)}) async-start(bf16[8,96,256]{2,1,0:T(8,128)(2,1)} %bitcast.29), calls=%async_computation.6 | async-start | bytes 786432 | tf_op jit(solution)/shard_map/all_to_all | solution.py:13
  36.3 24.5 %all-to-all-start = ((f32[16,152,128]{2,1,0:T(8,128)}), f32[16,152,128]{2,1,0:T(8,128)}, u32[]{:S(2)}, u32[]{:S(2)}) async-start(f32[16,152,128]{2,1,0:T(8,128)} %pad_maximum_fusion), calls=%async_computation | async-start | bytes 2490368 | tf_op jit(solution)/shard_map/all_to_all | solution.py:13
  61.6 16.6 %all-to-all-start.7 = ((bf16[8,96,256]{2,1,0:T(8,128)(2,1)}), bf16[8,96,256]{2,1,0:T(8,128)(2,1)S(1)}, u32[]{:S(2)}, u32[]{:S(2)}) async-start(bf16[8,96,256]{2,1,0:T(8,128)(2,1)} %broadcast_in_dim.26), calls=%async_computation.7 | async-start | bytes 786432 | tf_op jit(solution)/shard_map/all_to_all | solution.py:13
  68.6 7.2 %copy-start.13 = (f32[48,128]{1,0:T(8,128)}, f32[48,128]{1,0:T(8,128)S(1)}, u32[]{:S(2)}) copy-start(f32[48,128]{1,0:T(8,128)S(1)} %slice.156) | copy-start | bytes 73732
  68.6 7.5 %collective-permute-start = (f32[48,128]{1,0:T(8,128)S(1)}, f32[48,128]{1,0:T(8,128)}, u32[]{:S(2)}, u32[]{:S(2)}) collective-permute-start(f32[48,128]{1,0:T(8,128)S(1)} %slice.156), channel_id=1, source_target_pairs={{0,0},{1,16},{2,32},{3,48},{4,64},{5,80},{6,96},{7,112},{8,128},{9... | collective-permute-start | bytes 73736 | tf_op jit(solution)/shard_map/ppermute | solution.py:71
  78.2 34.8 %copy-start.4 = (bf16[8,96,256]{2,1,0:T(8,128)(2,1)}, bf16[8,96,256]{2,1,0:T(8,128)(2,1)S(1)}, u32[]{:S(2)}) copy-start(bf16[8,96,256]{2,1,0:T(8,128)(2,1)S(1)} %all-to-all-done.7) | copy-start | bytes 1179652
  79.6 33.4 %all-to-all-start.1 = ((f32[8,48,128]{2,1,0:T(8,128)}), f32[8,48,128]{2,1,0:T(8,128)}, u32[]{:S(2)}, u32[]{:S(2)}) async-start(f32[8,48,128]{2,1,0:T(8,128)} %broadcast_in_dim.22), calls=%async_computation.1 | async-start | bytes 393216 | tf_op jit(solution)/shard_map/all_to_all | solution.py:13
  119.3 14.0 %all-to-all-start.3 = ((f32[16,56,128]{2,1,0:T(8,128)}), f32[16,56,128]{2,1,0:T(8,128)}, u32[]{:S(2)}, u32[]{:S(2)}) async-start(f32[16,56,128]{2,1,0:T(8,128)} %broadcast_in_dim.24), calls=%async_computation.3 | async-start | bytes 917504 | tf_op jit(solution)/shard_map/all_to_all | solution.py:13
  135.3 45.6 %copy-start.5 = (bf16[8,96,256]{2,1,0:T(8,128)(2,1)S(1)}, bf16[8,96,256]{2,1,0:T(8,128)(2,1)}, u32[]{:S(2)}) copy-start(bf16[8,96,256]{2,1,0:T(8,128)(2,1)} %copy-done.4) | copy-start | bytes 1179652
  135.3 45.6 %all-to-all-start.4 = ((f32[16,144,128]{2,1,0:T(8,128)}), f32[16,144,128]{2,1,0:T(8,128)}, u32[]{:S(2)}, u32[]{:S(2)}) async-start(f32[16,144,128]{2,1,0:T(8,128)} %broadcast_in_dim.25), calls=%async_computation.4 | async-start | bytes 2359296 | tf_op jit(solution)/shard_map/all_to_all | solution.py:13
  181.9 7.5 %copy-start.7 = (f32[16,16,128]{2,1,0:T(8,128)S(1)}, f32[16,16,128]{2,1,0:T(8,128)}, u32[]{:S(2)}) copy-start(f32[16,16,128]{2,1,0:T(8,128)} %slice.160) | copy-start | bytes 393220
  181.9 7.5 %copy-start.12 = (f32[1,128,128]{1,2,0:T(8,128)S(1)}, f32[1,128,128]{1,2,0:T(8,128)}, u32[]{:S(2)}) copy-start(f32[1,128,128]{1,2,0:T(8,128)} %custom-call.28) | copy-start | bytes 196612
  181.9 94.5 %all-to-all-start.8 = ((bf16[2,8,96,256]{3,2,1,0:T(8,128)(2,1)}), bf16[2,8,96,256]{3,2,1,0:T(8,128)(2,1)}, u32[]{:S(2)}, u32[]{:S(2)}) async-start(bf16[2,8,96,256]{3,2,1,0:T(8,128)(2,1)} %broadcast_in_dim.27), calls=%async_computation.8 | async-start | bytes 1572864 | tf_op jit(solution)/shard_map/all_to_all | solution.py:13
  190.6 2.6 copy-start.2
  200.9 0.7 copy-start.9
  237.3 2.0 copy-start.8
  266.1 4.9 %copy-start.11 = (f32[2,128,128]{1,2,0:T(8,128)}, f32[2,128,128]{1,2,0:T(8,128)S(1)}, u32[]{:S(2)}) copy-start(f32[2,128,128]{1,2,0:T(8,128)S(1)} %custom-call.30) | copy-start | bytes 393220
  267.7 5.2 %copy-start.1 = (f32[768,768]{1,0:T(8,128)S(1)}, f32[768,768]{1,0:T(8,128)}, u32[]{:S(2)}) copy-start(f32[768,768]{1,0:T(8,128)} %param.4) | copy-start | bytes 7077892
  267.7 5.2 %copy-start.3 = (f32[128,1024]{1,0:T(8,128)S(1)}, f32[128,1024]{1,0:T(8,128)}, u32[]{:S(2)}) copy-start(f32[128,1024]{1,0:T(8,128)} %copy-done.2) | copy-start | bytes 1572868
  267.7 5.2 %copy-start.6 = (f32[3,16,16,128]{3,2,1,0:T(8,128)S(1)}, f32[3,16,16,128]{3,2,1,0:T(8,128)}, u32[]{:S(2)}) copy-start(f32[3,16,16,128]{3,2,1,0:T(8,128)} %copy.41) | copy-start | bytes 1179652
  272.9 3.5 %copy-start.10 = (bf16[128,768]{1,0:T(8,128)(2,1)S(1)}, bf16[128,768]{1,0:T(8,128)(2,1)}, u32[]{:S(2)}) copy-start(bf16[128,768]{1,0:T(8,128)(2,1)} %get-tuple-element.26) | copy-start | bytes 589828

commit v2 on v1

v2 whole, which is shorter than its diff:
```python
import jax
import jax.numpy as jnp
from jax import lax
from jax.experimental import pallas as pl
from jax.experimental.pallas import tpu as pltpu
from jax.sharding import Mesh
from jax.sharding import PartitionSpec as P

B = 256
L = 128
COL = ("z", "core")
F32 = jnp.float32
BF16 = jnp.bfloat16
HIGHEST = lax.Precision.HIGHEST


def exchanged(parts, axis):
    return lax.all_to_all(parts, axis, split_axis=0, concat_axis=0, tiled=True)


def dot(a, b, dims=((1,), (0,))):
    return lax.dot_general(a, b, (dims, ((), ())), precision=HIGHEST, preferred_element_type=F32)


def dot_nt(a, b):
    return dot(a, b, ((1,), (1,)))


def in_three(x):
    first = x.astype(BF16)
    rest = x - first.astype(F32)
    second = rest.astype(BF16)
    third = (rest - second.astype(F32)).astype(BF16)
    return first, second, third


def place_of(block_ref, groups):
    owner = block_ref[0] // groups
    return owner, block_ref[0] - owner * groups


def first_kernel(block_ref, h_ref, calib_ref, w_ref, sent_ref, window_ref, rows_ref, cols_ref, sems):
    n, lines, _ = window_ref.shape
    tile = h_ref.shape[1]
    groups, wide, thin = tile // B, tile // L, B // n
    _, sub = place_of(block_ref, groups)
    row = lax.axis_index("row")
    col = lax.axis_index("z") * lax.axis_size("core") + lax.axis_index("core")
    offset = pl.multiple_of(sub * B, B)
    copies = [
        pltpu.make_async_copy(
            calib_ref.at[:, pl.ds(pl.multiple_of(row * tile, L), tile)], rows_ref, sems.at[0]
        ),
        pltpu.make_async_copy(
            calib_ref.at[:, pl.ds(pl.multiple_of(col * tile, L), tile)], cols_ref, sems.at[1]
        ),
        pltpu.make_async_copy(w_ref.at[:, :, pl.ds(offset, B)], window_ref, sems.at[2]),
    ]
    for copy in copies:
        copy.start()
    copies[0].wait()
    copies[1].wait()
    first, second, third = in_three(h_ref[...])
    rows = rows_ref[...]
    left = jnp.dot(rows, first, preferred_element_type=F32)
    left += jnp.dot(rows, second, preferred_element_type=F32)
    left += jnp.dot(rows, third, preferred_element_type=F32)
    right = left.T
    cols = cols_ref[...]
    dims = (((1,), (1,)), ((), ()))
    first, second, third = in_three(left)
    inner = lax.dot_general(first, cols, dims, preferred_element_type=F32)
    inner += lax.dot_general(second, cols, dims, preferred_element_type=F32)
    inner += lax.dot_general(third, cols, dims, preferred_element_type=F32)
    cut = L // n
    for p in range(n):
        for s in range(groups):
            at = s * B + p * thin
            sent_ref[p, s * thin : (s + 1) * thin, :] = right[at : at + thin]
        at = groups * thin
        sent_ref[p, at : at + cut, :] = inner[p * cut : (p + 1) * cut]
        at += cut
        for w in range(wide):
            sent_ref[p, at + w * thin : at + (w + 1) * thin, :] = h_ref[
                pl.ds(pl.multiple_of(offset + p * thin, thin), thin), w * L : (w + 1) * L
            ]
    copies[2].wait()


def second_kernel(block_ref, arrived_ref, small_ref, piece_ref, strip_ref):
    n = arrived_ref.shape[0]
    rows = piece_ref.shape[0]
    thin, cut = B // n, L // n
    owner, sub = place_of(block_ref, rows // thin)
    total = arrived_ref[0, 0 : rows + cut, :]
    for p in range(1, n):
        total = total + arrived_ref[p, 0 : rows + cut, :]
    piece_ref[...] = total[:rows]
    strip_ref[...] = arrived_ref[owner, rows + cut :, :]
    small_ref[0:cut] = total[rows:]
    small_ref[cut : cut + thin] = piece_ref[pl.ds(pl.multiple_of(sub * thin, thin), thin), :]
    small_ref[cut + thin :] = strip_ref[
        pl.ds(pl.multiple_of(2 * sub * thin, 2 * thin), 2 * thin), :
    ]


def third_kernel(block_ref, gathered_ref, piece_ref, strip_ref, sent_ref, right_ref):
    n = gathered_ref.shape[0]
    rows = piece_ref.shape[0]
    thin, cut = B // n, L // n
    groups = rows // thin
    owner, _ = place_of(block_ref, groups)
    small = gathered_ref.shape[1] - rows
    total = gathered_ref[0, 0:cut, :]
    for p in range(1, n):
        total = total + gathered_ref[p, 0:cut, :]
    chosen = gathered_ref[owner, cut:small, :]
    piece, strip = piece_ref[...], strip_ref[...]
    for p in range(n):
        sent_ref[p, 0:cut, :] = total
        sent_ref[p, cut:small, :] = chosen
        sent_ref[p, small : small + rows, :] = piece
        sent_ref[p, small + rows :, :] = strip
        for s in range(groups):
            at = s * B + p * thin
            right_ref[at : at + thin, :] = gathered_ref[
                p, small + s * thin : small + (s + 1) * thin, :
            ]


def invert(a_ref):
    lane = lax.broadcasted_iota(jnp.int32, (8, L), 1)
    sub = lax.broadcasted_iota(jnp.int32, (8, L), 0)
    wide_lane = lax.broadcasted_iota(jnp.int32, (L, L), 1)

    def step(k, carry):
        base = pl.multiple_of(8 * k, 8)
        panel = a_ref[pl.ds(base, 8), :]
        columns = [
            jnp.broadcast_to(
                jnp.sum(jnp.where(lane == base + j, panel, 0.0), axis=1, keepdims=True), (8, L)
            )
            for j in range(8)
        ]
        whole = a_ref[...]
        factors = [
            jnp.sum(jnp.where(wide_lane == base + j, whole, 0.0), axis=1, keepdims=True)
            for j in range(8)
        ]
        for j in range(8):
            own = columns[j]
            inverse = 1.0 / own[j : j + 1, :]
            here = sub == j
            panel = jnp.where(lane == base + j, jnp.where(here, 1.0, 0.0), panel)
            scaled = panel[j : j + 1, :] * inverse
            panel = jnp.where(here, scaled, panel - own * scaled)
            for m in range(j + 1, 8):
                scaled = columns[m][j : j + 1, :] * inverse
                columns[m] = jnp.where(here, scaled, columns[m] - own * scaled)
        inside = (wide_lane >= base) & (wide_lane < base + 8)
        rest = jnp.where(inside, 0.0, whole)
        for j in range(8):
            rest = rest - factors[j] * panel[j : j + 1, :]
        a_ref[...] = rest
        a_ref[pl.ds(base, 8), :] = panel
        return carry

    lax.fori_loop(0, L // 8, step, 0)


def fourth_kernel(c_ref, solved_ref, comp_ref, a_ref, gm_ref, gc_ref, q_ref, st_ref):
    n = c_ref.shape[0]
    tile = gc_ref.shape[0]
    thin, cut, groups, wide = B // n, L // n, tile // B, tile // L
    for p in range(n):
        a_ref[p * cut : (p + 1) * cut, :] = c_ref[p, 0:cut, :]
        at = cut
        gm_ref[p * thin : (p + 1) * thin, :] = c_ref[p, at : at + thin, :]
        at += thin
        for w in range(2):
            q_ref[p * thin : (p + 1) * thin, w * L : (w + 1) * L] = c_ref[p, at : at + thin, :]
            at += thin
        for s in range(groups):
            gc_ref[s * B + p * thin : s * B + (p + 1) * thin, :] = c_ref[p, at : at + thin, :]
            at += thin
        for w in range(wide):
            st_ref[p * thin : (p + 1) * thin, w * L : (w + 1) * L] = c_ref[p, at : at + thin, :]
            at += thin
    inner = a_ref[...]
    same = lax.broadcasted_iota(jnp.int32, (L, L), 0) == lax.broadcasted_iota(
        jnp.int32, (L, L), 1
    )
    a_ref[...] = jnp.where(same, 1.0, 0.0) + 0.5 * (inner + inner.T)
    invert(a_ref)
    x = a_ref[...]
    block_right = gm_ref[...]
    right = gc_ref[...]
    half = dot(block_right, x)
    solved_ref[...] = dot(right, x)
    square = q_ref[...] - dot_nt(half, block_right)
    square = 0.5 * (square + square.T)
    a_ref[...] = square[:L, :L]
    st_ref[...] = st_ref[...] - dot_nt(half, right)
    invert(a_ref)
    u = a_ref[...]
    v = dot(square[L:, :L], u)
    a_ref[...] = square[L:, L:] - dot(v, square[:L, L:])
    top = st_ref[0:L, :]
    first = dot(u, top)
    second = st_ref[L:, :] - dot(v, top)
    invert(a_ref)
    second = dot(a_ref[...], second)
    comp_ref[0:L, :] = (first - dot(v.T, second)).astype(BF16)
    comp_ref[L:, :] = second.astype(BF16)


VMEM = pl.BlockSpec(memory_space=pltpu.VMEM)
PARAMS = pltpu.CompilerParams(vmem_limit_bytes=20 * 2**20)
SMEM = pl.BlockSpec(memory_space=pltpu.SMEM)
HBM = pl.BlockSpec(memory_space=pltpu.HBM)


def of(shape, dtype=F32):
    return jax.ShapeDtypeStruct(shape, dtype)


def per_device(inv_hessian, weights, calib, block):
    tile = inv_hessian.shape[0]
    n = lax.axis_size("row")
    lines = weights.shape[0] // n
    thin, cut, groups, wide = B // n, L // n, tile // B, tile // L
    rows = groups * thin
    strip_rows = wide * thin
    small_rows = cut + 3 * thin
    sent, window = pl.pallas_call(
        first_kernel,
        out_shape=(of((n, rows + cut + strip_rows, L)), of((n, lines, B), BF16)),
        in_specs=[SMEM, VMEM, HBM, HBM],
        out_specs=(VMEM, HBM),
        scratch_shapes=[
            pltpu.VMEM((L, tile), BF16),
            pltpu.VMEM((L, tile), BF16),
            pltpu.SemaphoreType.DMA((3,)),
        ],
        compiler_params=PARAMS,
        name="first",
    )(block, inv_hessian, calib, weights.reshape(n, lines, tile))
    arrived = exchanged(sent, "row")
    scattered = exchanged(window, COL)
    small, piece, strip = pl.pallas_call(
        second_kernel,
        out_shape=(of((small_rows, L)), of((rows, L)), of((strip_rows, L))),
        in_specs=[SMEM, VMEM],
        out_specs=(VMEM, VMEM, VMEM),
        compiler_params=PARAMS,
        name="second",
    )(block, arrived)
    turn = [(i * n + j, j * n + i) for i in range(n) for j in range(n)]
    turned = lax.ppermute(piece, ("row", *COL), turn)
    gathered = lax.all_gather(jnp.concatenate([small, turned], axis=0), COL)
    sent, right_rows = pl.pallas_call(
        third_kernel,
        out_shape=(of((n, small_rows + rows + strip_rows, L)), of((tile, L))),
        in_specs=[SMEM, VMEM, VMEM, VMEM],
        out_specs=(VMEM, VMEM),
        compiler_params=PARAMS,
        name="third",
    )(block, gathered, piece, strip)
    arrived = exchanged(sent, "row")
    owner = block[0] // groups
    window = lax.dynamic_index_in_dim(scattered, owner, 0, keepdims=False)
    window = exchanged(jnp.broadcast_to(window, (n, lines, B)), COL).reshape(n * lines, B)
    solved, comp = pl.pallas_call(
        fourth_kernel,
        out_shape=(of((tile, L)), of((B, tile), BF16)),
        in_specs=[VMEM],
        out_specs=(VMEM, VMEM),
        scratch_shapes=[
            pltpu.VMEM((L, L), F32),
            pltpu.VMEM((B, L), F32),
            pltpu.VMEM((tile, L), F32),
            pltpu.VMEM((B, B), F32),
            pltpu.VMEM((B, tile), F32),
        ],
        cost_estimate=pl.CostEstimate(
            flops=20_000_000_000, bytes_accessed=4_000_000, transcendentals=0
        ),
        compiler_params=PARAMS,
        name="fourth",
    )(arrived)
    updated = inv_hessian - dot_nt(right_rows, solved)
    product = jnp.dot(window, comp, preferred_element_type=F32)
    pruned = (weights.astype(F32) - product).astype(BF16)
    return (updated, pruned)


def solution(mesh):
    finer = Mesh(mesh.devices.reshape(mesh.shape["row"], 8, 2), ("row", "z", "core"))
    specs = (P("row", COL), P("row", COL), P(), P())
    return jax.shard_map(
        per_device, mesh=finer, in_specs=specs, out_specs=specs[:2], check_vma=False
    )
```

time: 283 us -> 150 us (0.53)
  other arithmetic: 97.8 us -> 0.01 us
  local copies, waits for them, and re-layouts: 45.4 us -> 6.19 us
  blocking collectives: 27 us -> 60.5 us
  starting transfers between devices: 57.2 us -> 25.1 us
  Pallas kernels: 0 us -> 17.3 us
  matrix products: 21.5 us -> 6.76 us
  waiting for transfers between devices: 28.4 us -> 32 us
    another operation x14 -> x0, other arithmetic: 83.9 us -> none  [the longest x6 34.2 us: per_device(): square_factor = jnp.linalg.cholesky(square)]
    all_to_all x8 -> x3, starting transfers between devices: 51.4 us -> 23 us  [exchanged(): return lax.all_to_all(parts, axis, split_axis=0, concat_axis=0, tiled=True)]
    all_to_all x1, blocking collectives: 3.84 us -> 25.3 us  [exchanged(): return lax.all_to_all(parts, axis, split_axis=0, concat_axis=0, tiled=True)]
    pallas_call x0 -> x4, Pallas kernels: none -> 17.3 us  [the longest x1 14.6 us: per_device(): pl.pallas_call(fourth_kernel, out_shape=(of((tile, L)), of((B, tile), BF1...]
    all_gather x1, blocking collectives: 23.2 us -> 35.2 us  [per_device(): gathered = lax.all_gather(jnp.concatenate([small, turned], axis=0), COL)]
    another operation x10 -> x0, matrix products: 10.1 us -> none  [the longest x6 6.68 us: per_device(): jax.scipy.linalg.cho_solve((square_factor, True), strip)]
    reshape x4 -> x0, local copies, waits for them, and re-layouts: 7.05 us -> none  [the longest x2 3.03 us: per_device(): inner = small[:, :inner_rows].reshape(128, 128)]
    broadcast_in_dim x6 -> x1, local copies, waits for them, and re-layouts: 7.63 us -> 0.96 us  [per_device(): jnp.broadcast_to(window, (n, lines, B))]
  transfers between devices with their start and end apart: 9 -> 4, of which waited for: 6 -> 3; matrix products, arithmetic and copies ran while one was open for 53% -> 2% of each run, Pallas kernels for 0% -> 11%
where the time goes in v2:
time: 150 us; the launch traced here: 149 us
  blocking collectives  60.5 us (40%)
  waiting for transfers between devices  32 us (21%)
  starting transfers between devices  25.1 us (17%)
  Pallas kernels  17.3 us (12%)
  matrix products  6.76 us (5%)
  local copies, waits for them, and re-layouts  6.19 us (4%)
    all_gather x1, blocking collectives, per_device(): gathered = lax.all_gather(jnp.concatenate([small, turned], axis=0), COL)  35.2 us
    all_to_all x3, waiting for transfers between devices, exchanged(): return lax.all_to_all(parts, axis, split_axis=0, concat_axis=0, tiled=True)  29 us
    all_to_all x1, blocking collectives, exchanged(): return lax.all_to_all(parts, axis, split_axis=0, concat_axis=0, tiled=True)  25.3 us
    all_to_all x3, starting transfers between devices, exchanged(): return lax.all_to_all(parts, axis, split_axis=0, concat_axis=0, tiled=True)  23 us
    pallas_call x1, Pallas kernels, per_device(): pl.pallas_call(fourth_kernel, out_shape=(of((tile, L)), of((B, tile), BF1...  14.6 us
    unnamed x10, local copies, waits for them, and re-layouts  5.22 us
    dot_general x1, matrix products, dot(): lax.dot_general(a, b, (dims, ((), ())), precision=HIGHEST, preferred_elem...  3.44 us
    dot_general x1, matrix products, per_device(): product = jnp.dot(window, comp, preferred_element_type=F32)  3.32 us
  transfers between devices with their start and end apart: 4, of which 3 were waited for; matrix products, arithmetic and copies ran while one was open for 2% of the time, Pallas kernels for 11%

profile of v2, /device:TPU:1, one launch (start us, length us, event | category | flops | bytes accessed | tf_op | source)
XLA Modules:
  0.0 149.2 jit_solution(18414038705021944648)
XLA Ops:
  1.3 0.0 copy-start
  1.3 1.7 %copy-done = f32[768,768]{1,0:T(8,128)S(1)} copy-done((f32[768,768]{1,0:T(8,128)S(1)}, f32[768,768]{1,0:T(8,128)}, u32[]{:S(2)}) %copy-start) | copy-done | bytes 2359320
  2.9 0.0 copy-start.2
  2.9 1.7 %copy-done.2 = bf16[1536,768]{1,0:T(8,128)(2,1)S(1)} copy-done((bf16[1536,768]{1,0:T(8,128)(2,1)S(1)}, bf16[1536,768]{1,0:T(8,128)(2,1)}, u32[]{:S(2)}) %copy-start.2) | copy-done | bytes 2359320
  4.6 0.0 copy-start.4
  4.6 1.9 %copy-done.4 = bf16[128,12288]{1,0:T(8,128)(2,1)S(1)} copy-done((bf16[128,12288]{1,0:T(8,128)(2,1)S(1)}, bf16[128,12288]{1,0:T(8,128)(2,1)}, u32[]{:S(2)}) %copy-start.4) | copy-done | bytes 3145752
  6.5 1.4 first.1
  7.9 25.3 %all_to_all.20.arrived_ref = f32[16,152,128]{2,1,0:T(8,128)S(1)} all-to-all(f32[16,152,128]{2,1,0:T(8,128)S(1)} %get-tuple-element.11), channel_id=1, replica_groups=mesh['row'=16,'z'=8,'core'=2] {'row'}, dimensions={0} | all-to-all | bytes 2490368 | tf_op jit(solution)/shard_map/all_to_all | solution.py:18
  33.2 10.6 %all-to-all-start.2 = ((bf16[16,96,256]{2,1,0:T(8,128)(2,1)}), bf16[16,96,256]{2,1,0:T(8,128)(2,1)S(1)}, u32[]{:S(2)}, u32[]{:S(2)}) async-start(bf16[16,96,256]{2,1,0:T(8,128)(2,1)} %get-tuple-element.18), calls=%async_computation.2 | async-start | bytes 1572864 | tf_op jit(solution)/shard_map/all_to_all | solution.py:18
  43.8 2.1 %collective-permute-start = (f32[48,128]{1,0:T(8,128)S(1)}, f32[48,128]{1,0:T(8,128)S(1)}, u32[]{:S(2)}, u32[]{:S(2)}) collective-permute-start(f32[48,128]{1,0:T(8,128)S(1)} %get-tuple-element.13.piece_ref), channel_id=1, source_target_pairs={{0,0},{1,16},{2,32},{3,48},{4,64},{5,80},{6,96},{7,112},{8,128},{9... | collective-permute-start | bytes 73736 | tf_op jit(solution)/shard_map/ppermute | solution.py:259
  45.9 3.1 %collective-permute-done = f32[48,128]{1,0:T(8,128)S(1)} collective-permute-done((f32[48,128]{1,0:T(8,128)S(1)}, f32[48,128]{1,0:T(8,128)S(1)}, u32[]{:S(2)}, u32[]{:S(2)}) %collective-permute-start) | collective-permute-done | bytes 24608 | tf_op jit(solution)/shard_map/ppermute | solution.py:259
  48.9 35.2 %all-gather = f32[1664,128]{1,0:T(8,128)S(1)} all-gather(f32[104,128]{1,0:T(8,128)S(1)} %pad_maximum_fusion), channel_id=2, replica_groups=mesh['row'=16,'z'=8,'core'=2] {'z','core'}, dimensions={0}, use_global_device_ids=true | all-gather | bytes 905216 | tf_op jit(solution)/shard_map/all_gather | solution.py:260
  84.1 1.3 third.1
  85.4 0.0 all-to-all-done.2
  85.4 6.6 %all-to-all-start.1 = ((f32[16,200,128]{2,1,0:T(8,128)}), f32[16,200,128]{2,1,0:T(8,128)S(1)}, u32[]{:S(2)}, u32[]{:S(2)}) async-start(f32[16,200,128]{2,1,0:T(8,128)} %get-tuple-element.16), calls=%async_computation.1 | async-start | bytes 3276800 | tf_op jit(solution)/shard_map/all_to_all | solution.py:18
  92.1 24.2 %all-to-all-done.1.c_ref = f32[16,200,128]{2,1,0:T(8,128)S(1)} async-done(((f32[16,200,128]{2,1,0:T(8,128)}), f32[16,200,128]{2,1,0:T(8,128)S(1)}, u32[]{:S(2)}, u32[]{:S(2)}) %all-to-all-start.1) | async-done | bytes 1638432 | tf_op jit(solution)/shard_map/all_to_all | solution.py:18
  116.2 1.0 broadcast_in_dim.3
  117.2 5.8 %all-to-all-start.3 = ((bf16[16,96,256]{2,1,0:T(8,128)(2,1)}), bf16[16,96,256]{2,1,0:T(8,128)(2,1)}, u32[]{:S(2)}, u32[]{:S(2)}) async-start(bf16[16,96,256]{2,1,0:T(8,128)(2,1)} %broadcast_in_dim.3), calls=%async_computation.3 | async-start | bytes 1572864 | tf_op jit(solution)/shard_map/all_to_all | solution.py:18
  123.0 0.0 copy-start.1
  123.0 14.6 %fourth.1 = (f32[768,128]{1,0:T(8,128)S(1)}, bf16[256,768]{1,0:T(8,128)(2,1)S(1)}) custom-call(f32[16,200,128]{2,1,0:T(8,128)S(1)} %all-to-all-done.1.c_ref), custom_call_target="tpu_custom_call" | custom-call | flops 20000000000 | bytes 4000000 | tf_op jit(solution)/shard_map/fourth/pallas_call | solution.py:273
  137.6 0.0 copy-done.1
  137.6 0.0 copy-start.3
  137.7 3.4 %convolution_subtract_fusion = f32[768,768]{1,0:T(8,128)} fusion(f32[768,768]{1,0:T(8,128)S(1)} %copy-done.1, f32[768,128]{1,0:T(8,128)S(1)} %get-tuple-element.15, f32[768,128]{1,0:T(8,128)S(1)} %get-tuple-element.17), kind=kOutput, calls=%fused_computation.1 | convolution fusion | flops 906559488 | bytes 5505024 | tf_op jit(solution)/shard_map/dot_general | solution.py:22
  141.1 4.8 %all-to-all-done.3 = bf16[16,96,256]{2,1,0:T(8,128)(2,1)} async-done(((bf16[16,96,256]{2,1,0:T(8,128)(2,1)}), bf16[16,96,256]{2,1,0:T(8,128)(2,1)}, u32[]{:S(2)}, u32[]{:S(2)}) %all-to-all-start.3) | async-done | bytes 786464 | tf_op jit(solution)/shard_map/all_to_all | solution.py:18
  145.9 0.0 copy-done.3
  145.9 3.3 %subtract_convert_fusion = bf16[1536,768]{1,0:T(8,128)(2,1)} fusion(bf16[1536,768]{1,0:T(8,128)(2,1)S(1)} %copy-done.3, bf16[1536,256]{1,0:T(8,128)(2,1)} %bitcast.5, bf16[256,768]{1,0:T(8,128)(2,1)S(1)} %get-tuple-element.19), kind=kOutput, calls=%fused_computation | convolution fusion | flops 607518720 | bytes 5898240 | tf_op jit(solution)/shard_map/dot_general | solution.py:292
  (3 shorter events, 0.0 us)
Async XLA Ops:
  1.3 1.7 %copy-start = (f32[768,768]{1,0:T(8,128)S(1)}, f32[768,768]{1,0:T(8,128)}, u32[]{:S(2)}) copy-start(f32[768,768]{1,0:T(8,128)} %h_ref.1) | copy-start | bytes 7077892
  2.9 1.7 %copy-start.2 = (bf16[1536,768]{1,0:T(8,128)(2,1)S(1)}, bf16[1536,768]{1,0:T(8,128)(2,1)}, u32[]{:S(2)}) copy-start(bf16[1536,768]{1,0:T(8,128)(2,1)} %param.5) | copy-start | bytes 7077892
  4.6 1.9 %copy-start.4 = (bf16[128,12288]{1,0:T(8,128)(2,1)S(1)}, bf16[128,12288]{1,0:T(8,128)(2,1)}, u32[]{:S(2)}) copy-start(bf16[128,12288]{1,0:T(8,128)(2,1)} %calib_ref.1) | copy-start | bytes 9437188
  33.2 52.3 %all-to-all-start.2 = ((bf16[16,96,256]{2,1,0:T(8,128)(2,1)}), bf16[16,96,256]{2,1,0:T(8,128)(2,1)S(1)}, u32[]{:S(2)}, u32[]{:S(2)}) async-start(bf16[16,96,256]{2,1,0:T(8,128)(2,1)} %get-tuple-element.18), calls=%async_computation.2 | async-start | bytes 1572864 | tf_op jit(solution)/shard_map/all_to_all | solution.py:18
  43.8 5.1 %collective-permute-start = (f32[48,128]{1,0:T(8,128)S(1)}, f32[48,128]{1,0:T(8,128)S(1)}, u32[]{:S(2)}, u32[]{:S(2)}) collective-permute-start(f32[48,128]{1,0:T(8,128)S(1)} %get-tuple-element.13.piece_ref), channel_id=1, source_target_pairs={{0,0},{1,16},{2,32},{3,48},{4,64},{5,80},{6,96},{7,112},{8,128},{9... | collective-permute-start | bytes 73736 | tf_op jit(solution)/shard_map/ppermute | solution.py:259
  85.4 30.8 %all-to-all-start.1 = ((f32[16,200,128]{2,1,0:T(8,128)}), f32[16,200,128]{2,1,0:T(8,128)S(1)}, u32[]{:S(2)}, u32[]{:S(2)}) async-start(f32[16,200,128]{2,1,0:T(8,128)} %get-tuple-element.16), calls=%async_computation.1 | async-start | bytes 3276800 | tf_op jit(solution)/shard_map/all_to_all | solution.py:18
  117.2 28.7 %all-to-all-start.3 = ((bf16[16,96,256]{2,1,0:T(8,128)(2,1)}), bf16[16,96,256]{2,1,0:T(8,128)(2,1)}, u32[]{:S(2)}, u32[]{:S(2)}) async-start(bf16[16,96,256]{2,1,0:T(8,128)(2,1)} %broadcast_in_dim.3), calls=%async_computation.3 | async-start | bytes 1572864 | tf_op jit(solution)/shard_map/all_to_all | solution.py:18
  123.0 14.6 %copy-start.1 = (f32[768,768]{1,0:T(8,128)S(1)}, f32[768,768]{1,0:T(8,128)}, u32[]{:S(2)}) copy-start(f32[768,768]{1,0:T(8,128)} %h_ref.1) | copy-start | bytes 7077892
  137.6 8.3 %copy-start.3 = (bf16[1536,768]{1,0:T(8,128)(2,1)S(1)}, bf16[1536,768]{1,0:T(8,128)(2,1)}, u32[]{:S(2)}) copy-start(bf16[1536,768]{1,0:T(8,128)(2,1)} %param.5) | copy-start | bytes 7077892

commit v3 on v2

v3 whole, which is shorter than its diff:
```python
from functools import partial

import jax
import jax.numpy as jnp
from jax import lax
from jax.experimental import pallas as pl
from jax.experimental.pallas import tpu as pltpu
from jax.sharding import Mesh
from jax.sharding import PartitionSpec as P

B = 256
L = 128
ROW = ("x", "y")
COL = ("z", "core")
F32 = jnp.float32
BF16 = jnp.bfloat16
HIGHEST = lax.Precision.HIGHEST


def exchanged(parts, axis):
    return lax.all_to_all(parts, axis, split_axis=0, concat_axis=0, tiled=True)


def dot(a, b, dims=((1,), (0,))):
    return lax.dot_general(a, b, (dims, ((), ())), precision=HIGHEST, preferred_element_type=F32)


def dot_nt(a, b):
    return dot(a, b, ((1,), (1,)))


def in_three(x):
    first = x.astype(BF16)
    rest = x - first.astype(F32)
    second = rest.astype(BF16)
    third = (rest - second.astype(F32)).astype(BF16)
    return first, second, third


def place_of(block_ref, groups):
    owner = block_ref[0] // groups
    return owner, block_ref[0] - owner * groups


def first_kernel(
    block_ref, h_ref, calib_ref, w_ref, sent_ref, keep_ref, give_ref, rows_ref, cols_ref, sems
):
    n = sent_ref.shape[0]
    half = keep_ref.shape[0]
    tile = h_ref.shape[1]
    groups, wide, thin = tile // B, tile // L, B // n
    _, sub = place_of(block_ref, groups)
    row = lax.axis_index("x") * lax.axis_size("y") + lax.axis_index("y")
    core = lax.axis_index("core")
    col = lax.axis_index("z") * lax.axis_size("core") + core
    offset = pl.multiple_of(sub * B, B)

    def window_of(which):
        return w_ref.at[pl.ds(which * half, half), :, pl.ds(offset, B)]

    copies = [
        pltpu.make_async_copy(
            calib_ref.at[:, pl.ds(pl.multiple_of(row * tile, L), tile)], rows_ref, sems.at[0]
        ),
        pltpu.make_async_copy(
            calib_ref.at[:, pl.ds(pl.multiple_of(col * tile, L), tile)], cols_ref, sems.at[1]
        ),
        pltpu.make_async_copy(window_of(core), keep_ref, sems.at[2]),
        pltpu.make_async_copy(window_of(1 - core), give_ref, sems.at[3]),
    ]
    for copy in copies:
        copy.start()
    copies[0].wait()
    copies[1].wait()
    first, second, third = in_three(h_ref[...])
    rows = rows_ref[...]
    left = jnp.dot(rows, first, preferred_element_type=F32)
    left += jnp.dot(rows, second, preferred_element_type=F32)
    left += jnp.dot(rows, third, preferred_element_type=F32)
    right = left.T
    cols = cols_ref[...]
    dims = (((1,), (1,)), ((), ()))
    first, second, third = in_three(left)
    inner = lax.dot_general(first, cols, dims, preferred_element_type=F32)
    inner += lax.dot_general(second, cols, dims, preferred_element_type=F32)
    inner += lax.dot_general(third, cols, dims, preferred_element_type=F32)
    cut = L // n
    for p in range(n):
        for s in range(groups):
            at = s * B + p * thin
            sent_ref[p, s * thin : (s + 1) * thin, :] = right[at : at + thin]
        at = groups * thin
        sent_ref[p, at : at + cut, :] = inner[p * cut : (p + 1) * cut]
        at += cut
        for w in range(wide):
            sent_ref[p, at + w * thin : at + (w + 1) * thin, :] = h_ref[
                pl.ds(pl.multiple_of(offset + p * thin, thin), thin), w * L : (w + 1) * L
            ]
    copies[2].wait()
    copies[3].wait()


def choose_kernel(block_ref, keep_ref, got_ref, *turned_refs, groups):
    count = len(turned_refs)
    owner, _ = place_of(block_ref, groups)
    z = lax.axis_index("z")
    own = owner % 2 == lax.axis_index("core")
    for k in range(count):
        at = (z + k) % count
        turned_refs[k][...] = jnp.where(own, keep_ref[at], got_ref[at])


def second_kernel(block_ref, arrived_ref, *refs):
    *shifted, small_ref, piece_ref, sent_ref, window_ref = refs
    n = arrived_ref.shape[0]
    rows = piece_ref.shape[0]
    thin, cut = B // n, L // n
    owner, sub = place_of(block_ref, rows // thin)
    z = lax.axis_index("z")
    for k, ref in enumerate(shifted):

        @pl.when((z + len(shifted) - owner // 2) % len(shifted) == k)
        def _(ref=ref):
            window_ref[...] = ref[...]

    total = arrived_ref[0, 0 : rows + cut, :]
    for p in range(1, n):
        total = total + arrived_ref[p, 0 : rows + cut, :]
    piece = total[:rows]
    strip = arrived_ref[owner, rows + cut :, :]
    piece_ref[...] = piece
    for p in range(n):
        sent_ref[p, 0:rows, :] = piece
        sent_ref[p, rows:, :] = strip
    small_ref[0:cut] = total[rows:]
    small_ref[cut : cut + thin] = piece_ref[pl.ds(pl.multiple_of(sub * thin, thin), thin), :]
    small_ref[cut + thin :] = arrived_ref[
        owner,
        pl.ds(pl.multiple_of(rows + cut + 2 * sub * thin, 8), 2 * thin),
        :,
    ]


def third_kernel(block_ref, gathered_ref, sent_ref, *, groups):
    n, small, _ = gathered_ref.shape
    cut = L // n
    owner, _ = place_of(block_ref, groups)
    total = gathered_ref[0, 0:cut, :]
    for p in range(1, n):
        total = total + gathered_ref[p, 0:cut, :]
    sent_ref[0:cut] = total
    sent_ref[cut:] = gathered_ref[owner, cut:small, :]


def pack_kernel(window_ref, turned_ref, sent_ref):
    lines = window_ref.shape[0]
    window = window_ref[...]
    turned = turned_ref[...]
    first = turned.astype(BF16)
    second = (turned - first.astype(F32)).astype(BF16)
    for p in range(sent_ref.shape[0]):
        sent_ref[p, 0:lines, :] = window
        sent_ref[p, lines:, 0:L] = first
        sent_ref[p, lines:, L:] = second


def last_kernel(
    h_ref, w_ref, own_ref, other_ref, twice_ref, low_ref, comp_ref, updated_ref, pruned_ref,
    right_ref, window_ref,
):
    count, lines, _ = own_ref.shape
    step = pl.program_id(0)
    tile = right_ref.shape[0]
    thin = B // (2 * count)
    groups = tile // B
    lines -= groups * thin

    @pl.when(step == 0)
    def _():
        core = lax.axis_index("core")
        for ref, c in ((own_ref, core), (other_ref, 1 - core)):
            for z in range(count):
                window_ref[c * count + z] = ref[z, 0:lines, :]
                for s in range(groups):
                    at = s * B + (2 * z + c) * thin
                    right_ref[pl.ds(pl.multiple_of(at, thin), thin), :] = ref[
                        z, lines + s * thin : lines + (s + 1) * thin, :
                    ]

    part = h_ref.shape[0]
    right = right_ref[pl.ds(pl.multiple_of(step * part, 16), part), :]
    dims = (((1,), (1,)), ((), ()))
    change = lax.dot_general(right, twice_ref[...], dims, preferred_element_type=F32)
    change += lax.dot_general(right[:, :L], low_ref[...], dims, preferred_element_type=F32)
    updated_ref[...] = h_ref[...] - change
    some = w_ref.shape[0] // lines
    comp = comp_ref[...]
    for q in range(some):
        window = window_ref[step * some + q]
        product = jnp.dot(window, comp, preferred_element_type=F32)
        pruned_ref[q * lines : (q + 1) * lines, :] = (
            w_ref[q * lines : (q + 1) * lines, :].astype(F32) - product
        ).astype(BF16)


def invert(a_ref):
    lane = lax.broadcasted_iota(jnp.int32, (8, L), 1)
    sub = lax.broadcasted_iota(jnp.int32, (8, L), 0)
    wide_lane = lax.broadcasted_iota(jnp.int32, (L, L), 1)

    def step(k, carry):
        base = pl.multiple_of(8 * k, 8)
        panel = a_ref[pl.ds(base, 8), :]
        columns = [
            jnp.broadcast_to(
                jnp.sum(jnp.where(lane == base + j, panel, 0.0), axis=1, keepdims=True), (8, L)
            )
            for j in range(8)
        ]
        whole = a_ref[...]
        factors = [
            jnp.sum(jnp.where(wide_lane == base + j, whole, 0.0), axis=1, keepdims=True)
            for j in range(8)
        ]
        for j in range(8):
            own = columns[j]
            inverse = 1.0 / own[j : j + 1, :]
            here = sub == j
            panel = jnp.where(lane == base + j, jnp.where(here, 1.0, 0.0), panel)
            scaled = panel[j : j + 1, :] * inverse
            panel = jnp.where(here, scaled, panel - own * scaled)
            for m in range(j + 1, 8):
                scaled = columns[m][j : j + 1, :] * inverse
                columns[m] = jnp.where(here, scaled, columns[m] - own * scaled)
        inside = (wide_lane >= base) & (wide_lane < base + 8)
        rest = jnp.where(inside, 0.0, whole)
        for j in range(8):
            rest = rest - factors[j] * panel[j : j + 1, :]
        a_ref[...] = rest
        a_ref[pl.ds(base, 8), :] = panel
        return carry

    lax.fori_loop(0, L // 8, step, 0)


def fourth_kernel(
    c_ref, large_ref, twice_ref, low_ref, comp_ref, a_ref, gm_ref, gc_ref, q_ref, st_ref
):
    n = c_ref.shape[0]
    tile = gc_ref.shape[0]
    thin, cut, groups, wide = B // n, L // n, tile // B, tile // L
    for p in range(n):
        a_ref[p * cut : (p + 1) * cut, :] = c_ref[p, 0:cut, :]
        at = cut
        gm_ref[p * thin : (p + 1) * thin, :] = c_ref[p, at : at + thin, :]
        at += thin
        for w in range(2):
            q_ref[p * thin : (p + 1) * thin, w * L : (w + 1) * L] = c_ref[p, at : at + thin, :]
            at += thin
        at = 0
        for s in range(groups):
            gc_ref[s * B + p * thin : s * B + (p + 1) * thin, :] = large_ref[p, at : at + thin, :]
            at += thin
        for w in range(wide):
            st_ref[p * thin : (p + 1) * thin, w * L : (w + 1) * L] = large_ref[
                p, at : at + thin, :
            ]
            at += thin
    inner = a_ref[...]
    same = lax.broadcasted_iota(jnp.int32, (L, L), 0) == lax.broadcasted_iota(
        jnp.int32, (L, L), 1
    )
    a_ref[...] = jnp.where(same, 1.0, 0.0) + 0.5 * (inner + inner.T)
    invert(a_ref)
    x = a_ref[...]
    block_right = gm_ref[...]
    right = gc_ref[...]
    half = dot(block_right, x)
    solved = dot(right, x)
    high = solved.astype(BF16)
    twice_ref[:, 0:L] = high
    twice_ref[:, L:] = high
    low_ref[...] = (solved - high.astype(F32)).astype(BF16)
    square = q_ref[...] - dot_nt(half, block_right)
    square = 0.5 * (square + square.T)
    a_ref[...] = square[:L, :L]
    st_ref[...] = st_ref[...] - dot_nt(half, right)
    invert(a_ref)
    u = a_ref[...]
    v = dot(square[L:, :L], u)
    a_ref[...] = square[L:, L:] - dot(v, square[:L, L:])
    top = st_ref[0:L, :]
    first = dot(u, top)
    second = st_ref[L:, :] - dot(v, top)
    invert(a_ref)
    second = dot(a_ref[...], second)
    comp_ref[0:L, :] = (first - dot(v.T, second)).astype(BF16)
    comp_ref[L:, :] = second.astype(BF16)


VMEM = pl.BlockSpec(memory_space=pltpu.VMEM)
PARAMS = pltpu.CompilerParams(vmem_limit_bytes=10 * 2**20)
FIRST_PARAMS = pltpu.CompilerParams(vmem_limit_bytes=58 * 2**20)
SMEM = pl.BlockSpec(memory_space=pltpu.SMEM)
HBM = pl.BlockSpec(memory_space=pltpu.HBM)


def of(shape, dtype=F32):
    return jax.ShapeDtypeStruct(shape, dtype)


def all_steps(inv_hessian, weights, calib, block):
    tile = inv_hessian.shape[0]
    n = lax.axis_size(ROW)
    count = lax.axis_size("z")
    lines = weights.shape[0] // n
    thin, cut, groups, wide = B // n, L // n, tile // B, tile // L
    rows = groups * thin
    strip_rows = wide * thin
    small_rows = cut + 3 * thin
    sent, keep, give = pl.pallas_call(
        first_kernel,
        out_shape=(
            of((n, rows + cut + strip_rows, L)),
            of((count, lines, B), BF16),
            of((count, lines, B), BF16),
        ),
        in_specs=[SMEM, VMEM, HBM, HBM],
        out_specs=(VMEM, VMEM, VMEM),
        scratch_shapes=[
            pltpu.VMEM((L, tile), BF16),
            pltpu.VMEM((L, tile), BF16),
            pltpu.SemaphoreType.DMA((4,)),
        ],
        compiler_params=FIRST_PARAMS,
        name="first",
    )(block, inv_hessian, calib, weights.reshape(n, lines, tile))
    arrived = exchanged(sent, ROW)
    got = lax.ppermute(give, "core", [(0, 1), (1, 0)])
    turned = pl.pallas_call(
        partial(choose_kernel, groups=groups),
        out_shape=(of((lines, B), BF16),) * count,
        in_specs=[SMEM, VMEM, VMEM],
        out_specs=(VMEM,) * count,
        compiler_params=PARAMS,
        name="choose",
    )(block, keep, got)
    shifted = [turned[0]]
    for k in range(1, count):
        perm = [(i, (i + k) % count) for i in range(count)]
        shifted.append(lax.ppermute(turned[k], "z", perm))
    small, piece, large, window = pl.pallas_call(
        second_kernel,
        out_shape=(
            of((small_rows, L)),
            of((rows, L)),
            of((n, rows + strip_rows, L)),
            of((lines, B), BF16),
        ),
        in_specs=[SMEM] + [VMEM] * (1 + count),
        out_specs=(VMEM, VMEM, VMEM, VMEM),
        compiler_params=PARAMS,
        name="second",
    )(block, arrived, *shifted)
    turn = [(i * n + j, j * n + i) for i in range(n) for j in range(n)]
    turned = lax.ppermute(piece, (*ROW, *COL), turn)
    large = exchanged(large, ROW)
    gathered = lax.all_gather(small, "core")
    gathered = lax.all_gather(gathered, "z").reshape(n, small_rows, L)
    sent = pl.pallas_call(
        partial(third_kernel, groups=groups),
        out_shape=of((small_rows, L)),
        in_specs=[SMEM, VMEM],
        out_specs=VMEM,
        compiler_params=PARAMS,
        name="third",
    )(block, gathered)
    arrived = lax.all_gather(sent, "y")
    arrived = lax.all_gather(arrived, "x").reshape(n, small_rows, L)
    packed = pl.pallas_call(
        pack_kernel,
        out_shape=of((count, lines + rows, B), BF16),
        in_specs=[VMEM, VMEM],
        out_specs=VMEM,
        compiler_params=PARAMS,
        name="pack",
    )(window, turned)
    packed = exchanged(packed, "z")
    other = lax.ppermute(packed, "core", [(0, 1), (1, 0)])
    twice, low, comp = pl.pallas_call(
        fourth_kernel,
        out_shape=(of((tile, 2 * L), BF16), of((tile, L), BF16), of((B, tile), BF16)),
        in_specs=[VMEM, VMEM],
        out_specs=(VMEM, VMEM, VMEM),
        scratch_shapes=[
            pltpu.VMEM((L, L), F32),
            pltpu.VMEM((B, L), F32),
            pltpu.VMEM((tile, L), F32),
            pltpu.VMEM((B, B), F32),
            pltpu.VMEM((B, tile), F32),
        ],
        cost_estimate=pl.CostEstimate(
            flops=20_000_000_000, bytes_accessed=4_000_000, transcendentals=0
        ),
        compiler_params=PARAMS,
        name="fourth",
    )(arrived, large)
    steps = 4
    return pl.pallas_call(
        last_kernel,
        grid=(steps,),
        out_shape=(of((tile, tile)), of((n * lines, tile), BF16)),
        in_specs=[
            pl.BlockSpec((tile // steps, tile), lambda i: (i, 0)),
            pl.BlockSpec((n * lines // steps, tile), lambda i: (i, 0)),
            VMEM,
            VMEM,
            VMEM,
            VMEM,
            VMEM,
        ],
        out_specs=(
            pl.BlockSpec((tile // steps, tile), lambda i: (i, 0)),
            pl.BlockSpec((n * lines // steps, tile), lambda i: (i, 0)),
        ),
        scratch_shapes=[pltpu.VMEM((tile, 2 * L), BF16), pltpu.VMEM((n, lines, B), BF16)],
        compiler_params=PARAMS,
        name="last",
    )(inv_hessian, weights, packed, other, twice, low, comp)


def solution(mesh):
    finer = Mesh(mesh.devices.reshape(4, 4, 8, 2), (*ROW, *COL))
    specs = (P(ROW, COL), P(ROW, COL), P(), P())
    return jax.shard_map(
        all_steps, mesh=finer, in_specs=specs, out_specs=specs[:2], check_vma=False
    )
```

time: 150 us -> 156 us (1.040)
  waiting for transfers between devices: 32 us -> 7.97 us
  starting transfers between devices: 25.1 us -> 46 us
  blocking collectives: 60.5 us -> 73.4 us
  Pallas kernels: 17.3 us -> 26.2 us
  matrix products: 6.76 us -> 0 us
  local copies, waits for them, and re-layouts: 6.19 us -> 1.04 us
    ppermute x1 -> x10, starting transfers between devices: 2.09 us -> 32.5 us  [the longest x7 16.5 us: all_steps(): shifted.append(lax.ppermute(turned[k], 'z', perm))]
    all_to_all x3 -> x2, waiting for transfers between devices: 29 us -> 0.01 us  [exchanged(): return lax.all_to_all(parts, axis, split_axis=0, concat_axis=0, tiled=True)]
    all_gather x1 -> x4, blocking collectives: 35.2 us -> 46 us  [the longest x1 20.5 us: all_steps(): gathered = lax.all_gather(gathered, 'z').reshape(n, small_rows, L)]
    all_to_all x3 -> x2, starting transfers between devices: 23 us -> 13.5 us  [exchanged(): return lax.all_to_all(parts, axis, split_axis=0, concat_axis=0, tiled=True)]
    pallas_call x4 -> x7, Pallas kernels: 17.3 us -> 26.2 us  [the longest x1 16 us: all_steps(): pl.pallas_call(fourth_kernel, out_shape=(of((tile, 2 * L), BF16), of((til...]
    dot_general x2 -> x0, matrix products: 6.76 us -> none  [the longest x1 3.44 us: dot(): lax.dot_general(a, b, (dims, ((), ())), precision=HIGHEST, preferred_elem...]
    ppermute x1 -> x10, waiting for transfers between devices: 3.05 us -> 7.96 us  [the longest x7 5.11 us: all_steps(): shifted.append(lax.ppermute(turned[k], 'z', perm))]
    unnamed x10, local copies, waits for them, and re-layouts: 5.22 us -> 1.04 us
  transfers between devices with their start and end apart: 4 -> 12, of which waited for: 3 -> 4; matrix products, arithmetic and copies ran while one was open for 2% -> 0% of each run, Pallas kernels for 11% -> 10%
where the time goes in v3:
time: 156 us
  blocking collectives  73.4 us (47%)
  starting transfers between devices  46 us (29%)
  Pallas kernels  26.2 us (17%)
  waiting for transfers between devices  7.97 us (5%)
    all_to_all x1, blocking collectives, exchanged(): return lax.all_to_all(parts, axis, split_axis=0, concat_axis=0, tiled=True)  27.4 us
    all_gather x1, blocking collectives, all_steps(): gathered = lax.all_gather(gathered, 'z').reshape(n, small_rows, L)  20.5 us
    ppermute x7, starting transfers between devices, all_steps(): shifted.append(lax.ppermute(turned[k], 'z', perm))  16.5 us
    pallas_call x1, Pallas kernels, all_steps(): pl.pallas_call(fourth_kernel, out_shape=(of((tile, 2 * L), BF16), of((til...  16 us
    all_to_all x2, starting transfers between devices, exchanged(): return lax.all_to_all(parts, axis, split_axis=0, concat_axis=0, tiled=True)  13.5 us
    all_gather x1, blocking collectives, all_steps(): arrived = lax.all_gather(arrived, 'x').reshape(n, small_rows, L)  11.6 us
    ppermute x1, starting transfers between devices, all_steps(): other = lax.ppermute(packed, 'core', [(0, 1), (1, 0)])  10.3 us
    all_gather x1, blocking collectives, all_steps(): arrived = lax.all_gather(sent, 'y')  9.54 us
  transfers between devices with their start and end apart: 12, of which 4 were waited for; matrix products, arithmetic and copies ran while one was open for 0% of the time, Pallas kernels for 10%

profile of v3, /device:TPU:1, one launch (start us, length us, event | category | flops | bytes accessed | tf_op | source)
XLA Modules:
  0.0 155.9 jit_solution(8443492383242970748)
XLA Ops:
  1.3 5.3 %first.1 = (f32[16,152,128]{2,1,0:T(8,128)}, bf16[8,96,256]{2,1,0:T(8,128)(2,1)}, bf16[8,96,256]{2,1,0:T(8,128)(2,1)}) custom-call(s32[1]{0:T(128)S(6)} %copy.6.block_ref, f32[768,768]{1,0:T(8,128)} %h_ref.3, bf16[128,12288]{1,0:T(8,128)(2,1)} %calib_ref.1, bf16[16,96,768]{2,1,0:T(8,128)(2,1)} %bitcast.3), custom_call_target="tpu_custom_call" | custom-call | tf_op jit(solution)/shard_map/first/pallas_call | solution.py:321
  6.6 0.0 copy-start.3
  6.6 7.7 %all-to-all-start = ((f32[16,152,128]{2,1,0:T(8,128)}), f32[16,152,128]{2,1,0:T(8,128)S(1)}, u32[]{:S(2)}, u32[]{:S(2)}) async-start(f32[16,152,128]{2,1,0:T(8,128)} %get-tuple-element.20), calls=%async_computation | async-start | bytes 2490368 | tf_op jit(solution)/shard_map/all_to_all | solution.py:21
  14.4 1.0 collective-permute-start
  15.4 1.3 collective-permute-done.got_ref
  16.8 1.7 %collective-permute-start.1 = (bf16[96,256]{1,0:T(8,128)(2,1)S(1)}, bf16[96,256]{1,0:T(8,128)(2,1)S(1)}, u32[]{:S(2)}, u32[]{:S(2)}) collective-permute-start(bf16[96,256]{1,0:T(8,128)(2,1)S(1)} %get-tuple-element.24), channel_id=1, source_target_pairs={{0,2},{2,4},{4,6},{6,8},{8,10},{10,12},{12,14},{14,0},{1,3},{3,5},... | collective-permute-start | bytes 147464 | tf_op jit(solution)/shard_map/ppermute | solution.py:351
  18.5 3.0 %collective-permute-start.2 = (bf16[96,256]{1,0:T(8,128)(2,1)S(1)}, bf16[96,256]{1,0:T(8,128)(2,1)S(1)}, u32[]{:S(2)}, u32[]{:S(2)}) collective-permute-start(bf16[96,256]{1,0:T(8,128)(2,1)S(1)} %get-tuple-element.25), channel_id=1, source_target_pairs={{0,4},{2,6},{4,8},{6,10},{8,12},{10,14},{12,0},{14,2},{1,5},{3,7},... | collective-permute-start | bytes 147464 | tf_op jit(solution)/shard_map/ppermute | solution.py:351
  21.5 3.8 %collective-permute-start.3 = (bf16[96,256]{1,0:T(8,128)(2,1)S(1)}, bf16[96,256]{1,0:T(8,128)(2,1)S(1)}, u32[]{:S(2)}, u32[]{:S(2)}) collective-permute-start(bf16[96,256]{1,0:T(8,128)(2,1)S(1)} %get-tuple-element.26), channel_id=1, source_target_pairs={{0,6},{2,8},{4,10},{6,12},{8,14},{10,0},{12,2},{14,4},{1,7},{3,9},... | collective-permute-start | bytes 147464 | tf_op jit(solution)/shard_map/ppermute | solution.py:351
  25.3 0.5 collective-permute-start.4
  25.7 4.5 %collective-permute-start.5 = (bf16[96,256]{1,0:T(8,128)(2,1)S(1)}, bf16[96,256]{1,0:T(8,128)(2,1)S(1)}, u32[]{:S(2)}, u32[]{:S(2)}) collective-permute-start(bf16[96,256]{1,0:T(8,128)(2,1)S(1)} %get-tuple-element.28), channel_id=1, source_target_pairs={{0,10},{2,12},{4,14},{6,0},{8,2},{10,4},{12,6},{14,8},{1,11},{3,13... | collective-permute-start | bytes 147464 | tf_op jit(solution)/shard_map/ppermute | solution.py:351
  30.2 2.4 %collective-permute-start.6 = (bf16[96,256]{1,0:T(8,128)(2,1)S(1)}, bf16[96,256]{1,0:T(8,128)(2,1)S(1)}, u32[]{:S(2)}, u32[]{:S(2)}) collective-permute-start(bf16[96,256]{1,0:T(8,128)(2,1)S(1)} %get-tuple-element.29), channel_id=1, source_target_pairs={{0,12},{2,14},{4,0},{6,2},{8,4},{10,6},{12,8},{14,10},{1,13},{3,15... | collective-permute-start | bytes 147464 | tf_op jit(solution)/shard_map/ppermute | solution.py:351
  32.6 0.0 collective-permute-done.2.refs_2_
  32.6 0.7 collective-permute-start.7
  33.3 0.0 collective-permute-done.3.refs_3_
  33.3 0.0 collective-permute-done.4.refs_4_
  33.3 4.7 %collective-permute-done.6.refs_6_ = bf16[96,256]{1,0:T(8,128)(2,1)S(1)} collective-permute-done((bf16[96,256]{1,0:T(8,128)(2,1)S(1)}, bf16[96,256]{1,0:T(8,128)(2,1)S(1)}, u32[]{:S(2)}, u32[]{:S(2)}) %collective-permute-start.6) | collective-permute-done | bytes 49184 | tf_op jit(solution)/shard_map/ppermute | solution.py:351
  38.0 0.4 collective-permute-done.7.refs_7_
  38.4 1.1 second.1
  39.6 4.7 %collective-permute-start.8 = (f32[48,128]{1,0:T(8,128)S(1)}, f32[48,128]{1,0:T(8,128)S(1)}, u32[]{:S(2)}, u32[]{:S(2)}) collective-permute-start(f32[48,128]{1,0:T(8,128)S(1)} %get-tuple-element.32), channel_id=1, source_target_pairs={{0,0},{1,16},{2,32},{3,48},{4,64},{5,80},{6,96},{7,112},{8,128},{9... | collective-permute-start | bytes 73736 | tf_op jit(solution)/shard_map/ppermute | solution.py:366
  44.2 1.5 collective-permute-done.8.turned_ref
  45.7 0.1 pack.1
  45.8 27.4 %all_to_all.15.own_ref = bf16[8,144,256]{2,1,0:T(8,128)(2,1)S(1)} all-to-all(bf16[8,144,256]{2,1,0:T(8,128)(2,1)S(1)} %pack.1), channel_id=1, replica_groups=mesh['x'=4,'y'=4,'z'=8,'core'=2] {'z'}, dimensions={0} | all-to-all | bytes 1179648 | tf_op jit(solution)/shard_map/all_to_all | solution.py:21
  73.2 5.7 %all-to-all-start.2 = ((f32[16,144,128]{2,1,0:T(8,128)}), f32[16,144,128]{2,1,0:T(8,128)}, u32[]{:S(2)}, u32[]{:S(2)}) async-start(f32[16,144,128]{2,1,0:T(8,128)} %get-tuple-element.34), calls=%async_computation.2 | async-start | bytes 2359296 | tf_op jit(solution)/shard_map/all_to_all | solution.py:21
  78.9 4.3 %all-gather = f32[112,128]{1,0:T(8,128)S(1)} all-gather(f32[56,128]{1,0:T(8,128)S(1)} %get-tuple-element.33), channel_id=2, replica_groups=mesh['x'=4,'y'=4,'z'=8,'core'=2] {'core'}, dimensions={0}, use_global_device_ids=true | all-gather | bytes 86016 | tf_op jit(solution)/shard_map/all_gather | solution.py:368
  83.3 20.5 %all-gather.1.gathered_ref = f32[16,56,128]{2,1,0:T(8,128)S(1)} all-gather(f32[2,56,128]{2,1,0:T(8,128)S(1)} %bitcast.5), channel_id=3, replica_groups=mesh['x'=4,'y'=4,'z'=8,'core'=2] {'z'}, dimensions={0}, use_global_device_ids=true | all-gather | bytes 516096 | tf_op jit(solution)/shard_map/all_gather | solution.py:369
  103.8 9.5 %all-gather.2 = f32[224,128]{1,0:T(8,128)S(1)} all-gather(f32[56,128]{1,0:T(8,128)S(1)} %third.1), channel_id=4, replica_groups=mesh['x'=4,'y'=4,'z'=8,'core'=2] {'y'}, dimensions={0}, use_global_device_ids=true | all-gather | bytes 143360 | tf_op jit(solution)/shard_map/all_gather | solution.py:378
  113.3 11.6 %all-gather.3.c_ref = f32[16,56,128]{2,1,0:T(8,128)} all-gather(f32[4,56,128]{2,1,0:T(8,128)S(1)} %bitcast.4), channel_id=5, replica_groups=mesh['x'=4,'y'=4,'z'=8,'core'=2] {'x'}, dimensions={0}, use_global_device_ids=true | all-gather | bytes 573440 | tf_op jit(solution)/shard_map/all_gather | solution.py:379
  124.9 10.3 %collective-permute-start.9 = (bf16[8,144,256]{2,1,0:T(8,128)(2,1)S(1)}, bf16[8,144,256]{2,1,0:T(8,128)(2,1)S(1)}, u32[]{:S(2)}, u32[]{:S(2)}) collective-permute-start(bf16[8,144,256]{2,1,0:T(8,128)(2,1)S(1)} %all_to_all.15.own_ref), channel_id=1, source_target_pairs={{0,1},{1,0},{2,3},{3,2},{4,5},{5,4},{6,7},{7,6},{8,9},{9,8},{10,11... | collective-permute-start | bytes 1769480 | tf_op jit(solution)/shard_map/ppermute | solution.py:389
  135.2 0.0 all-to-all-done.2.large_ref
  135.2 1.0 copy-done.2
  136.2 16.0 %fourth.1 = (bf16[768,256]{1,0:T(8,128)(2,1)S(1)}, bf16[768,128]{1,0:T(8,128)(2,1)S(1)}, bf16[256,768]{1,0:T(8,128)(2,1)S(1)}) custom-call(f32[16,56,128]{2,1,0:T(8,128)S(1)} %copy-done.2, f32[16,144,128]{2,1,0:T(8,128)} %all-to-all-done.2.large_ref), custom_call_target="tpu_custom_call" | custom-call | flops 20000000000 | bytes 4000000 | tf_op jit(solution)/shard_map/fourth/pallas_call | solution.py:390
  152.3 3.6 %last.1 = (f32[768,768]{1,0:T(8,128)}, bf16[1536,768]{1,0:T(8,128)(2,1)}) custom-call(f32[768,768]{1,0:T(8,128)S(1)} %copy-done, bf16[1536,768]{1,0:T(8,128)(2,1)S(1)} %copy-done.1, bf16[8,144,256]{2,1,0:T(8,128)(2,1)S(1)} %all_to_all.15.own_ref, bf16[8,144,256]{2,1,0:T(8,128)(2,1)S(1)} %collective-permute-done.9.other_ref, ...), custom_call_target="tpu_custom_call" | custom-call | tf_op jit(solution)/shard_map/last/pallas_call | solution.py:409
  (14 shorter events, 0.1 us)
Async XLA Ops:
  6.6 7.7 %copy-start.4 = (bf16[8,96,256]{2,1,0:T(8,128)(2,1)S(1)}, bf16[8,96,256]{2,1,0:T(8,128)(2,1)}, u32[]{:S(2)}) copy-start(bf16[8,96,256]{2,1,0:T(8,128)(2,1)} %get-tuple-element.22) | copy-start | bytes 1179652
  6.6 10.1 %copy-start.3 = (bf16[8,96,256]{2,1,0:T(8,128)(2,1)S(1)}, bf16[8,96,256]{2,1,0:T(8,128)(2,1)}, u32[]{:S(2)}) copy-start(bf16[8,96,256]{2,1,0:T(8,128)(2,1)} %get-tuple-element.21.keep_ref) | copy-start | bytes 1179652
  6.6 31.8 %all-to-all-start = ((f32[16,152,128]{2,1,0:T(8,128)}), f32[16,152,128]{2,1,0:T(8,128)S(1)}, u32[]{:S(2)}, u32[]{:S(2)}) async-start(f32[16,152,128]{2,1,0:T(8,128)} %get-tuple-element.20), calls=%async_computation | async-start | bytes 2490368 | tf_op jit(solution)/shard_map/all_to_all | solution.py:21
  14.4 2.4 %collective-permute-start = (bf16[8,96,256]{2,1,0:T(8,128)(2,1)S(1)}, bf16[8,96,256]{2,1,0:T(8,128)(2,1)S(1)}, u32[]{:S(2)}, u32[]{:S(2)}) collective-permute-start(bf16[8,96,256]{2,1,0:T(8,128)(2,1)S(1)} %copy-done.4), channel_id=1, source_target_pairs={{0,1},{1,0},{2,3},{3,2},{4,5},{5,4},{6,7},{7,6},{8,9},{9,8},{10,11... | collective-permute-start | bytes 1179656 | tf_op jit(solution)/shard_map/ppermute | solution.py:339
  16.8 13.4 %collective-permute-start.1 = (bf16[96,256]{1,0:T(8,128)(2,1)S(1)}, bf16[96,256]{1,0:T(8,128)(2,1)S(1)}, u32[]{:S(2)}, u32[]{:S(2)}) collective-permute-start(bf16[96,256]{1,0:T(8,128)(2,1)S(1)} %get-tuple-element.24), channel_id=1, source_target_pairs={{0,2},{2,4},{4,6},{6,8},{8,10},{10,12},{12,14},{14,0},{1,3},{3,5},... | collective-permute-start | bytes 147464 | tf_op jit(solution)/shard_map/ppermute | solution.py:351
  18.5 14.1 %collective-permute-start.2 = (bf16[96,256]{1,0:T(8,128)(2,1)S(1)}, bf16[96,256]{1,0:T(8,128)(2,1)S(1)}, u32[]{:S(2)}, u32[]{:S(2)}) collective-permute-start(bf16[96,256]{1,0:T(8,128)(2,1)S(1)} %get-tuple-element.25), channel_id=1, source_target_pairs={{0,4},{2,6},{4,8},{6,10},{8,12},{10,14},{12,0},{14,2},{1,5},{3,7},... | collective-permute-start | bytes 147464 | tf_op jit(solution)/shard_map/ppermute | solution.py:351
  21.5 11.8 %collective-permute-start.3 = (bf16[96,256]{1,0:T(8,128)(2,1)S(1)}, bf16[96,256]{1,0:T(8,128)(2,1)S(1)}, u32[]{:S(2)}, u32[]{:S(2)}) collective-permute-start(bf16[96,256]{1,0:T(8,128)(2,1)S(1)} %get-tuple-element.26), channel_id=1, source_target_pairs={{0,6},{2,8},{4,10},{6,12},{8,14},{10,0},{12,2},{14,4},{1,7},{3,9},... | collective-permute-start | bytes 147464 | tf_op jit(solution)/shard_map/ppermute | solution.py:351
  25.3 8.1 %collective-permute-start.4 = (bf16[96,256]{1,0:T(8,128)(2,1)S(1)}, bf16[96,256]{1,0:T(8,128)(2,1)S(1)}, u32[]{:S(2)}, u32[]{:S(2)}) collective-permute-start(bf16[96,256]{1,0:T(8,128)(2,1)S(1)} %get-tuple-element.27), channel_id=1, source_target_pairs={{0,8},{2,10},{4,12},{6,14},{8,0},{10,2},{12,4},{14,6},{1,9},{3,11}... | collective-permute-start | bytes 147464 | tf_op jit(solution)/shard_map/ppermute | solution.py:351
  25.7 7.6 %collective-permute-start.5 = (bf16[96,256]{1,0:T(8,128)(2,1)S(1)}, bf16[96,256]{1,0:T(8,128)(2,1)S(1)}, u32[]{:S(2)}, u32[]{:S(2)}) collective-permute-start(bf16[96,256]{1,0:T(8,128)(2,1)S(1)} %get-tuple-element.28), channel_id=1, source_target_pairs={{0,10},{2,12},{4,14},{6,0},{8,2},{10,4},{12,6},{14,8},{1,11},{3,13... | collective-permute-start | bytes 147464 | tf_op jit(solution)/shard_map/ppermute | solution.py:351
  30.2 7.8 %collective-permute-start.6 = (bf16[96,256]{1,0:T(8,128)(2,1)S(1)}, bf16[96,256]{1,0:T(8,128)(2,1)S(1)}, u32[]{:S(2)}, u32[]{:S(2)}) collective-permute-start(bf16[96,256]{1,0:T(8,128)(2,1)S(1)} %get-tuple-element.29), channel_id=1, source_target_pairs={{0,12},{2,14},{4,0},{6,2},{8,4},{10,6},{12,8},{14,10},{1,13},{3,15... | collective-permute-start | bytes 147464 | tf_op jit(solution)/shard_map/ppermute | solution.py:351
  32.6 5.8 %collective-permute-start.7 = (bf16[96,256]{1,0:T(8,128)(2,1)S(1)}, bf16[96,256]{1,0:T(8,128)(2,1)S(1)}, u32[]{:S(2)}, u32[]{:S(2)}) collective-permute-start(bf16[96,256]{1,0:T(8,128)(2,1)S(1)} %get-tuple-element.30), channel_id=1, source_target_pairs={{0,14},{2,0},{4,2},{6,4},{8,6},{10,8},{12,10},{14,12},{1,15},{3,1}... | collective-permute-start | bytes 147464 | tf_op jit(solution)/shard_map/ppermute | solution.py:351
  39.6 6.2 %collective-permute-start.8 = (f32[48,128]{1,0:T(8,128)S(1)}, f32[48,128]{1,0:T(8,128)S(1)}, u32[]{:S(2)}, u32[]{:S(2)}) collective-permute-start(f32[48,128]{1,0:T(8,128)S(1)} %get-tuple-element.32), channel_id=1, source_target_pairs={{0,0},{1,16},{2,32},{3,48},{4,64},{5,80},{6,96},{7,112},{8,128},{9... | collective-permute-start | bytes 73736 | tf_op jit(solution)/shard_map/ppermute | solution.py:366
  73.2 62.1 %all-to-all-start.2 = ((f32[16,144,128]{2,1,0:T(8,128)}), f32[16,144,128]{2,1,0:T(8,128)}, u32[]{:S(2)}, u32[]{:S(2)}) async-start(f32[16,144,128]{2,1,0:T(8,128)} %get-tuple-element.34), calls=%async_computation.2 | async-start | bytes 2359296 | tf_op jit(solution)/shard_map/all_to_all | solution.py:21
  124.9 27.4 %copy-start = (f32[768,768]{1,0:T(8,128)S(1)}, f32[768,768]{1,0:T(8,128)}, u32[]{:S(2)}) copy-start(f32[768,768]{1,0:T(8,128)} %h_ref.3) | copy-start | bytes 7077892
  124.9 27.3 %collective-permute-start.9 = (bf16[8,144,256]{2,1,0:T(8,128)(2,1)S(1)}, bf16[8,144,256]{2,1,0:T(8,128)(2,1)S(1)}, u32[]{:S(2)}, u32[]{:S(2)}) collective-permute-start(bf16[8,144,256]{2,1,0:T(8,128)(2,1)S(1)} %all_to_all.15.own_ref), channel_id=1, source_target_pairs={{0,1},{1,0},{2,3},{3,2},{4,5},{5,4},{6,7},{7,6},{8,9},{9,8},{10,11... | collective-permute-start | bytes 1769480 | tf_op jit(solution)/shard_map/ppermute | solution.py:389
  135.2 1.0 copy-start.2
  136.2 16.0 %copy-start.1 = (bf16[1536,768]{1,0:T(8,128)(2,1)S(1)}, bf16[1536,768]{1,0:T(8,128)(2,1)}, u32[]{:S(2)}) copy-start(bf16[1536,768]{1,0:T(8,128)(2,1)} %w_ref.1) | copy-start | bytes 7077892

commit v4 on v3

--- a/solution.py
+++ b/solution.py
@@ -110,55 +110,63 @@
         turned_refs[k][...] = jnp.where(own, keep_ref[at], got_ref[at])
 
 
-def second_kernel(block_ref, arrived_ref, *refs):
-    *shifted, small_ref, piece_ref, sent_ref, window_ref = refs
+def pick_shifted(block_ref, shifted, window_ref, groups, count, first=0):
+    owner, _ = place_of(block_ref, groups)
+    away = (lax.axis_index("z") + count - owner // 2) % count
+    for k, ref in enumerate(shifted):
+
+        @pl.when(away == first + k)
+        def _(ref=ref):
+            window_ref[...] = ref[...]
+
+
+def second_kernel(block_ref, arrived_ref, *refs, count):
+    *shifted, small_ref, piece_ref, strip_ref, window_ref = refs
     n = arrived_ref.shape[0]
     rows = piece_ref.shape[0]
     thin, cut = B // n, L // n
     owner, sub = place_of(block_ref, rows // thin)
-    z = lax.axis_index("z")
-    for k, ref in enumerate(shifted):
-
-        @pl.when((z + len(shifted) - owner // 2) % len(shifted) == k)
-        def _(ref=ref):
-            window_ref[...] = ref[...]
-
+    pick_shifted(block_ref, shifted, window_ref, rows // thin, count)
     total = arrived_ref[0, 0 : rows + cut, :]
     for p in range(1, n):
         total = total + arrived_ref[p, 0 : rows + cut, :]
-    piece = total[:rows]
-    strip = arrived_ref[owner, rows + cut :, :]
-    piece_ref[...] = piece
-    for p in range(n):
-        sent_ref[p, 0:rows, :] = piece
-        sent_ref[p, rows:, :] = strip
+    piece_ref[...] = total[:rows]
+    strip_ref[...] = arrived_ref[owner, rows + cut :, :]
     small_ref[0:cut] = total[rows:]
     small_ref[cut : cut + thin] = piece_ref[pl.ds(pl.multiple_of(sub * thin, thin), thin), :]
-    small_ref[cut + thin :] = arrived_ref[
-        owner,
-        pl.ds(pl.multiple_of(rows + cut + 2 * sub * thin, 8), 2 * thin),
-        :,
+    small_ref[cut + thin :] = strip_ref[
+        pl.ds(pl.multiple_of(2 * sub * thin, 2 * thin), 2 * thin), :
     ]
 
 
-def third_kernel(block_ref, gathered_ref, sent_ref, *, groups):
+def third_kernel(block_ref, gathered_ref, piece_ref, strip_ref, sent_ref):
     n, small, _ = gathered_ref.shape
+    rows = piece_ref.shape[0]
     cut = L // n
-    owner, _ = place_of(block_ref, groups)
+    owner, _ = place_of(block_ref, rows * n // B)
     total = gathered_ref[0, 0:cut, :]
     for p in range(1, n):
         total = total + gathered_ref[p, 0:cut, :]
-    sent_ref[0:cut] = total
-    sent_ref[cut:] = gathered_ref[owner, cut:small, :]
-
-
-def pack_kernel(window_ref, turned_ref, sent_ref):
+    chosen = gathered_ref[owner, cut:small, :]
+    piece, strip = piece_ref[...], strip_ref[...]
+    for p in range(n):
+        sent_ref[p, 0:cut, :] = total
+        sent_ref[p, cut:small, :] = chosen
+        sent_ref[p, small : small + rows, :] = piece
+        sent_ref[p, small + rows :, :] = strip
+
+
+def pack_kernel(block_ref, window_ref, turned_ref, *refs, groups):
+    *shifted, sent_ref, chosen_ref = refs
     lines = window_ref.shape[0]
-    window = window_ref[...]
+    count = sent_ref.shape[0]
+    chosen_ref[...] = window_ref[...]
+    pick_shifted(block_ref, shifted, chosen_ref, groups, count, count - len(shifted))
+    window = chosen_ref[...]
     turned = turned_ref[...]
     first = turned.astype(BF16)
     second = (turned - first.astype(F32)).astype(BF16)
-    for p in range(sent_ref.shape[0]):
+    for p in range(count):
         sent_ref[p, 0:lines, :] = window
         sent_ref[p, lines:, 0:L] = first
         sent_ref[p, lines:, L:] = second
@@ -244,7 +252,7 @@
 
 
 def fourth_kernel(
-    c_ref, large_ref, twice_ref, low_ref, comp_ref, a_ref, gm_ref, gc_ref, q_ref, st_ref
+    c_ref, twice_ref, low_ref, comp_ref, a_ref, gm_ref, gc_ref, q_ref, st_ref
 ):
     n = c_ref.shape[0]
     tile = gc_ref.shape[0]
@@ -257,14 +265,11 @@
         for w in range(2):
             q_ref[p * thin : (p + 1) * thin, w * L : (w + 1) * L] = c_ref[p, at : at + thin, :]
             at += thin
-        at = 0
         for s in range(groups):
-            gc_ref[s * B + p * thin : s * B + (p + 1) * thin, :] = large_ref[p, at : at + thin, :]
+            gc_ref[s * B + p * thin : s * B + (p + 1) * thin, :] = c_ref[p, at : at + thin, :]
             at += thin
         for w in range(wide):
-            st_ref[p * thin : (p + 1) * thin, w * L : (w + 1) * L] = large_ref[
-                p, at : at + thin, :
-            ]
+            st_ref[p * thin : (p + 1) * thin, w * L : (w + 1) * L] = c_ref[p, at : at + thin, :]
             at += thin
     inner = a_ref[...]
     same = lax.broadcasted_iota(jnp.int32, (L, L), 0) == lax.broadcasted_iota(
@@ -301,6 +306,7 @@
 VMEM = pl.BlockSpec(memory_space=pltpu.VMEM)
 PARAMS = pltpu.CompilerParams(vmem_limit_bytes=10 * 2**20)
 FIRST_PARAMS = pltpu.CompilerParams(vmem_limit_bytes=58 * 2**20)
+LAST_PARAMS = pltpu.CompilerParams(vmem_limit_bytes=51 * 2**20)
 SMEM = pl.BlockSpec(memory_space=pltpu.SMEM)
 HBM = pl.BlockSpec(memory_space=pltpu.HBM)
 
@@ -345,52 +351,52 @@
         compiler_params=PARAMS,
         name="choose",
     )(block, keep, got)
+    early = count // 2 + 1
     shifted = [turned[0]]
     for k in range(1, count):
         perm = [(i, (i + k) % count) for i in range(count)]
         shifted.append(lax.ppermute(turned[k], "z", perm))
-    small, piece, large, window = pl.pallas_call(
-        second_kernel,
+    small, piece, strip, window = pl.pallas_call(
+        partial(second_kernel, count=count),
         out_shape=(
             of((small_rows, L)),
             of((rows, L)),
-            of((n, rows + strip_rows, L)),
+            of((strip_rows, L)),
             of((lines, B), BF16),
         ),
-        in_specs=[SMEM] + [VMEM] * (1 + count),
+        in_specs=[SMEM] + [VMEM] * (1 + early),
         out_specs=(VMEM, VMEM, VMEM, VMEM),
         compiler_params=PARAMS,
         name="second",
-    )(block, arrived, *shifted)
+    )(block, arrived, *shifted[:early])
     turn = [(i * n + j, j * n + i) for i in range(n) for j in range(n)]
     turned = lax.ppermute(piece, (*ROW, *COL), turn)
-    large = exchanged(large, ROW)
     gathered = lax.all_gather(small, "core")
     gathered = lax.all_gather(gathered, "z").reshape(n, small_rows, L)
     sent = pl.pallas_call(
-        partial(third_kernel, groups=groups),
-        out_shape=of((small_rows, L)),
-        in_specs=[SMEM, VMEM],
+        third_kernel,
+        out_shape=of((n, small_rows + rows + strip_rows, L)),
+        in_specs=[SMEM, VMEM, VMEM, VMEM],
         out_specs=VMEM,
         compiler_params=PARAMS,
         name="third",
-    )(block, gathered)
-    arrived = lax.all_gather(sent, "y")
-    arrived = lax.all_gather(arrived, "x").reshape(n, small_rows, L)
+    )(block, gathered, piece, strip)
+    arrived = exchanged(sent, ROW)
     packed = pl.pallas_call(
-        pack_kernel,
+        partial(pack_kernel, groups=groups),
         out_shape=of((count, lines + rows, B), BF16),
-        in_specs=[VMEM, VMEM],
+        in_specs=[SMEM] + [VMEM] * (2 + count - early),
         out_specs=VMEM,
+        scratch_shapes=[pltpu.VMEM((lines, B), BF16)],
         compiler_params=PARAMS,
         name="pack",
-    )(window, turned)
+    )(block, window, turned, *shifted[early:])
     packed = exchanged(packed, "z")
     other = lax.ppermute(packed, "core", [(0, 1), (1, 0)])
     twice, low, comp = pl.pallas_call(
         fourth_kernel,
         out_shape=(of((tile, 2 * L), BF16), of((tile, L), BF16), of((B, tile), BF16)),
-        in_specs=[VMEM, VMEM],
+        in_specs=[VMEM],
         out_specs=(VMEM, VMEM, VMEM),
         scratch_shapes=[
             pltpu.VMEM((L, L), F32),
@@ -404,7 +410,7 @@
         ),
         compiler_params=PARAMS,
         name="fourth",
-    )(arrived, large)
+    )(arrived)
     steps = 4
     return pl.pallas_call(
         last_kernel,
@@ -424,7 +430,7 @@
             pl.BlockSpec((n * lines // steps, tile), lambda i: (i, 0)),
         ),
         scratch_shapes=[pltpu.VMEM((tile, 2 * L), BF16), pltpu.VMEM((n, lines, B), BF16)],
-        compiler_params=PARAMS,
+        compiler_params=LAST_PARAMS,
         name="last",
     )(inv_hessian, weights, packed, other, twice, low, comp)
 

time: 156 us -> 132 us (0.85)
  the two profiles are of different devices: /device:TPU:1 before, /device:TPU:2 now
where the time goes in v4:
time: 132 us
  starting transfers between devices  48.6 us (37%)
  blocking collectives  32 us (24%)
  Pallas kernels  28.1 us (21%)
  waiting for transfers between devices  21.5 us (16%)
  between operations  1.39 us (1%)
    all_gather x1, blocking collectives, all_steps(): gathered = lax.all_gather(gathered, 'z').reshape(n, small_rows, L)  30.2 us
    all_to_all x3, starting transfers between devices, exchanged(): return lax.all_to_all(parts, axis, split_axis=0, concat_axis=0, tiled=True)  25.7 us
    ppermute x7, starting transfers between devices, all_steps(): shifted.append(lax.ppermute(turned[k], 'z', perm))  18.5 us
    all_to_all x3, waiting for transfers between devices, exchanged(): return lax.all_to_all(parts, axis, split_axis=0, concat_axis=0, tiled=True)  16.6 us
    pallas_call x1, Pallas kernels, all_steps(): pl.pallas_call(fourth_kernel, out_shape=(of((tile, 2 * L), BF16), of((til...  14.6 us
    pallas_call x1, Pallas kernels, all_steps(): pl.pallas_call(last_kernel, grid=(steps,), out_shape=(of((tile, tile)), o...  5.89 us
    pallas_call x1, Pallas kernels, all_steps(): pl.pallas_call(first_kernel, out_shape=(of((n, rows + cut + strip_rows, L...  5.31 us
    ppermute x1, starting transfers between devices, all_steps(): turned = lax.ppermute(piece, (*ROW, *COL), turn)  4.35 us
  transfers between devices with their start and end apart: 13, of which 3 were waited for; matrix products, arithmetic and copies ran while one was open for 0% of the time, Pallas kernels for 12%

profile of v4, /device:TPU:2, one launch (start us, length us, event | category | flops | bytes accessed | tf_op | source)
XLA Modules:
  0.0 131.5 jit_solution(8731895990534829423)
XLA Ops:
  1.3 5.3 %first.1 = (f32[16,152,128]{2,1,0:T(8,128)}, bf16[8,96,256]{2,1,0:T(8,128)(2,1)}, bf16[8,96,256]{2,1,0:T(8,128)(2,1)}) custom-call(s32[1]{0:T(128)S(6)} %copy.6.block_ref, f32[768,768]{1,0:T(8,128)} %h_ref.3, bf16[128,12288]{1,0:T(8,128)(2,1)} %calib_ref.1, bf16[16,96,768]{2,1,0:T(8,128)(2,1)} %bitcast.2), custom_call_target="tpu_custom_call" | custom-call | tf_op jit(solution)/shard_map/first/pallas_call | solution.py:327
  6.6 0.0 copy-start
  6.6 7.6 %all-to-all-start = ((f32[16,152,128]{2,1,0:T(8,128)}), f32[16,152,128]{2,1,0:T(8,128)S(1)}, u32[]{:S(2)}, u32[]{:S(2)}) async-start(f32[16,152,128]{2,1,0:T(8,128)} %get-tuple-element.20), calls=%async_computation | async-start | bytes 2490368 | tf_op jit(solution)/shard_map/all_to_all | solution.py:21
  14.2 0.1 collective-permute-start
  14.3 1.7 %collective-permute-done.got_ref = bf16[8,96,256]{2,1,0:T(8,128)(2,1)S(1)} collective-permute-done((bf16[8,96,256]{2,1,0:T(8,128)(2,1)S(1)}, bf16[8,96,256]{2,1,0:T(8,128)(2,1)S(1)}, u32[]{:S(2)}, u32[]{:S(2)}) %collective-permute-start) | collective-permute-done | bytes 393248 | tf_op jit(solution)/shard_map/ppermute | solution.py:345
  16.1 2.0 %collective-permute-start.1 = (bf16[96,256]{1,0:T(8,128)(2,1)S(1)}, bf16[96,256]{1,0:T(8,128)(2,1)S(1)}, u32[]{:S(2)}, u32[]{:S(2)}) collective-permute-start(bf16[96,256]{1,0:T(8,128)(2,1)S(1)} %get-tuple-element.24), channel_id=1, source_target_pairs={{0,2},{2,4},{4,6},{6,8},{8,10},{10,12},{12,14},{14,0},{1,3},{3,5},... | collective-permute-start | bytes 147464 | tf_op jit(solution)/shard_map/ppermute | solution.py:358
  18.1 3.3 %collective-permute-start.2 = (bf16[96,256]{1,0:T(8,128)(2,1)S(1)}, bf16[96,256]{1,0:T(8,128)(2,1)S(1)}, u32[]{:S(2)}, u32[]{:S(2)}) collective-permute-start(bf16[96,256]{1,0:T(8,128)(2,1)S(1)} %get-tuple-element.25), channel_id=1, source_target_pairs={{0,4},{2,6},{4,8},{6,10},{8,12},{10,14},{12,0},{14,2},{1,5},{3,7},... | collective-permute-start | bytes 147464 | tf_op jit(solution)/shard_map/ppermute | solution.py:358
  21.4 4.0 %collective-permute-start.3 = (bf16[96,256]{1,0:T(8,128)(2,1)S(1)}, bf16[96,256]{1,0:T(8,128)(2,1)S(1)}, u32[]{:S(2)}, u32[]{:S(2)}) collective-permute-start(bf16[96,256]{1,0:T(8,128)(2,1)S(1)} %get-tuple-element.26), channel_id=1, source_target_pairs={{0,6},{2,8},{4,10},{6,12},{8,14},{10,0},{12,2},{14,4},{1,7},{3,9},... | collective-permute-start | bytes 147464 | tf_op jit(solution)/shard_map/ppermute | solution.py:358
  25.4 0.5 collective-permute-start.4
  26.0 4.9 %collective-permute-start.6 = (bf16[96,256]{1,0:T(8,128)(2,1)S(1)}, bf16[96,256]{1,0:T(8,128)(2,1)S(1)}, u32[]{:S(2)}, u32[]{:S(2)}) collective-permute-start(bf16[96,256]{1,0:T(8,128)(2,1)S(1)} %get-tuple-element.30), channel_id=1, source_target_pairs={{0,10},{2,12},{4,14},{6,0},{8,2},{10,4},{12,6},{14,8},{1,11},{3,13... | collective-permute-start | bytes 147464 | tf_op jit(solution)/shard_map/ppermute | solution.py:358
  30.9 0.0 collective-permute-done.1.refs_1_
  30.9 2.7 %collective-permute-start.7 = (bf16[96,256]{1,0:T(8,128)(2,1)S(1)}, bf16[96,256]{1,0:T(8,128)(2,1)S(1)}, u32[]{:S(2)}, u32[]{:S(2)}) collective-permute-start(bf16[96,256]{1,0:T(8,128)(2,1)S(1)} %get-tuple-element.31), channel_id=1, source_target_pairs={{0,12},{2,14},{4,0},{6,2},{8,4},{10,6},{12,8},{14,10},{1,13},{3,15... | collective-permute-start | bytes 147464 | tf_op jit(solution)/shard_map/ppermute | solution.py:358
  33.6 0.0 collective-permute-done.2.refs_2_
  33.6 1.0 collective-permute-start.8
  34.6 0.0 collective-permute-done.3.refs_3_
  34.6 0.0 collective-permute-done.4.refs_4_
  34.6 0.1 second.1
  34.7 4.3 %collective-permute-start.5 = (f32[48,128]{1,0:T(8,128)S(1)}, f32[48,128]{1,0:T(8,128)S(1)}, u32[]{:S(2)}, u32[]{:S(2)}) collective-permute-start(f32[48,128]{1,0:T(8,128)S(1)} %get-tuple-element.29.piece_ref), channel_id=1, source_target_pairs={{0,0},{1,16},{2,32},{3,48},{4,64},{5,80},{6,96},{7,112},{8,128},{9... | collective-permute-start | bytes 73736 | tf_op jit(solution)/shard_map/ppermute | solution.py:373
  39.0 0.0 collective-permute-done.6.refs_0_
  39.1 0.0 collective-permute-done.7.refs_1_
  39.1 3.1 %collective-permute-done.5.turned_ref = f32[48,128]{1,0:T(8,128)S(1)} collective-permute-done((f32[48,128]{1,0:T(8,128)S(1)}, f32[48,128]{1,0:T(8,128)S(1)}, u32[]{:S(2)}, u32[]{:S(2)}) %collective-permute-start.5) | collective-permute-done | bytes 24608 | tf_op jit(solution)/shard_map/ppermute | solution.py:373
  42.2 0.9 pack.1
  43.1 11.0 %all-to-all-start.1 = ((bf16[8,144,256]{2,1,0:T(8,128)(2,1)}), bf16[8,144,256]{2,1,0:T(8,128)(2,1)S(1)}, u32[]{:S(2)}, u32[]{:S(2)}) async-start(bf16[8,144,256]{2,1,0:T(8,128)(2,1)} %pack.1), calls=%async_computation.1 | async-start | bytes 1179648 | tf_op jit(solution)/shard_map/all_to_all | solution.py:21
  54.1 1.8 %all-gather = f32[112,128]{1,0:T(8,128)S(1)} all-gather(f32[56,128]{1,0:T(8,128)S(1)} %get-tuple-element.33), channel_id=2, replica_groups=mesh['x'=4,'y'=4,'z'=8,'core'=2] {'core'}, dimensions={0}, use_global_device_ids=true | all-gather | bytes 86016 | tf_op jit(solution)/shard_map/all_gather | solution.py:374
  56.0 30.2 %all-gather.1.gathered_ref = f32[16,56,128]{2,1,0:T(8,128)S(1)} all-gather(f32[2,56,128]{2,1,0:T(8,128)S(1)} %bitcast.3), channel_id=3, replica_groups=mesh['x'=4,'y'=4,'z'=8,'core'=2] {'z'}, dimensions={0}, use_global_device_ids=true | all-gather | bytes 516096 | tf_op jit(solution)/shard_map/all_gather | solution.py:375
  86.1 1.3 third.1
  87.4 0.0 all-to-all-done.1.own_ref
  87.4 7.0 %all-to-all-start.2 = ((f32[16,200,128]{2,1,0:T(8,128)}), f32[16,200,128]{2,1,0:T(8,128)S(1)}, u32[]{:S(2)}, u32[]{:S(2)}) async-start(f32[16,200,128]{2,1,0:T(8,128)} %third.1), calls=%async_computation.2 | async-start | bytes 3276800 | tf_op jit(solution)/shard_map/all_to_all | solution.py:21
  94.4 0.0 collective-permute-start.9
  94.4 16.6 %all-to-all-done.2.c_ref = f32[16,200,128]{2,1,0:T(8,128)S(1)} async-done(((f32[16,200,128]{2,1,0:T(8,128)}), f32[16,200,128]{2,1,0:T(8,128)S(1)}, u32[]{:S(2)}, u32[]{:S(2)}) %all-to-all-start.2) | async-done | bytes 1638432 | tf_op jit(solution)/shard_map/all_to_all | solution.py:21
  111.0 14.6 %fourth.1 = (bf16[768,256]{1,0:T(8,128)(2,1)S(1)}, bf16[768,128]{1,0:T(8,128)(2,1)S(1)}, bf16[256,768]{1,0:T(8,128)(2,1)S(1)}) custom-call(f32[16,200,128]{2,1,0:T(8,128)S(1)} %all-to-all-done.2.c_ref), custom_call_target="tpu_custom_call" | custom-call | flops 20000000000 | bytes 4000000 | tf_op jit(solution)/shard_map/fourth/pallas_call | solution.py:396
  125.7 5.9 %last.1 = (f32[768,768]{1,0:T(8,128)}, bf16[1536,768]{1,0:T(8,128)(2,1)}) custom-call(f32[768,768]{1,0:T(8,128)} %h_ref.3, bf16[1536,768]{1,0:T(8,128)(2,1)} %w_ref.1, bf16[8,144,256]{2,1,0:T(8,128)(2,1)S(1)} %all-to-all-done.1.own_ref, bf16[8,144,256]{2,1,0:T(8,128)(2,1)S(1)} %collective-permute-done.9.other_ref, ...), custom_call_target="tpu_custom_call" | custom-call | tf_op jit(solution)/shard_map/last/pallas_call | solution.py:415
  (7 shorter events, 0.1 us)
Async XLA Ops:
  6.6 7.6 %copy-start.1 = (bf16[8,96,256]{2,1,0:T(8,128)(2,1)S(1)}, bf16[8,96,256]{2,1,0:T(8,128)(2,1)}, u32[]{:S(2)}) copy-start(bf16[8,96,256]{2,1,0:T(8,128)(2,1)} %get-tuple-element.22) | copy-start | bytes 1179652
  6.6 9.5 %copy-start = (bf16[8,96,256]{2,1,0:T(8,128)(2,1)S(1)}, bf16[8,96,256]{2,1,0:T(8,128)(2,1)}, u32[]{:S(2)}) copy-start(bf16[8,96,256]{2,1,0:T(8,128)(2,1)} %get-tuple-element.21.keep_ref) | copy-start | bytes 1179652
  6.6 28.0 %all-to-all-start = ((f32[16,152,128]{2,1,0:T(8,128)}), f32[16,152,128]{2,1,0:T(8,128)S(1)}, u32[]{:S(2)}, u32[]{:S(2)}) async-start(f32[16,152,128]{2,1,0:T(8,128)} %get-tuple-element.20), calls=%async_computation | async-start | bytes 2490368 | tf_op jit(solution)/shard_map/all_to_all | solution.py:21
  14.2 1.8 %collective-permute-start = (bf16[8,96,256]{2,1,0:T(8,128)(2,1)S(1)}, bf16[8,96,256]{2,1,0:T(8,128)(2,1)S(1)}, u32[]{:S(2)}, u32[]{:S(2)}) collective-permute-start(bf16[8,96,256]{2,1,0:T(8,128)(2,1)S(1)} %copy-done.1), channel_id=1, source_target_pairs={{0,1},{1,0},{2,3},{3,2},{4,5},{5,4},{6,7},{7,6},{8,9},{9,8},{10,11... | collective-permute-start | bytes 1179656 | tf_op jit(solution)/shard_map/ppermute | solution.py:345
  16.1 14.8 %collective-permute-start.1 = (bf16[96,256]{1,0:T(8,128)(2,1)S(1)}, bf16[96,256]{1,0:T(8,128)(2,1)S(1)}, u32[]{:S(2)}, u32[]{:S(2)}) collective-permute-start(bf16[96,256]{1,0:T(8,128)(2,1)S(1)} %get-tuple-element.24), channel_id=1, source_target_pairs={{0,2},{2,4},{4,6},{6,8},{8,10},{10,12},{12,14},{14,0},{1,3},{3,5},... | collective-permute-start | bytes 147464 | tf_op jit(solution)/shard_map/ppermute | solution.py:358
  18.1 15.5 %collective-permute-start.2 = (bf16[96,256]{1,0:T(8,128)(2,1)S(1)}, bf16[96,256]{1,0:T(8,128)(2,1)S(1)}, u32[]{:S(2)}, u32[]{:S(2)}) collective-permute-start(bf16[96,256]{1,0:T(8,128)(2,1)S(1)} %get-tuple-element.25), channel_id=1, source_target_pairs={{0,4},{2,6},{4,8},{6,10},{8,12},{10,14},{12,0},{14,2},{1,5},{3,7},... | collective-permute-start | bytes 147464 | tf_op jit(solution)/shard_map/ppermute | solution.py:358
  21.4 13.2 %collective-permute-start.3 = (bf16[96,256]{1,0:T(8,128)(2,1)S(1)}, bf16[96,256]{1,0:T(8,128)(2,1)S(1)}, u32[]{:S(2)}, u32[]{:S(2)}) collective-permute-start(bf16[96,256]{1,0:T(8,128)(2,1)S(1)} %get-tuple-element.26), channel_id=1, source_target_pairs={{0,6},{2,8},{4,10},{6,12},{8,14},{10,0},{12,2},{14,4},{1,7},{3,9},... | collective-permute-start | bytes 147464 | tf_op jit(solution)/shard_map/ppermute | solution.py:358
  25.4 9.2 %collective-permute-start.4 = (bf16[96,256]{1,0:T(8,128)(2,1)S(1)}, bf16[96,256]{1,0:T(8,128)(2,1)S(1)}, u32[]{:S(2)}, u32[]{:S(2)}) collective-permute-start(bf16[96,256]{1,0:T(8,128)(2,1)S(1)} %get-tuple-element.27), channel_id=1, source_target_pairs={{0,8},{2,10},{4,12},{6,14},{8,0},{10,2},{12,4},{14,6},{1,9},{3,11}... | collective-permute-start | bytes 147464 | tf_op jit(solution)/shard_map/ppermute | solution.py:358
  26.0 13.1 %collective-permute-start.6 = (bf16[96,256]{1,0:T(8,128)(2,1)S(1)}, bf16[96,256]{1,0:T(8,128)(2,1)S(1)}, u32[]{:S(2)}, u32[]{:S(2)}) collective-permute-start(bf16[96,256]{1,0:T(8,128)(2,1)S(1)} %get-tuple-element.30), channel_id=1, source_target_pairs={{0,10},{2,12},{4,14},{6,0},{8,2},{10,4},{12,6},{14,8},{1,11},{3,13... | collective-permute-start | bytes 147464 | tf_op jit(solution)/shard_map/ppermute | solution.py:358
  30.9 8.1 %collective-permute-start.7 = (bf16[96,256]{1,0:T(8,128)(2,1)S(1)}, bf16[96,256]{1,0:T(8,128)(2,1)S(1)}, u32[]{:S(2)}, u32[]{:S(2)}) collective-permute-start(bf16[96,256]{1,0:T(8,128)(2,1)S(1)} %get-tuple-element.31), channel_id=1, source_target_pairs={{0,12},{2,14},{4,0},{6,2},{8,4},{10,6},{12,8},{14,10},{1,13},{3,15... | collective-permute-start | bytes 147464 | tf_op jit(solution)/shard_map/ppermute | solution.py:358
  33.6 5.5 %collective-permute-start.8 = (bf16[96,256]{1,0:T(8,128)(2,1)S(1)}, bf16[96,256]{1,0:T(8,128)(2,1)S(1)}, u32[]{:S(2)}, u32[]{:S(2)}) collective-permute-start(bf16[96,256]{1,0:T(8,128)(2,1)S(1)} %get-tuple-element.32), channel_id=1, source_target_pairs={{0,14},{2,0},{4,2},{6,4},{8,6},{10,8},{12,10},{14,12},{1,15},{3,1}... | collective-permute-start | bytes 147464 | tf_op jit(solution)/shard_map/ppermute | solution.py:358
  34.7 7.5 %collective-permute-start.5 = (f32[48,128]{1,0:T(8,128)S(1)}, f32[48,128]{1,0:T(8,128)S(1)}, u32[]{:S(2)}, u32[]{:S(2)}) collective-permute-start(f32[48,128]{1,0:T(8,128)S(1)} %get-tuple-element.29.piece_ref), channel_id=1, source_target_pairs={{0,0},{1,16},{2,32},{3,48},{4,64},{5,80},{6,96},{7,112},{8,128},{9... | collective-permute-start | bytes 73736 | tf_op jit(solution)/shard_map/ppermute | solution.py:373
  43.1 44.3 %all-to-all-start.1 = ((bf16[8,144,256]{2,1,0:T(8,128)(2,1)}), bf16[8,144,256]{2,1,0:T(8,128)(2,1)S(1)}, u32[]{:S(2)}, u32[]{:S(2)}) async-start(bf16[8,144,256]{2,1,0:T(8,128)(2,1)} %pack.1), calls=%async_computation.1 | async-start | bytes 1179648 | tf_op jit(solution)/shard_map/all_to_all | solution.py:21
  87.4 23.6 %all-to-all-start.2 = ((f32[16,200,128]{2,1,0:T(8,128)}), f32[16,200,128]{2,1,0:T(8,128)S(1)}, u32[]{:S(2)}, u32[]{:S(2)}) async-start(f32[16,200,128]{2,1,0:T(8,128)} %third.1), calls=%async_computation.2 | async-start | bytes 3276800 | tf_op jit(solution)/shard_map/all_to_all | solution.py:21
  94.4 31.2 %collective-permute-start.9 = (bf16[8,144,256]{2,1,0:T(8,128)(2,1)S(1)}, bf16[8,144,256]{2,1,0:T(8,128)(2,1)S(1)}, u32[]{:S(2)}, u32[]{:S(2)}) collective-permute-start(bf16[8,144,256]{2,1,0:T(8,128)(2,1)S(1)} %all-to-all-done.1.own_ref), channel_id=1, source_target_pairs={{0,1},{1,0},{2,3},{3,2},{4,5},{5,4},{6,7},{7,6},{8,9},{9,8},{10,11... | collective-permute-start | bytes 1769480 | tf_op jit(solution)/shard_map/ppermute | solution.py:395

commit v5 on v4

--- a/solution.py
+++ b/solution.py
@@ -43,7 +43,8 @@
 
 
 def first_kernel(
-    block_ref, h_ref, calib_ref, w_ref, sent_ref, keep_ref, give_ref, rows_ref, cols_ref, sems
+    block_ref, source_ref, calib_ref, w_ref, sent_ref, keep_ref, give_ref,
+    h_ref, rows_ref, cols_ref, sems,
 ):
     n = sent_ref.shape[0]
     half = keep_ref.shape[0]
@@ -68,15 +69,26 @@
         pltpu.make_async_copy(window_of(core), keep_ref, sems.at[2]),
         pltpu.make_async_copy(window_of(1 - core), give_ref, sems.at[3]),
     ]
-    for copy in copies:
+    blocks = [
+        pltpu.make_async_copy(
+            source_ref.at[g * B : (g + 1) * B, :], h_ref.at[g * B : (g + 1) * B, :], sems.at[4 + g]
+        )
+        for g in range(groups)
+    ]
+    copies[0].start()
+    blocks[0].start()
+    copies[1].start()
+    for copy in blocks[1:] + copies[2:]:
         copy.start()
     copies[0].wait()
+    left = None
+    for g in range(groups):
+        blocks[g].wait()
+        rows = rows_ref[:, g * B : (g + 1) * B]
+        for part in in_three(h_ref[g * B : (g + 1) * B, :]):
+            more = jnp.dot(rows, part, preferred_element_type=F32)
+            left = more if left is None else left + more
     copies[1].wait()
-    first, second, third = in_three(h_ref[...])
-    rows = rows_ref[...]
-    left = jnp.dot(rows, first, preferred_element_type=F32)
-    left += jnp.dot(rows, second, preferred_element_type=F32)
-    left += jnp.dot(rows, third, preferred_element_type=F32)
     right = left.T
     cols = cols_ref[...]
     dims = (((1,), (1,)), ((), ()))
@@ -331,12 +343,13 @@
             of((count, lines, B), BF16),
             of((count, lines, B), BF16),
         ),
-        in_specs=[SMEM, VMEM, HBM, HBM],
+        in_specs=[SMEM, HBM, HBM, HBM],
         out_specs=(VMEM, VMEM, VMEM),
         scratch_shapes=[
+            pltpu.VMEM((tile, tile), F32),
             pltpu.VMEM((L, tile), BF16),
             pltpu.VMEM((L, tile), BF16),
-            pltpu.SemaphoreType.DMA((4,)),
+            pltpu.SemaphoreType.DMA((4 + groups,)),
         ],
         compiler_params=FIRST_PARAMS,
         name="first",
@@ -371,8 +384,7 @@
     )(block, arrived, *shifted[:early])
     turn = [(i * n + j, j * n + i) for i in range(n) for j in range(n)]
     turned = lax.ppermute(piece, (*ROW, *COL), turn)
-    gathered = lax.all_gather(small, "core")
-    gathered = lax.all_gather(gathered, "z").reshape(n, small_rows, L)
+    gathered = lax.all_gather(small, COL)
     sent = pl.pallas_call(
         third_kernel,
         out_shape=of((n, small_rows + rows + strip_rows, L)),

time: 132 us -> 131 us (level)
  the two profiles are of different devices: /device:TPU:2 before, /device:TPU:1 now
where the time goes in v5:
time: 131 us
  starting transfers between devices  47.3 us (36%)
  blocking collectives  28.7 us (22%)
  Pallas kernels  26.8 us (20%)
  waiting for transfers between devices  26.5 us (20%)
  between operations  1.39 us (1%)
    all_gather x1, blocking collectives, all_steps(): gathered = lax.all_gather(small, COL)  28.7 us
    all_to_all x3, waiting for transfers between devices, exchanged(): return lax.all_to_all(parts, axis, split_axis=0, concat_axis=0, tiled=True)  23.7 us
    all_to_all x3, starting transfers between devices, exchanged(): return lax.all_to_all(parts, axis, split_axis=0, concat_axis=0, tiled=True)  23.3 us
    ppermute x7, starting transfers between devices, all_steps(): shifted.append(lax.ppermute(turned[k], 'z', perm))  16.5 us
    pallas_call x1, Pallas kernels, all_steps(): pl.pallas_call(fourth_kernel, out_shape=(of((tile, 2 * L), BF16), of((til...  14.6 us
    pallas_call x1, Pallas kernels, all_steps(): pl.pallas_call(last_kernel, grid=(steps,), out_shape=(of((tile, tile)), o...  5.89 us
    ppermute x1, starting transfers between devices, all_steps(): turned = lax.ppermute(piece, (*ROW, *COL), turn)  5.77 us
    pallas_call x1, Pallas kernels, all_steps(): pl.pallas_call(first_kernel, out_shape=(of((n, rows + cut + strip_rows, L...  4.02 us
  transfers between devices with their start and end apart: 13, of which 3 were waited for; matrix products, arithmetic and copies ran while one was open for 0% of the time, Pallas kernels for 12%

profile of v5, /device:TPU:1, one launch (start us, length us, event | category | flops | bytes accessed | tf_op | source)
XLA Modules:
  0.0 130.7 jit_solution(15358342497342483467)
XLA Ops:
  1.3 4.0 %first.1 = (f32[16,152,128]{2,1,0:T(8,128)}, bf16[8,96,256]{2,1,0:T(8,128)(2,1)}, bf16[8,96,256]{2,1,0:T(8,128)(2,1)}) custom-call(s32[1]{0:T(128)S(6)} %copy.6.block_ref, f32[768,768]{1,0:T(8,128)} %h_ref.1, bf16[128,12288]{1,0:T(8,128)(2,1)} %calib_ref.1, bf16[16,96,768]{2,1,0:T(8,128)(2,1)} %bitcast.3), custom_call_target="tpu_custom_call" | custom-call | tf_op jit(solution)/shard_map/first/pallas_call | solution.py:339
  5.3 0.0 copy-start
  5.3 7.7 %all-to-all-start = ((f32[16,152,128]{2,1,0:T(8,128)}), f32[16,152,128]{2,1,0:T(8,128)S(1)}, u32[]{:S(2)}, u32[]{:S(2)}) async-start(f32[16,152,128]{2,1,0:T(8,128)} %get-tuple-element.20), calls=%async_computation | async-start | bytes 2490368 | tf_op jit(solution)/shard_map/all_to_all | solution.py:21
  13.1 1.1 collective-permute-start
  14.1 1.3 %collective-permute-done.got_ref = bf16[8,96,256]{2,1,0:T(8,128)(2,1)S(1)} collective-permute-done((bf16[8,96,256]{2,1,0:T(8,128)(2,1)S(1)}, bf16[8,96,256]{2,1,0:T(8,128)(2,1)S(1)}, u32[]{:S(2)}, u32[]{:S(2)}) %collective-permute-start) | collective-permute-done | bytes 393248 | tf_op jit(solution)/shard_map/ppermute | solution.py:358
  15.5 1.7 %collective-permute-start.1 = (bf16[96,256]{1,0:T(8,128)(2,1)S(1)}, bf16[96,256]{1,0:T(8,128)(2,1)S(1)}, u32[]{:S(2)}, u32[]{:S(2)}) collective-permute-start(bf16[96,256]{1,0:T(8,128)(2,1)S(1)} %get-tuple-element.24), channel_id=1, source_target_pairs={{0,2},{2,4},{4,6},{6,8},{8,10},{10,12},{12,14},{14,0},{1,3},{3,5},... | collective-permute-start | bytes 147464 | tf_op jit(solution)/shard_map/ppermute | solution.py:371
  17.2 3.0 %collective-permute-start.2 = (bf16[96,256]{1,0:T(8,128)(2,1)S(1)}, bf16[96,256]{1,0:T(8,128)(2,1)S(1)}, u32[]{:S(2)}, u32[]{:S(2)}) collective-permute-start(bf16[96,256]{1,0:T(8,128)(2,1)S(1)} %get-tuple-element.25), channel_id=1, source_target_pairs={{0,4},{2,6},{4,8},{6,10},{8,12},{10,14},{12,0},{14,2},{1,5},{3,7},... | collective-permute-start | bytes 147464 | tf_op jit(solution)/shard_map/ppermute | solution.py:371
  20.2 3.8 %collective-permute-start.3 = (bf16[96,256]{1,0:T(8,128)(2,1)S(1)}, bf16[96,256]{1,0:T(8,128)(2,1)S(1)}, u32[]{:S(2)}, u32[]{:S(2)}) collective-permute-start(bf16[96,256]{1,0:T(8,128)(2,1)S(1)} %get-tuple-element.26), channel_id=1, source_target_pairs={{0,6},{2,8},{4,10},{6,12},{8,14},{10,0},{12,2},{14,4},{1,7},{3,9},... | collective-permute-start | bytes 147464 | tf_op jit(solution)/shard_map/ppermute | solution.py:371
  24.0 0.5 collective-permute-start.4
  24.4 4.5 %collective-permute-start.6 = (bf16[96,256]{1,0:T(8,128)(2,1)S(1)}, bf16[96,256]{1,0:T(8,128)(2,1)S(1)}, u32[]{:S(2)}, u32[]{:S(2)}) collective-permute-start(bf16[96,256]{1,0:T(8,128)(2,1)S(1)} %get-tuple-element.30), channel_id=1, source_target_pairs={{0,10},{2,12},{4,14},{6,0},{8,2},{10,4},{12,6},{14,8},{1,11},{3,13... | collective-permute-start | bytes 147464 | tf_op jit(solution)/shard_map/ppermute | solution.py:371
  28.9 0.0 collective-permute-done.1.refs_1_
  28.9 2.4 %collective-permute-start.7 = (bf16[96,256]{1,0:T(8,128)(2,1)S(1)}, bf16[96,256]{1,0:T(8,128)(2,1)S(1)}, u32[]{:S(2)}, u32[]{:S(2)}) collective-permute-start(bf16[96,256]{1,0:T(8,128)(2,1)S(1)} %get-tuple-element.31), channel_id=1, source_target_pairs={{0,12},{2,14},{4,0},{6,2},{8,4},{10,6},{12,8},{14,10},{1,13},{3,15... | collective-permute-start | bytes 147464 | tf_op jit(solution)/shard_map/ppermute | solution.py:371
  31.3 0.0 collective-permute-done.2.refs_2_
  31.3 0.7 collective-permute-start.8
  32.0 0.0 collective-permute-done.3.refs_3_
  32.0 0.0 all-to-all-done.arrived_ref
  32.0 0.1 second.1
  32.1 5.8 %collective-permute-start.5 = (f32[48,128]{1,0:T(8,128)S(1)}, f32[48,128]{1,0:T(8,128)S(1)}, u32[]{:S(2)}, u32[]{:S(2)}) collective-permute-start(f32[48,128]{1,0:T(8,128)S(1)} %get-tuple-element.29.piece_ref), channel_id=1, source_target_pairs={{0,0},{1,16},{2,32},{3,48},{4,64},{5,80},{6,96},{7,112},{8,128},{9... | collective-permute-start | bytes 73736 | tf_op jit(solution)/shard_map/ppermute | solution.py:386
  37.9 0.0 collective-permute-done.7.refs_1_
  37.9 0.0 collective-permute-done.8.refs_2_
  37.9 1.5 %collective-permute-done.5.turned_ref = f32[48,128]{1,0:T(8,128)S(1)} collective-permute-done((f32[48,128]{1,0:T(8,128)S(1)}, f32[48,128]{1,0:T(8,128)S(1)}, u32[]{:S(2)}, u32[]{:S(2)}) %collective-permute-start.5) | collective-permute-done | bytes 24608 | tf_op jit(solution)/shard_map/ppermute | solution.py:386
  39.4 0.9 pack.1
  40.3 11.9 %all-to-all-start.1 = ((bf16[8,144,256]{2,1,0:T(8,128)(2,1)}), bf16[8,144,256]{2,1,0:T(8,128)(2,1)S(1)}, u32[]{:S(2)}, u32[]{:S(2)}) async-start(bf16[8,144,256]{2,1,0:T(8,128)(2,1)} %pack.1), calls=%async_computation.1 | async-start | bytes 1179648 | tf_op jit(solution)/shard_map/all_to_all | solution.py:21
  52.2 28.7 %all-gather = f32[896,128]{1,0:T(8,128)S(1)} all-gather(f32[56,128]{1,0:T(8,128)S(1)} %get-tuple-element.33), channel_id=2, replica_groups=mesh['x'=4,'y'=4,'z'=8,'core'=2] {'z','core'}, dimensions={0}, use_global_device_ids=true | all-gather | bytes 487424 | tf_op jit(solution)/shard_map/all_gather | solution.py:387
  80.9 1.3 third.1
  82.2 0.0 all-to-all-done.1.own_ref
  82.2 3.7 %all-to-all-start.2 = ((f32[16,200,128]{2,1,0:T(8,128)}), f32[16,200,128]{2,1,0:T(8,128)S(1)}, u32[]{:S(2)}, u32[]{:S(2)}) async-start(f32[16,200,128]{2,1,0:T(8,128)} %third.1), calls=%async_computation.2 | async-start | bytes 3276800 | tf_op jit(solution)/shard_map/all_to_all | solution.py:21
  85.9 0.6 collective-permute-start.9
  86.5 23.7 %all-to-all-done.2.c_ref = f32[16,200,128]{2,1,0:T(8,128)S(1)} async-done(((f32[16,200,128]{2,1,0:T(8,128)}), f32[16,200,128]{2,1,0:T(8,128)S(1)}, u32[]{:S(2)}, u32[]{:S(2)}) %all-to-all-start.2) | async-done | bytes 1638432 | tf_op jit(solution)/shard_map/all_to_all | solution.py:21
  110.2 14.6 %fourth.1 = (bf16[768,256]{1,0:T(8,128)(2,1)S(1)}, bf16[768,128]{1,0:T(8,128)(2,1)S(1)}, bf16[256,768]{1,0:T(8,128)(2,1)S(1)}) custom-call(f32[16,200,128]{2,1,0:T(8,128)S(1)} %all-to-all-done.2.c_ref), custom_call_target="tpu_custom_call" | custom-call | flops 20000000000 | bytes 4000000 | tf_op jit(solution)/shard_map/fourth/pallas_call | solution.py:408
  124.8 0.0 collective-permute-done.9.other_ref
  124.8 5.9 %last.1 = (f32[768,768]{1,0:T(8,128)}, bf16[1536,768]{1,0:T(8,128)(2,1)}) custom-call(f32[768,768]{1,0:T(8,128)} %h_ref.1, bf16[1536,768]{1,0:T(8,128)(2,1)} %w_ref.1, bf16[8,144,256]{2,1,0:T(8,128)(2,1)S(1)} %all-to-all-done.1.own_ref, bf16[8,144,256]{2,1,0:T(8,128)(2,1)S(1)} %collective-permute-done.9.other_ref, ...), custom_call_target="tpu_custom_call" | custom-call | tf_op jit(solution)/shard_map/last/pallas_call | solution.py:427
  (6 shorter events, 0.1 us)
Async XLA Ops:
  5.3 7.7 %copy-start.1 = (bf16[8,96,256]{2,1,0:T(8,128)(2,1)S(1)}, bf16[8,96,256]{2,1,0:T(8,128)(2,1)}, u32[]{:S(2)}) copy-start(bf16[8,96,256]{2,1,0:T(8,128)(2,1)} %get-tuple-element.22) | copy-start | bytes 1179652
  5.3 10.1 %copy-start = (bf16[8,96,256]{2,1,0:T(8,128)(2,1)S(1)}, bf16[8,96,256]{2,1,0:T(8,128)(2,1)}, u32[]{:S(2)}) copy-start(bf16[8,96,256]{2,1,0:T(8,128)(2,1)} %get-tuple-element.21.keep_ref) | copy-start | bytes 1179652
  5.3 26.7 %all-to-all-start = ((f32[16,152,128]{2,1,0:T(8,128)}), f32[16,152,128]{2,1,0:T(8,128)S(1)}, u32[]{:S(2)}, u32[]{:S(2)}) async-start(f32[16,152,128]{2,1,0:T(8,128)} %get-tuple-element.20), calls=%async_computation | async-start | bytes 2490368 | tf_op jit(solution)/shard_map/all_to_all | solution.py:21
  13.1 2.4 %collective-permute-start = (bf16[8,96,256]{2,1,0:T(8,128)(2,1)S(1)}, bf16[8,96,256]{2,1,0:T(8,128)(2,1)S(1)}, u32[]{:S(2)}, u32[]{:S(2)}) collective-permute-start(bf16[8,96,256]{2,1,0:T(8,128)(2,1)S(1)} %copy-done.1), channel_id=1, source_target_pairs={{0,1},{1,0},{2,3},{3,2},{4,5},{5,4},{6,7},{7,6},{8,9},{9,8},{10,11... | collective-permute-start | bytes 1179656 | tf_op jit(solution)/shard_map/ppermute | solution.py:358
  15.5 13.4 %collective-permute-start.1 = (bf16[96,256]{1,0:T(8,128)(2,1)S(1)}, bf16[96,256]{1,0:T(8,128)(2,1)S(1)}, u32[]{:S(2)}, u32[]{:S(2)}) collective-permute-start(bf16[96,256]{1,0:T(8,128)(2,1)S(1)} %get-tuple-element.24), channel_id=1, source_target_pairs={{0,2},{2,4},{4,6},{6,8},{8,10},{10,12},{12,14},{14,0},{1,3},{3,5},... | collective-permute-start | bytes 147464 | tf_op jit(solution)/shard_map/ppermute | solution.py:371
  17.2 14.1 %collective-permute-start.2 = (bf16[96,256]{1,0:T(8,128)(2,1)S(1)}, bf16[96,256]{1,0:T(8,128)(2,1)S(1)}, u32[]{:S(2)}, u32[]{:S(2)}) collective-permute-start(bf16[96,256]{1,0:T(8,128)(2,1)S(1)} %get-tuple-element.25), channel_id=1, source_target_pairs={{0,4},{2,6},{4,8},{6,10},{8,12},{10,14},{12,0},{14,2},{1,5},{3,7},... | collective-permute-start | bytes 147464 | tf_op jit(solution)/shard_map/ppermute | solution.py:371
  20.2 11.8 %collective-permute-start.3 = (bf16[96,256]{1,0:T(8,128)(2,1)S(1)}, bf16[96,256]{1,0:T(8,128)(2,1)S(1)}, u32[]{:S(2)}, u32[]{:S(2)}) collective-permute-start(bf16[96,256]{1,0:T(8,128)(2,1)S(1)} %get-tuple-element.26), channel_id=1, source_target_pairs={{0,6},{2,8},{4,10},{6,12},{8,14},{10,0},{12,2},{14,4},{1,7},{3,9},... | collective-permute-start | bytes 147464 | tf_op jit(solution)/shard_map/ppermute | solution.py:371
  24.0 8.1 %collective-permute-start.4 = (bf16[96,256]{1,0:T(8,128)(2,1)S(1)}, bf16[96,256]{1,0:T(8,128)(2,1)S(1)}, u32[]{:S(2)}, u32[]{:S(2)}) collective-permute-start(bf16[96,256]{1,0:T(8,128)(2,1)S(1)} %get-tuple-element.27), channel_id=1, source_target_pairs={{0,8},{2,10},{4,12},{6,14},{8,0},{10,2},{12,4},{14,6},{1,9},{3,11}... | collective-permute-start | bytes 147464 | tf_op jit(solution)/shard_map/ppermute | solution.py:371
  24.4 13.5 %collective-permute-start.6 = (bf16[96,256]{1,0:T(8,128)(2,1)S(1)}, bf16[96,256]{1,0:T(8,128)(2,1)S(1)}, u32[]{:S(2)}, u32[]{:S(2)}) collective-permute-start(bf16[96,256]{1,0:T(8,128)(2,1)S(1)} %get-tuple-element.30), channel_id=1, source_target_pairs={{0,10},{2,12},{4,14},{6,0},{8,2},{10,4},{12,6},{14,8},{1,11},{3,13... | collective-permute-start | bytes 147464 | tf_op jit(solution)/shard_map/ppermute | solution.py:371
  28.9 9.0 %collective-permute-start.7 = (bf16[96,256]{1,0:T(8,128)(2,1)S(1)}, bf16[96,256]{1,0:T(8,128)(2,1)S(1)}, u32[]{:S(2)}, u32[]{:S(2)}) collective-permute-start(bf16[96,256]{1,0:T(8,128)(2,1)S(1)} %get-tuple-element.31), channel_id=1, source_target_pairs={{0,12},{2,14},{4,0},{6,2},{8,4},{10,6},{12,8},{14,10},{1,13},{3,15... | collective-permute-start | bytes 147464 | tf_op jit(solution)/shard_map/ppermute | solution.py:371
  31.3 6.6 %collective-permute-start.8 = (bf16[96,256]{1,0:T(8,128)(2,1)S(1)}, bf16[96,256]{1,0:T(8,128)(2,1)S(1)}, u32[]{:S(2)}, u32[]{:S(2)}) collective-permute-start(bf16[96,256]{1,0:T(8,128)(2,1)S(1)} %get-tuple-element.32), channel_id=1, source_target_pairs={{0,14},{2,0},{4,2},{6,4},{8,6},{10,8},{12,10},{14,12},{1,15},{3,1}... | collective-permute-start | bytes 147464 | tf_op jit(solution)/shard_map/ppermute | solution.py:371
  32.1 7.3 %collective-permute-start.5 = (f32[48,128]{1,0:T(8,128)S(1)}, f32[48,128]{1,0:T(8,128)S(1)}, u32[]{:S(2)}, u32[]{:S(2)}) collective-permute-start(f32[48,128]{1,0:T(8,128)S(1)} %get-tuple-element.29.piece_ref), channel_id=1, source_target_pairs={{0,0},{1,16},{2,32},{3,48},{4,64},{5,80},{6,96},{7,112},{8,128},{9... | collective-permute-start | bytes 73736 | tf_op jit(solution)/shard_map/ppermute | solution.py:386
  40.3 41.9 %all-to-all-start.1 = ((bf16[8,144,256]{2,1,0:T(8,128)(2,1)}), bf16[8,144,256]{2,1,0:T(8,128)(2,1)S(1)}, u32[]{:S(2)}, u32[]{:S(2)}) async-start(bf16[8,144,256]{2,1,0:T(8,128)(2,1)} %pack.1), calls=%async_computation.1 | async-start | bytes 1179648 | tf_op jit(solution)/shard_map/all_to_all | solution.py:21
  82.2 28.0 %all-to-all-start.2 = ((f32[16,200,128]{2,1,0:T(8,128)}), f32[16,200,128]{2,1,0:T(8,128)S(1)}, u32[]{:S(2)}, u32[]{:S(2)}) async-start(f32[16,200,128]{2,1,0:T(8,128)} %third.1), calls=%async_computation.2 | async-start | bytes 3276800 | tf_op jit(solution)/shard_map/all_to_all | solution.py:21
  85.9 38.9 %collective-permute-start.9 = (bf16[8,144,256]{2,1,0:T(8,128)(2,1)S(1)}, bf16[8,144,256]{2,1,0:T(8,128)(2,1)S(1)}, u32[]{:S(2)}, u32[]{:S(2)}) collective-permute-start(bf16[8,144,256]{2,1,0:T(8,128)(2,1)S(1)} %all-to-all-done.1.own_ref), channel_id=1, source_target_pairs={{0,1},{1,0},{2,3},{3,2},{4,5},{5,4},{6,7},{7,6},{8,9},{9,8},{10,11... | collective-permute-start | bytes 1769480 | tf_op jit(solution)/shard_map/ppermute | solution.py:407

commit v6 on v5

--- a/solution.py
+++ b/solution.py
@@ -184,43 +184,59 @@
         sent_ref[p, lines:, L:] = second
 
 
-def last_kernel(
-    h_ref, w_ref, own_ref, other_ref, twice_ref, low_ref, comp_ref, updated_ref, pruned_ref,
-    right_ref, window_ref,
-):
-    count, lines, _ = own_ref.shape
+def last_kernel(core_ref, h_ref, w_ref, half_ref, high_ref, low_ref, comp_ref, *refs):
+    updated_ref, pruned_ref, right_ref = refs[-3:]
+    count, lines, _ = half_ref.shape
     step = pl.program_id(0)
-    tile = right_ref.shape[0]
-    thin = B // (2 * count)
+    pairs, _, thin, tile = h_ref.shape
     groups = tile // B
     lines -= groups * thin
 
     @pl.when(step == 0)
     def _():
-        core = lax.axis_index("core")
-        for ref, c in ((own_ref, core), (other_ref, 1 - core)):
-            for z in range(count):
-                window_ref[c * count + z] = ref[z, 0:lines, :]
-                for s in range(groups):
-                    at = s * B + (2 * z + c) * thin
-                    right_ref[pl.ds(pl.multiple_of(at, thin), thin), :] = ref[
-                        z, lines + s * thin : lines + (s + 1) * thin, :
-                    ]
-
-    part = h_ref.shape[0]
+        for z in range(count):
+            for s in range(groups):
+                at = (s * count + z) * thin
+                right_ref[at : at + thin, :] = half_ref[
+                    z, lines + s * thin : lines + (s + 1) * thin, :
+                ]
+
+    part = pairs * thin
     right = right_ref[pl.ds(pl.multiple_of(step * part, 16), part), :]
     dims = (((1,), (1,)), ((), ()))
-    change = lax.dot_general(right, twice_ref[...], dims, preferred_element_type=F32)
+    change = lax.dot_general(right[:, L:], high_ref[...], dims, preferred_element_type=F32)
+    change += lax.dot_general(right[:, :L], high_ref[...], dims, preferred_element_type=F32)
     change += lax.dot_general(right[:, :L], low_ref[...], dims, preferred_element_type=F32)
-    updated_ref[...] = h_ref[...] - change
-    some = w_ref.shape[0] // lines
+    for q in range(pairs):
+        updated_ref[q, 0] = h_ref[q, 0] - change[q * thin : (q + 1) * thin]
+    some = w_ref.shape[1]
     comp = comp_ref[...]
     for q in range(some):
-        window = window_ref[step * some + q]
+        window = half_ref[step * some + q, 0:lines, :]
         product = jnp.dot(window, comp, preferred_element_type=F32)
-        pruned_ref[q * lines : (q + 1) * lines, :] = (
-            w_ref[q * lines : (q + 1) * lines, :].astype(F32) - product
-        ).astype(BF16)
+        pruned_ref[0, q] = (w_ref[0, q].astype(F32) - product).astype(BF16)
+
+
+def last_part(core, h, w, half, high, low, comp, done=()):
+    steps = 4
+    pairs, _, thin, tile = h.shape
+    _, count, lines, _ = w.shape
+    h_spec = pl.BlockSpec((pairs // steps, 1, thin, tile), lambda i, c: (i, c[0], 0, 0))
+    w_spec = pl.BlockSpec((1, count // steps, lines, tile), lambda i, c: (c[0], i, 0, 0))
+    return pl.pallas_call(
+        last_kernel,
+        grid_spec=pltpu.PrefetchScalarGridSpec(
+            num_scalar_prefetch=1,
+            grid=(steps,),
+            in_specs=[h_spec, w_spec, VMEM, VMEM, VMEM, VMEM] + [HBM] * len(done),
+            out_specs=(h_spec, w_spec),
+            scratch_shapes=[pltpu.VMEM((pairs * thin, 2 * L), BF16)],
+        ),
+        out_shape=(of(h.shape), of(w.shape, BF16)),
+        input_output_aliases={7 + k: k for k in range(len(done))},
+        compiler_params=LAST_PARAMS,
+        name="last",
+    )(core, h, w, half, high, low, comp, *done)
 
 
 def invert(a_ref):
@@ -264,7 +280,7 @@
 
 
 def fourth_kernel(
-    c_ref, twice_ref, low_ref, comp_ref, a_ref, gm_ref, gc_ref, q_ref, st_ref
+    c_ref, high_ref, low_ref, comp_ref, a_ref, gm_ref, gc_ref, q_ref, st_ref
 ):
     n = c_ref.shape[0]
     tile = gc_ref.shape[0]
@@ -295,8 +311,7 @@
     half = dot(block_right, x)
     solved = dot(right, x)
     high = solved.astype(BF16)
-    twice_ref[:, 0:L] = high
-    twice_ref[:, L:] = high
+    high_ref[...] = high
     low_ref[...] = (solved - high.astype(F32)).astype(BF16)
     square = q_ref[...] - dot_nt(half, block_right)
     square = 0.5 * (square + square.T)
@@ -364,7 +379,7 @@
         compiler_params=PARAMS,
         name="choose",
     )(block, keep, got)
-    early = count // 2 + 1
+    early = count // 2
     shifted = [turned[0]]
     for k in range(1, count):
         perm = [(i, (i + k) % count) for i in range(count)]
@@ -405,9 +420,9 @@
     )(block, window, turned, *shifted[early:])
     packed = exchanged(packed, "z")
     other = lax.ppermute(packed, "core", [(0, 1), (1, 0)])
-    twice, low, comp = pl.pallas_call(
+    high, low, comp = pl.pallas_call(
         fourth_kernel,
-        out_shape=(of((tile, 2 * L), BF16), of((tile, L), BF16), of((B, tile), BF16)),
+        out_shape=(of((tile, L), BF16), of((tile, L), BF16), of((B, tile), BF16)),
         in_specs=[VMEM],
         out_specs=(VMEM, VMEM, VMEM),
         scratch_shapes=[
@@ -423,28 +438,12 @@
         compiler_params=PARAMS,
         name="fourth",
     )(arrived)
-    steps = 4
-    return pl.pallas_call(
-        last_kernel,
-        grid=(steps,),
-        out_shape=(of((tile, tile)), of((n * lines, tile), BF16)),
-        in_specs=[
-            pl.BlockSpec((tile // steps, tile), lambda i: (i, 0)),
-            pl.BlockSpec((n * lines // steps, tile), lambda i: (i, 0)),
-            VMEM,
-            VMEM,
-            VMEM,
-            VMEM,
-            VMEM,
-        ],
-        out_specs=(
-            pl.BlockSpec((tile // steps, tile), lambda i: (i, 0)),
-            pl.BlockSpec((n * lines // steps, tile), lambda i: (i, 0)),
-        ),
-        scratch_shapes=[pltpu.VMEM((tile, 2 * L), BF16), pltpu.VMEM((n, lines, B), BF16)],
-        compiler_params=LAST_PARAMS,
-        name="last",
-    )(inv_hessian, weights, packed, other, twice, low, comp)
+    core = lax.axis_index("core").astype(jnp.int32).reshape(1)
+    h = inv_hessian.reshape(groups * count, 2, thin, tile)
+    w = weights.reshape(2, count, lines, tile)
+    done = last_part(core, h, w, packed, high, low, comp)
+    updated, pruned = last_part(1 - core, h, w, other, high, low, comp, done)
+    return (updated.reshape(tile, tile), pruned.reshape(n * lines, tile))
 
 
 def solution(mesh):

time: 131 us -> 135 us (1.031)
  Pallas kernels: 26.8 us -> 30.3 us
    pallas_call x2 -> x3, Pallas kernels: 20.5 us -> 24 us  [the longest x1 14.6 us: all_steps(): pl.pallas_call(fourth_kernel, out_shape=(of((tile, L), BF16), of((tile, L...]
  transfers between devices with their start and end apart: 13 -> 13, of which waited for: 3 -> 3; matrix products, arithmetic and copies ran while one was open for 0% -> 0% of each run, Pallas kernels for 12% -> 15%
where the time goes in v6:
time: 135 us; the launch traced here: 134 us
  starting transfers between devices  47.3 us (35%)
  Pallas kernels  30.3 us (22%)
  blocking collectives  28.7 us (21%)
  waiting for transfers between devices  26.7 us (20%)
  between operations  1.39 us (1%)
    all_gather x1, blocking collectives, all_steps(): gathered = lax.all_gather(small, COL)  28.7 us
    all_to_all x3, waiting for transfers between devices, exchanged(): return lax.all_to_all(parts, axis, split_axis=0, concat_axis=0, tiled=True)  23.8 us
    all_to_all x3, starting transfers between devices, exchanged(): return lax.all_to_all(parts, axis, split_axis=0, concat_axis=0, tiled=True)  23.4 us
    ppermute x7, starting transfers between devices, all_steps(): shifted.append(lax.ppermute(turned[k], 'z', perm))  16.5 us
    pallas_call x1, Pallas kernels, all_steps(): pl.pallas_call(fourth_kernel, out_shape=(of((tile, L), BF16), of((tile, L...  14.6 us
    pallas_call x2, Pallas kernels, last_part(): pl.pallas_call(last_kernel, grid_spec=pltpu.PrefetchScalarGridSpec(num_sc...  9.45 us
    ppermute x1, starting transfers between devices, all_steps(): turned = lax.ppermute(piece, (*ROW, *COL), turn)  5.77 us
    pallas_call x1, Pallas kernels, all_steps(): pl.pallas_call(first_kernel, out_shape=(of((n, rows + cut + strip_rows, L...  4.02 us
  transfers between devices with their start and end apart: 13, of which 3 were waited for; matrix products, arithmetic and copies ran while one was open for 0% of the time, Pallas kernels for 15%

profile of v6, /device:TPU:1, one launch (start us, length us, event | category | flops | bytes accessed | tf_op | source)
XLA Modules:
  0.0 134.3 jit_solution(9536162035049445130)
XLA Ops:
  1.3 4.0 %first.1 = (f32[16,152,128]{2,1,0:T(8,128)}, bf16[8,96,256]{2,1,0:T(8,128)(2,1)}, bf16[8,96,256]{2,1,0:T(8,128)(2,1)}) custom-call(s32[1]{0:T(128)S(6)} %copy.10.block_ref, f32[768,768]{1,0:T(8,128)} %source_ref.1, bf16[128,12288]{1,0:T(8,128)(2,1)} %calib_ref.1, bf16[16,96,768]{2,1,0:T(8,128)(2,1)} %bitcast.10), custom_call_target="tpu_custom_call" | custom-call | tf_op jit(solution)/shard_map/first/pallas_call | solution.py:354
  5.3 0.0 copy-start
  5.3 7.7 %all-to-all-start = ((f32[16,152,128]{2,1,0:T(8,128)}), f32[16,152,128]{2,1,0:T(8,128)S(1)}, u32[]{:S(2)}, u32[]{:S(2)}) async-start(f32[16,152,128]{2,1,0:T(8,128)} %get-tuple-element.24), calls=%async_computation | async-start | bytes 2490368 | tf_op jit(solution)/shard_map/all_to_all | solution.py:21
  13.1 1.1 collective-permute-start
  14.1 1.3 %collective-permute-done.got_ref = bf16[8,96,256]{2,1,0:T(8,128)(2,1)S(1)} collective-permute-done((bf16[8,96,256]{2,1,0:T(8,128)(2,1)S(1)}, bf16[8,96,256]{2,1,0:T(8,128)(2,1)S(1)}, u32[]{:S(2)}, u32[]{:S(2)}) %collective-permute-start) | collective-permute-done | bytes 393248 | tf_op jit(solution)/shard_map/ppermute | solution.py:373
  15.5 1.7 %collective-permute-start.1 = (bf16[96,256]{1,0:T(8,128)(2,1)S(1)}, bf16[96,256]{1,0:T(8,128)(2,1)S(1)}, u32[]{:S(2)}, u32[]{:S(2)}) collective-permute-start(bf16[96,256]{1,0:T(8,128)(2,1)S(1)} %get-tuple-element.28), channel_id=1, source_target_pairs={{0,2},{2,4},{4,6},{6,8},{8,10},{10,12},{12,14},{14,0},{1,3},{3,5},... | collective-permute-start | bytes 147464 | tf_op jit(solution)/shard_map/ppermute | solution.py:386
  17.2 3.0 %collective-permute-start.2 = (bf16[96,256]{1,0:T(8,128)(2,1)S(1)}, bf16[96,256]{1,0:T(8,128)(2,1)S(1)}, u32[]{:S(2)}, u32[]{:S(2)}) collective-permute-start(bf16[96,256]{1,0:T(8,128)(2,1)S(1)} %get-tuple-element.29), channel_id=1, source_target_pairs={{0,4},{2,6},{4,8},{6,10},{8,12},{10,14},{12,0},{14,2},{1,5},{3,7},... | collective-permute-start | bytes 147464 | tf_op jit(solution)/shard_map/ppermute | solution.py:386
  20.2 3.8 %collective-permute-start.3 = (bf16[96,256]{1,0:T(8,128)(2,1)S(1)}, bf16[96,256]{1,0:T(8,128)(2,1)S(1)}, u32[]{:S(2)}, u32[]{:S(2)}) collective-permute-start(bf16[96,256]{1,0:T(8,128)(2,1)S(1)} %get-tuple-element.30), channel_id=1, source_target_pairs={{0,6},{2,8},{4,10},{6,12},{8,14},{10,0},{12,2},{14,4},{1,7},{3,9},... | collective-permute-start | bytes 147464 | tf_op jit(solution)/shard_map/ppermute | solution.py:386
  24.0 0.5 collective-permute-start.5
  24.4 4.5 %collective-permute-start.6 = (bf16[96,256]{1,0:T(8,128)(2,1)S(1)}, bf16[96,256]{1,0:T(8,128)(2,1)S(1)}, u32[]{:S(2)}, u32[]{:S(2)}) collective-permute-start(bf16[96,256]{1,0:T(8,128)(2,1)S(1)} %get-tuple-element.34), channel_id=1, source_target_pairs={{0,10},{2,12},{4,14},{6,0},{8,2},{10,4},{12,6},{14,8},{1,11},{3,13... | collective-permute-start | bytes 147464 | tf_op jit(solution)/shard_map/ppermute | solution.py:386
  28.9 0.0 collective-permute-done.1.refs_1_
  28.9 2.4 %collective-permute-start.7 = (bf16[96,256]{1,0:T(8,128)(2,1)S(1)}, bf16[96,256]{1,0:T(8,128)(2,1)S(1)}, u32[]{:S(2)}, u32[]{:S(2)}) collective-permute-start(bf16[96,256]{1,0:T(8,128)(2,1)S(1)} %get-tuple-element.35), channel_id=1, source_target_pairs={{0,12},{2,14},{4,0},{6,2},{8,4},{10,6},{12,8},{14,10},{1,13},{3,15... | collective-permute-start | bytes 147464 | tf_op jit(solution)/shard_map/ppermute | solution.py:386
  31.3 0.0 collective-permute-done.2.refs_2_
  31.3 0.7 collective-permute-start.8
  32.0 0.0 collective-permute-done.3.refs_3_
  32.0 0.0 all-to-all-done.arrived_ref
  32.1 5.8 %collective-permute-start.4 = (f32[48,128]{1,0:T(8,128)S(1)}, f32[48,128]{1,0:T(8,128)S(1)}, u32[]{:S(2)}, u32[]{:S(2)}) collective-permute-start(f32[48,128]{1,0:T(8,128)S(1)} %get-tuple-element.32.piece_ref), channel_id=1, source_target_pairs={{0,0},{1,16},{2,32},{3,48},{4,64},{5,80},{6,96},{7,112},{8,128},{9... | collective-permute-start | bytes 73736 | tf_op jit(solution)/shard_map/ppermute | solution.py:401
  37.8 0.0 collective-permute-done.6.refs_1_
  37.9 0.0 collective-permute-done.7.refs_2_
  37.9 1.5 %collective-permute-done.4.turned_ref = f32[48,128]{1,0:T(8,128)S(1)} collective-permute-done((f32[48,128]{1,0:T(8,128)S(1)}, f32[48,128]{1,0:T(8,128)S(1)}, u32[]{:S(2)}, u32[]{:S(2)}) %collective-permute-start.4) | collective-permute-done | bytes 24608 | tf_op jit(solution)/shard_map/ppermute | solution.py:401
  39.3 0.9 pack.1
  40.2 12.0 %all-to-all-start.1 = ((bf16[8,144,256]{2,1,0:T(8,128)(2,1)}), bf16[8,144,256]{2,1,0:T(8,128)(2,1)S(1)}, u32[]{:S(2)}, u32[]{:S(2)}) async-start(bf16[8,144,256]{2,1,0:T(8,128)(2,1)} %pack.1), calls=%async_computation.1 | async-start | bytes 1179648 | tf_op jit(solution)/shard_map/all_to_all | solution.py:21
  52.2 28.7 %all-gather = f32[896,128]{1,0:T(8,128)S(1)} all-gather(f32[56,128]{1,0:T(8,128)S(1)} %get-tuple-element.37), channel_id=2, replica_groups=mesh['x'=4,'y'=4,'z'=8,'core'=2] {'z','core'}, dimensions={0}, use_global_device_ids=true | all-gather | bytes 487424 | tf_op jit(solution)/shard_map/all_gather | solution.py:402
  80.9 1.3 third.1
  82.2 0.0 all-to-all-done.1.half_ref
  82.2 3.7 %all-to-all-start.2 = ((f32[16,200,128]{2,1,0:T(8,128)}), f32[16,200,128]{2,1,0:T(8,128)S(1)}, u32[]{:S(2)}, u32[]{:S(2)}) async-start(f32[16,200,128]{2,1,0:T(8,128)} %third.1), calls=%async_computation.2 | async-start | bytes 3276800 | tf_op jit(solution)/shard_map/all_to_all | solution.py:21
  85.9 0.5 collective-permute-start.9
  86.4 23.8 %all-to-all-done.2.c_ref = f32[16,200,128]{2,1,0:T(8,128)S(1)} async-done(((f32[16,200,128]{2,1,0:T(8,128)}), f32[16,200,128]{2,1,0:T(8,128)S(1)}, u32[]{:S(2)}, u32[]{:S(2)}) %all-to-all-start.2) | async-done | bytes 1638432 | tf_op jit(solution)/shard_map/all_to_all | solution.py:21
  110.3 14.6 %fourth.1 = (bf16[768,128]{1,0:T(8,128)(2,1)S(1)}, bf16[768,128]{1,0:T(8,128)(2,1)S(1)}, bf16[256,768]{1,0:T(8,128)(2,1)S(1)}) custom-call(f32[16,200,128]{2,1,0:T(8,128)S(1)} %all-to-all-done.2.c_ref), custom_call_target="tpu_custom_call" | custom-call | flops 20000000000 | bytes 4000000 | tf_op jit(solution)/shard_map/fourth/pallas_call | solution.py:423
  124.9 4.7 %last.2 = (f32[24,2,16,768]{3,2,1,0:T(8,128)}, bf16[2,8,96,768]{3,2,1,0:T(8,128)(2,1)}) custom-call(s32[1]{0:T(128)} %bitcast.core_ref, f32[24,2,16,768]{3,2,1,0:T(8,128)} %bitcast.8, bf16[2,8,96,768]{3,2,1,0:T(8,128)(2,1)} %bitcast.11, bf16[8,144,256]{2,1,0:T(8,128)(2,1)S(1)} %all-to-all-done.1.half_ref, bf16[768,128]{1,0:T(8,128)(2,1)S(1)} %get-tuple-element.39.high_ref, ...), custom_call_target="tpu_custom_call" | custom-call | tf_op jit(solution)/shard_map/last/pallas_call | solution.py:226
  129.6 0.0 collective-permute-done.9.half_ref
  129.6 4.7 %last.3 = (f32[24,2,16,768]{3,2,1,0:T(8,128)}, bf16[2,8,96,768]{3,2,1,0:T(8,128)(2,1)}) custom-call(s32[1]{0:T(128)S(6)} %sub.3.core_ref, f32[24,2,16,768]{3,2,1,0:T(8,128)} %bitcast.9, bf16[2,8,96,768]{3,2,1,0:T(8,128)(2,1)} %bitcast.12, bf16[8,144,256]{2,1,0:T(8,128)(2,1)S(1)} %collective-permute-done.9.half_ref, ...), custom_call_target="tpu_custom_call", output_to_operand_aliasing={{0}: (7, {}), {1}: (8, {})} | custom-call | tf_op jit(solution)/shard_map/last/pallas_call | solution.py:226
  (7 shorter events, 0.1 us)
Async XLA Ops:
  5.3 7.7 %copy-start.1 = (bf16[8,96,256]{2,1,0:T(8,128)(2,1)S(1)}, bf16[8,96,256]{2,1,0:T(8,128)(2,1)}, u32[]{:S(2)}) copy-start(bf16[8,96,256]{2,1,0:T(8,128)(2,1)} %get-tuple-element.26) | copy-start | bytes 1179652
  5.3 10.1 %copy-start = (bf16[8,96,256]{2,1,0:T(8,128)(2,1)S(1)}, bf16[8,96,256]{2,1,0:T(8,128)(2,1)}, u32[]{:S(2)}) copy-start(bf16[8,96,256]{2,1,0:T(8,128)(2,1)} %get-tuple-element.25.keep_ref) | copy-start | bytes 1179652
  5.3 26.7 %all-to-all-start = ((f32[16,152,128]{2,1,0:T(8,128)}), f32[16,152,128]{2,1,0:T(8,128)S(1)}, u32[]{:S(2)}, u32[]{:S(2)}) async-start(f32[16,152,128]{2,1,0:T(8,128)} %get-tuple-element.24), calls=%async_computation | async-start | bytes 2490368 | tf_op jit(solution)/shard_map/all_to_all | solution.py:21
  13.1 2.4 %collective-permute-start = (bf16[8,96,256]{2,1,0:T(8,128)(2,1)S(1)}, bf16[8,96,256]{2,1,0:T(8,128)(2,1)S(1)}, u32[]{:S(2)}, u32[]{:S(2)}) collective-permute-start(bf16[8,96,256]{2,1,0:T(8,128)(2,1)S(1)} %copy-done.1), channel_id=1, source_target_pairs={{0,1},{1,0},{2,3},{3,2},{4,5},{5,4},{6,7},{7,6},{8,9},{9,8},{10,11... | collective-permute-start | bytes 1179656 | tf_op jit(solution)/shard_map/ppermute | solution.py:373
  15.5 13.4 %collective-permute-start.1 = (bf16[96,256]{1,0:T(8,128)(2,1)S(1)}, bf16[96,256]{1,0:T(8,128)(2,1)S(1)}, u32[]{:S(2)}, u32[]{:S(2)}) collective-permute-start(bf16[96,256]{1,0:T(8,128)(2,1)S(1)} %get-tuple-element.28), channel_id=1, source_target_pairs={{0,2},{2,4},{4,6},{6,8},{8,10},{10,12},{12,14},{14,0},{1,3},{3,5},... | collective-permute-start | bytes 147464 | tf_op jit(solution)/shard_map/ppermute | solution.py:386
  17.2 14.1 %collective-permute-start.2 = (bf16[96,256]{1,0:T(8,128)(2,1)S(1)}, bf16[96,256]{1,0:T(8,128)(2,1)S(1)}, u32[]{:S(2)}, u32[]{:S(2)}) collective-permute-start(bf16[96,256]{1,0:T(8,128)(2,1)S(1)} %get-tuple-element.29), channel_id=1, source_target_pairs={{0,4},{2,6},{4,8},{6,10},{8,12},{10,14},{12,0},{14,2},{1,5},{3,7},... | collective-permute-start | bytes 147464 | tf_op jit(solution)/shard_map/ppermute | solution.py:386
  20.2 11.8 %collective-permute-start.3 = (bf16[96,256]{1,0:T(8,128)(2,1)S(1)}, bf16[96,256]{1,0:T(8,128)(2,1)S(1)}, u32[]{:S(2)}, u32[]{:S(2)}) collective-permute-start(bf16[96,256]{1,0:T(8,128)(2,1)S(1)} %get-tuple-element.30), channel_id=1, source_target_pairs={{0,6},{2,8},{4,10},{6,12},{8,14},{10,0},{12,2},{14,4},{1,7},{3,9},... | collective-permute-start | bytes 147464 | tf_op jit(solution)/shard_map/ppermute | solution.py:386
  24.0 13.9 %collective-permute-start.5 = (bf16[96,256]{1,0:T(8,128)(2,1)S(1)}, bf16[96,256]{1,0:T(8,128)(2,1)S(1)}, u32[]{:S(2)}, u32[]{:S(2)}) collective-permute-start(bf16[96,256]{1,0:T(8,128)(2,1)S(1)} %get-tuple-element.33), channel_id=1, source_target_pairs={{0,8},{2,10},{4,12},{6,14},{8,0},{10,2},{12,4},{14,6},{1,9},{3,11}... | collective-permute-start | bytes 147464 | tf_op jit(solution)/shard_map/ppermute | solution.py:386
  24.4 13.4 %collective-permute-start.6 = (bf16[96,256]{1,0:T(8,128)(2,1)S(1)}, bf16[96,256]{1,0:T(8,128)(2,1)S(1)}, u32[]{:S(2)}, u32[]{:S(2)}) collective-permute-start(bf16[96,256]{1,0:T(8,128)(2,1)S(1)} %get-tuple-element.34), channel_id=1, source_target_pairs={{0,10},{2,12},{4,14},{6,0},{8,2},{10,4},{12,6},{14,8},{1,11},{3,13... | collective-permute-start | bytes 147464 | tf_op jit(solution)/shard_map/ppermute | solution.py:386
  28.9 9.0 %collective-permute-start.7 = (bf16[96,256]{1,0:T(8,128)(2,1)S(1)}, bf16[96,256]{1,0:T(8,128)(2,1)S(1)}, u32[]{:S(2)}, u32[]{:S(2)}) collective-permute-start(bf16[96,256]{1,0:T(8,128)(2,1)S(1)} %get-tuple-element.35), channel_id=1, source_target_pairs={{0,12},{2,14},{4,0},{6,2},{8,4},{10,6},{12,8},{14,10},{1,13},{3,15... | collective-permute-start | bytes 147464 | tf_op jit(solution)/shard_map/ppermute | solution.py:386
  31.3 6.6 %collective-permute-start.8 = (bf16[96,256]{1,0:T(8,128)(2,1)S(1)}, bf16[96,256]{1,0:T(8,128)(2,1)S(1)}, u32[]{:S(2)}, u32[]{:S(2)}) collective-permute-start(bf16[96,256]{1,0:T(8,128)(2,1)S(1)} %get-tuple-element.36), channel_id=1, source_target_pairs={{0,14},{2,0},{4,2},{6,4},{8,6},{10,8},{12,10},{14,12},{1,15},{3,1}... | collective-permute-start | bytes 147464 | tf_op jit(solution)/shard_map/ppermute | solution.py:386
  32.1 7.3 %collective-permute-start.4 = (f32[48,128]{1,0:T(8,128)S(1)}, f32[48,128]{1,0:T(8,128)S(1)}, u32[]{:S(2)}, u32[]{:S(2)}) collective-permute-start(f32[48,128]{1,0:T(8,128)S(1)} %get-tuple-element.32.piece_ref), channel_id=1, source_target_pairs={{0,0},{1,16},{2,32},{3,48},{4,64},{5,80},{6,96},{7,112},{8,128},{9... | collective-permute-start | bytes 73736 | tf_op jit(solution)/shard_map/ppermute | solution.py:401
  40.2 42.0 %all-to-all-start.1 = ((bf16[8,144,256]{2,1,0:T(8,128)(2,1)}), bf16[8,144,256]{2,1,0:T(8,128)(2,1)S(1)}, u32[]{:S(2)}, u32[]{:S(2)}) async-start(bf16[8,144,256]{2,1,0:T(8,128)(2,1)} %pack.1), calls=%async_computation.1 | async-start | bytes 1179648 | tf_op jit(solution)/shard_map/all_to_all | solution.py:21
  82.2 28.1 %all-to-all-start.2 = ((f32[16,200,128]{2,1,0:T(8,128)}), f32[16,200,128]{2,1,0:T(8,128)S(1)}, u32[]{:S(2)}, u32[]{:S(2)}) async-start(f32[16,200,128]{2,1,0:T(8,128)} %third.1), calls=%async_computation.2 | async-start | bytes 3276800 | tf_op jit(solution)/shard_map/all_to_all | solution.py:21
  85.9 43.7 %collective-permute-start.9 = (bf16[8,144,256]{2,1,0:T(8,128)(2,1)S(1)}, bf16[8,144,256]{2,1,0:T(8,128)(2,1)S(1)}, u32[]{:S(2)}, u32[]{:S(2)}) collective-permute-start(bf16[8,144,256]{2,1,0:T(8,128)(2,1)S(1)} %all-to-all-done.1.half_ref), channel_id=1, source_target_pairs={{0,1},{1,0},{2,3},{3,2},{4,5},{5,4},{6,7},{7,6},{8,9},{9,8},{10,11... | collective-permute-start | bytes 1769480 | tf_op jit(solution)/shard_map/ppermute | solution.py:422

commit v7 on v5

--- a/solution.py
+++ b/solution.py
@@ -215,12 +215,9 @@
     updated_ref[...] = h_ref[...] - change
     some = w_ref.shape[0] // lines
     comp = comp_ref[...]
-    for q in range(some):
-        window = window_ref[step * some + q]
-        product = jnp.dot(window, comp, preferred_element_type=F32)
-        pruned_ref[q * lines : (q + 1) * lines, :] = (
-            w_ref[q * lines : (q + 1) * lines, :].astype(F32) - product
-        ).astype(BF16)
+    window = window_ref[pl.ds(step * some, some)].reshape(some * lines, B)
+    product = jnp.dot(window, comp, preferred_element_type=F32)
+    pruned_ref[...] = (w_ref[...].astype(F32) - product).astype(BF16)
 
 
 def invert(a_ref):
@@ -364,7 +361,7 @@
         compiler_params=PARAMS,
         name="choose",
     )(block, keep, got)
-    early = count // 2 + 1
+    early = count // 2
     shifted = [turned[0]]
     for k in range(1, count):
         perm = [(i, (i + k) % count) for i in range(count)]

time: 131 us -> 131 us (level)
  no operation moved by 1% of the time
where the time goes in v7:
time: 131 us
  starting transfers between devices  47.3 us (36%)
  blocking collectives  28.7 us (22%)
  Pallas kernels  26.7 us (20%)
  waiting for transfers between devices  26.7 us (20%)
  between operations  1.4 us (1%)
    all_gather x1, blocking collectives, all_steps(): gathered = lax.all_gather(small, COL)  28.7 us
    all_to_all x3, waiting for transfers between devices, exchanged(): return lax.all_to_all(parts, axis, split_axis=0, concat_axis=0, tiled=True)  23.8 us
    all_to_all x3, starting transfers between devices, exchanged(): return lax.all_to_all(parts, axis, split_axis=0, concat_axis=0, tiled=True)  23.4 us
    ppermute x7, starting transfers between devices, all_steps(): shifted.append(lax.ppermute(turned[k], 'z', perm))  16.5 us
    pallas_call x1, Pallas kernels, all_steps(): pl.pallas_call(fourth_kernel, out_shape=(of((tile, 2 * L), BF16), of((til...  14.6 us
    pallas_call x1, Pallas kernels, all_steps(): pl.pallas_call(last_kernel, grid=(steps,), out_shape=(of((tile, tile)), o...  5.82 us
    ppermute x1, starting transfers between devices, all_steps(): turned = lax.ppermute(piece, (*ROW, *COL), turn)  5.77 us
    pallas_call x1, Pallas kernels, all_steps(): pl.pallas_call(first_kernel, out_shape=(of((n, rows + cut + strip_rows, L...  4.02 us
  transfers between devices with their start and end apart: 13, of which 3 were waited for; matrix products, arithmetic and copies ran while one was open for 0% of the time, Pallas kernels for 12%

profile of v7, /device:TPU:1, one launch (start us, length us, event | category | flops | bytes accessed | tf_op | source)
XLA Modules:
  0.0 130.7 jit_solution(13445972736247442807)
XLA Ops:
  1.3 4.0 %first.1 = (f32[16,152,128]{2,1,0:T(8,128)}, bf16[8,96,256]{2,1,0:T(8,128)(2,1)}, bf16[8,96,256]{2,1,0:T(8,128)(2,1)}) custom-call(s32[1]{0:T(128)S(6)} %copy.6.block_ref, f32[768,768]{1,0:T(8,128)} %h_ref.1, bf16[128,12288]{1,0:T(8,128)(2,1)} %calib_ref.1, bf16[16,96,768]{2,1,0:T(8,128)(2,1)} %bitcast.3), custom_call_target="tpu_custom_call" | custom-call | tf_op jit(solution)/shard_map/first/pallas_call | solution.py:336
  5.3 0.0 copy-start
  5.3 7.7 %all-to-all-start = ((f32[16,152,128]{2,1,0:T(8,128)}), f32[16,152,128]{2,1,0:T(8,128)S(1)}, u32[]{:S(2)}, u32[]{:S(2)}) async-start(f32[16,152,128]{2,1,0:T(8,128)} %get-tuple-element.20), calls=%async_computation | async-start | bytes 2490368 | tf_op jit(solution)/shard_map/all_to_all | solution.py:21
  13.1 1.1 collective-permute-start
  14.1 1.3 %collective-permute-done.got_ref = bf16[8,96,256]{2,1,0:T(8,128)(2,1)S(1)} collective-permute-done((bf16[8,96,256]{2,1,0:T(8,128)(2,1)S(1)}, bf16[8,96,256]{2,1,0:T(8,128)(2,1)S(1)}, u32[]{:S(2)}, u32[]{:S(2)}) %collective-permute-start) | collective-permute-done | bytes 393248 | tf_op jit(solution)/shard_map/ppermute | solution.py:355
  15.5 1.7 %collective-permute-start.1 = (bf16[96,256]{1,0:T(8,128)(2,1)S(1)}, bf16[96,256]{1,0:T(8,128)(2,1)S(1)}, u32[]{:S(2)}, u32[]{:S(2)}) collective-permute-start(bf16[96,256]{1,0:T(8,128)(2,1)S(1)} %get-tuple-element.24), channel_id=1, source_target_pairs={{0,2},{2,4},{4,6},{6,8},{8,10},{10,12},{12,14},{14,0},{1,3},{3,5},... | collective-permute-start | bytes 147464 | tf_op jit(solution)/shard_map/ppermute | solution.py:368
  17.2 3.0 %collective-permute-start.2 = (bf16[96,256]{1,0:T(8,128)(2,1)S(1)}, bf16[96,256]{1,0:T(8,128)(2,1)S(1)}, u32[]{:S(2)}, u32[]{:S(2)}) collective-permute-start(bf16[96,256]{1,0:T(8,128)(2,1)S(1)} %get-tuple-element.25), channel_id=1, source_target_pairs={{0,4},{2,6},{4,8},{6,10},{8,12},{10,14},{12,0},{14,2},{1,5},{3,7},... | collective-permute-start | bytes 147464 | tf_op jit(solution)/shard_map/ppermute | solution.py:368
  20.2 3.8 %collective-permute-start.3 = (bf16[96,256]{1,0:T(8,128)(2,1)S(1)}, bf16[96,256]{1,0:T(8,128)(2,1)S(1)}, u32[]{:S(2)}, u32[]{:S(2)}) collective-permute-start(bf16[96,256]{1,0:T(8,128)(2,1)S(1)} %get-tuple-element.26), channel_id=1, source_target_pairs={{0,6},{2,8},{4,10},{6,12},{8,14},{10,0},{12,2},{14,4},{1,7},{3,9},... | collective-permute-start | bytes 147464 | tf_op jit(solution)/shard_map/ppermute | solution.py:368
  24.0 0.5 collective-permute-start.5
  24.4 4.5 %collective-permute-start.6 = (bf16[96,256]{1,0:T(8,128)(2,1)S(1)}, bf16[96,256]{1,0:T(8,128)(2,1)S(1)}, u32[]{:S(2)}, u32[]{:S(2)}) collective-permute-start(bf16[96,256]{1,0:T(8,128)(2,1)S(1)} %get-tuple-element.30), channel_id=1, source_target_pairs={{0,10},{2,12},{4,14},{6,0},{8,2},{10,4},{12,6},{14,8},{1,11},{3,13... | collective-permute-start | bytes 147464 | tf_op jit(solution)/shard_map/ppermute | solution.py:368
  28.9 0.0 collective-permute-done.1.refs_1_
  28.9 2.4 %collective-permute-start.7 = (bf16[96,256]{1,0:T(8,128)(2,1)S(1)}, bf16[96,256]{1,0:T(8,128)(2,1)S(1)}, u32[]{:S(2)}, u32[]{:S(2)}) collective-permute-start(bf16[96,256]{1,0:T(8,128)(2,1)S(1)} %get-tuple-element.31), channel_id=1, source_target_pairs={{0,12},{2,14},{4,0},{6,2},{8,4},{10,6},{12,8},{14,10},{1,13},{3,15... | collective-permute-start | bytes 147464 | tf_op jit(solution)/shard_map/ppermute | solution.py:368
  31.3 0.0 collective-permute-done.2.refs_2_
  31.3 0.7 collective-permute-start.8
  32.0 0.0 collective-permute-done.3.refs_3_
  32.0 0.0 all-to-all-done.arrived_ref
  32.1 5.8 %collective-permute-start.4 = (f32[48,128]{1,0:T(8,128)S(1)}, f32[48,128]{1,0:T(8,128)S(1)}, u32[]{:S(2)}, u32[]{:S(2)}) collective-permute-start(f32[48,128]{1,0:T(8,128)S(1)} %get-tuple-element.28.piece_ref), channel_id=1, source_target_pairs={{0,0},{1,16},{2,32},{3,48},{4,64},{5,80},{6,96},{7,112},{8,128},{9... | collective-permute-start | bytes 73736 | tf_op jit(solution)/shard_map/ppermute | solution.py:383
  37.8 0.0 collective-permute-done.5.refs_0_
  37.8 0.0 collective-permute-done.6.refs_1_
  37.9 0.0 collective-permute-done.7.refs_2_
  37.9 1.5 %collective-permute-done.4.turned_ref = f32[48,128]{1,0:T(8,128)S(1)} collective-permute-done((f32[48,128]{1,0:T(8,128)S(1)}, f32[48,128]{1,0:T(8,128)S(1)}, u32[]{:S(2)}, u32[]{:S(2)}) %collective-permute-start.4) | collective-permute-done | bytes 24608 | tf_op jit(solution)/shard_map/ppermute | solution.py:383
  39.3 0.9 pack.1
  40.2 12.0 %all-to-all-start.1 = ((bf16[8,144,256]{2,1,0:T(8,128)(2,1)}), bf16[8,144,256]{2,1,0:T(8,128)(2,1)S(1)}, u32[]{:S(2)}, u32[]{:S(2)}) async-start(bf16[8,144,256]{2,1,0:T(8,128)(2,1)} %pack.1), calls=%async_computation.1 | async-start | bytes 1179648 | tf_op jit(solution)/shard_map/all_to_all | solution.py:21
  52.2 28.7 %all-gather = f32[896,128]{1,0:T(8,128)S(1)} all-gather(f32[56,128]{1,0:T(8,128)S(1)} %get-tuple-element.33), channel_id=2, replica_groups=mesh['x'=4,'y'=4,'z'=8,'core'=2] {'z','core'}, dimensions={0}, use_global_device_ids=true | all-gather | bytes 487424 | tf_op jit(solution)/shard_map/all_gather | solution.py:384
  80.9 1.3 third.1
  82.2 0.0 all-to-all-done.1.own_ref
  82.2 3.7 %all-to-all-start.2 = ((f32[16,200,128]{2,1,0:T(8,128)}), f32[16,200,128]{2,1,0:T(8,128)S(1)}, u32[]{:S(2)}, u32[]{:S(2)}) async-start(f32[16,200,128]{2,1,0:T(8,128)} %third.1), calls=%async_computation.2 | async-start | bytes 3276800 | tf_op jit(solution)/shard_map/all_to_all | solution.py:21
  85.9 0.5 collective-permute-start.9
  86.4 23.8 %all-to-all-done.2.c_ref = f32[16,200,128]{2,1,0:T(8,128)S(1)} async-done(((f32[16,200,128]{2,1,0:T(8,128)}), f32[16,200,128]{2,1,0:T(8,128)S(1)}, u32[]{:S(2)}, u32[]{:S(2)}) %all-to-all-start.2) | async-done | bytes 1638432 | tf_op jit(solution)/shard_map/all_to_all | solution.py:21
  110.3 14.6 %fourth.1 = (bf16[768,256]{1,0:T(8,128)(2,1)S(1)}, bf16[768,128]{1,0:T(8,128)(2,1)S(1)}, bf16[256,768]{1,0:T(8,128)(2,1)S(1)}) custom-call(f32[16,200,128]{2,1,0:T(8,128)S(1)} %all-to-all-done.2.c_ref), custom_call_target="tpu_custom_call" | custom-call | flops 20000000000 | bytes 4000000 | tf_op jit(solution)/shard_map/fourth/pallas_call | solution.py:405
  124.9 0.0 collective-permute-done.9.other_ref
  124.9 5.8 %last.1 = (f32[768,768]{1,0:T(8,128)}, bf16[1536,768]{1,0:T(8,128)(2,1)}) custom-call(f32[768,768]{1,0:T(8,128)} %h_ref.1, bf16[1536,768]{1,0:T(8,128)(2,1)} %w_ref.1, bf16[8,144,256]{2,1,0:T(8,128)(2,1)S(1)} %all-to-all-done.1.own_ref, bf16[8,144,256]{2,1,0:T(8,128)(2,1)S(1)} %collective-permute-done.9.other_ref, ...), custom_call_target="tpu_custom_call" | custom-call | tf_op jit(solution)/shard_map/last/pallas_call | solution.py:424
  (6 shorter events, 0.1 us)
Async XLA Ops:
  5.3 7.7 %copy-start.1 = (bf16[8,96,256]{2,1,0:T(8,128)(2,1)S(1)}, bf16[8,96,256]{2,1,0:T(8,128)(2,1)}, u32[]{:S(2)}) copy-start(bf16[8,96,256]{2,1,0:T(8,128)(2,1)} %get-tuple-element.22) | copy-start | bytes 1179652
  5.3 10.1 %copy-start = (bf16[8,96,256]{2,1,0:T(8,128)(2,1)S(1)}, bf16[8,96,256]{2,1,0:T(8,128)(2,1)}, u32[]{:S(2)}) copy-start(bf16[8,96,256]{2,1,0:T(8,128)(2,1)} %get-tuple-element.21.keep_ref) | copy-start | bytes 1179652
  5.3 26.7 %all-to-all-start = ((f32[16,152,128]{2,1,0:T(8,128)}), f32[16,152,128]{2,1,0:T(8,128)S(1)}, u32[]{:S(2)}, u32[]{:S(2)}) async-start(f32[16,152,128]{2,1,0:T(8,128)} %get-tuple-element.20), calls=%async_computation | async-start | bytes 2490368 | tf_op jit(solution)/shard_map/all_to_all | solution.py:21
  13.1 2.4 %collective-permute-start = (bf16[8,96,256]{2,1,0:T(8,128)(2,1)S(1)}, bf16[8,96,256]{2,1,0:T(8,128)(2,1)S(1)}, u32[]{:S(2)}, u32[]{:S(2)}) collective-permute-start(bf16[8,96,256]{2,1,0:T(8,128)(2,1)S(1)} %copy-done.1), channel_id=1, source_target_pairs={{0,1},{1,0},{2,3},{3,2},{4,5},{5,4},{6,7},{7,6},{8,9},{9,8},{10,11... | collective-permute-start | bytes 1179656 | tf_op jit(solution)/shard_map/ppermute | solution.py:355
  15.5 13.4 %collective-permute-start.1 = (bf16[96,256]{1,0:T(8,128)(2,1)S(1)}, bf16[96,256]{1,0:T(8,128)(2,1)S(1)}, u32[]{:S(2)}, u32[]{:S(2)}) collective-permute-start(bf16[96,256]{1,0:T(8,128)(2,1)S(1)} %get-tuple-element.24), channel_id=1, source_target_pairs={{0,2},{2,4},{4,6},{6,8},{8,10},{10,12},{12,14},{14,0},{1,3},{3,5},... | collective-permute-start | bytes 147464 | tf_op jit(solution)/shard_map/ppermute | solution.py:368
  17.2 14.1 %collective-permute-start.2 = (bf16[96,256]{1,0:T(8,128)(2,1)S(1)}, bf16[96,256]{1,0:T(8,128)(2,1)S(1)}, u32[]{:S(2)}, u32[]{:S(2)}) collective-permute-start(bf16[96,256]{1,0:T(8,128)(2,1)S(1)} %get-tuple-element.25), channel_id=1, source_target_pairs={{0,4},{2,6},{4,8},{6,10},{8,12},{10,14},{12,0},{14,2},{1,5},{3,7},... | collective-permute-start | bytes 147464 | tf_op jit(solution)/shard_map/ppermute | solution.py:368
  20.2 11.8 %collective-permute-start.3 = (bf16[96,256]{1,0:T(8,128)(2,1)S(1)}, bf16[96,256]{1,0:T(8,128)(2,1)S(1)}, u32[]{:S(2)}, u32[]{:S(2)}) collective-permute-start(bf16[96,256]{1,0:T(8,128)(2,1)S(1)} %get-tuple-element.26), channel_id=1, source_target_pairs={{0,6},{2,8},{4,10},{6,12},{8,14},{10,0},{12,2},{14,4},{1,7},{3,9},... | collective-permute-start | bytes 147464 | tf_op jit(solution)/shard_map/ppermute | solution.py:368
  24.0 13.9 %collective-permute-start.5 = (bf16[96,256]{1,0:T(8,128)(2,1)S(1)}, bf16[96,256]{1,0:T(8,128)(2,1)S(1)}, u32[]{:S(2)}, u32[]{:S(2)}) collective-permute-start(bf16[96,256]{1,0:T(8,128)(2,1)S(1)} %get-tuple-element.29), channel_id=1, source_target_pairs={{0,8},{2,10},{4,12},{6,14},{8,0},{10,2},{12,4},{14,6},{1,9},{3,11}... | collective-permute-start | bytes 147464 | tf_op jit(solution)/shard_map/ppermute | solution.py:368
  24.4 13.4 %collective-permute-start.6 = (bf16[96,256]{1,0:T(8,128)(2,1)S(1)}, bf16[96,256]{1,0:T(8,128)(2,1)S(1)}, u32[]{:S(2)}, u32[]{:S(2)}) collective-permute-start(bf16[96,256]{1,0:T(8,128)(2,1)S(1)} %get-tuple-element.30), channel_id=1, source_target_pairs={{0,10},{2,12},{4,14},{6,0},{8,2},{10,4},{12,6},{14,8},{1,11},{3,13... | collective-permute-start | bytes 147464 | tf_op jit(solution)/shard_map/ppermute | solution.py:368
  28.9 9.0 %collective-permute-start.7 = (bf16[96,256]{1,0:T(8,128)(2,1)S(1)}, bf16[96,256]{1,0:T(8,128)(2,1)S(1)}, u32[]{:S(2)}, u32[]{:S(2)}) collective-permute-start(bf16[96,256]{1,0:T(8,128)(2,1)S(1)} %get-tuple-element.31), channel_id=1, source_target_pairs={{0,12},{2,14},{4,0},{6,2},{8,4},{10,6},{12,8},{14,10},{1,13},{3,15... | collective-permute-start | bytes 147464 | tf_op jit(solution)/shard_map/ppermute | solution.py:368
  31.3 6.6 %collective-permute-start.8 = (bf16[96,256]{1,0:T(8,128)(2,1)S(1)}, bf16[96,256]{1,0:T(8,128)(2,1)S(1)}, u32[]{:S(2)}, u32[]{:S(2)}) collective-permute-start(bf16[96,256]{1,0:T(8,128)(2,1)S(1)} %get-tuple-element.32), channel_id=1, source_target_pairs={{0,14},{2,0},{4,2},{6,4},{8,6},{10,8},{12,10},{14,12},{1,15},{3,1}... | collective-permute-start | bytes 147464 | tf_op jit(solution)/shard_map/ppermute | solution.py:368
  32.1 7.3 %collective-permute-start.4 = (f32[48,128]{1,0:T(8,128)S(1)}, f32[48,128]{1,0:T(8,128)S(1)}, u32[]{:S(2)}, u32[]{:S(2)}) collective-permute-start(f32[48,128]{1,0:T(8,128)S(1)} %get-tuple-element.28.piece_ref), channel_id=1, source_target_pairs={{0,0},{1,16},{2,32},{3,48},{4,64},{5,80},{6,96},{7,112},{8,128},{9... | collective-permute-start | bytes 73736 | tf_op jit(solution)/shard_map/ppermute | solution.py:383
  40.2 42.0 %all-to-all-start.1 = ((bf16[8,144,256]{2,1,0:T(8,128)(2,1)}), bf16[8,144,256]{2,1,0:T(8,128)(2,1)S(1)}, u32[]{:S(2)}, u32[]{:S(2)}) async-start(bf16[8,144,256]{2,1,0:T(8,128)(2,1)} %pack.1), calls=%async_computation.1 | async-start | bytes 1179648 | tf_op jit(solution)/shard_map/all_to_all | solution.py:21
  82.2 28.1 %all-to-all-start.2 = ((f32[16,200,128]{2,1,0:T(8,128)}), f32[16,200,128]{2,1,0:T(8,128)S(1)}, u32[]{:S(2)}, u32[]{:S(2)}) async-start(f32[16,200,128]{2,1,0:T(8,128)} %third.1), calls=%async_computation.2 | async-start | bytes 3276800 | tf_op jit(solution)/shard_map/all_to_all | solution.py:21
  85.9 39.0 %collective-permute-start.9 = (bf16[8,144,256]{2,1,0:T(8,128)(2,1)S(1)}, bf16[8,144,256]{2,1,0:T(8,128)(2,1)S(1)}, u32[]{:S(2)}, u32[]{:S(2)}) collective-permute-start(bf16[8,144,256]{2,1,0:T(8,128)(2,1)S(1)} %all-to-all-done.1.own_ref), channel_id=1, source_target_pairs={{0,1},{1,0},{2,3},{3,2},{4,5},{5,4},{6,7},{7,6},{8,9},{9,8},{10,11... | collective-permute-start | bytes 1769480 | tf_op jit(solution)/shard_map/ppermute | solution.py:404
